TPU v7x, 32 devices: a whole 2x2x4 slice. The times are simulated.
32 devices in a mesh: slab: 8 (over z, x), blk: 4 (over y, core).
Axes of the slice: x: 2, y: 2, z: 4, core: 2. Of those that a mesh axis runs over, the one named last changes fastest.
Arguments:
- incident: float32 [16, 2, 336, 128], P('slab', None, 'blk'), may hold values from -6 to 6
- mie_coef: float32 [16, 2, 336], P('slab', None, 'blk'), may hold values from -0.6 to 0.6
- translation: bfloat16 [16, 8, 2, 336, 336], P('slab', None, None, 'blk'), may hold values from -0.078125 to 0.078125
- pair_shift: int32 [16, 8], P('slab'), may hold values from -1 to 1
- pair_member: int32 [16, 8], P('slab'), may hold values from 0 to 1
- positions: float32 [16, 3], P('slab'), may hold values from 0 to 1
- wave_index: int32 [256, 3], replicated, may hold values from -4 to 4
- plane_coef: bfloat16 [256, 2, 336], replicated, may hold values from -0.25 to 0.25
- ewald_weight: float32 [256], replicated, may hold values from 0.002 to 0.04
Outputs:
- basis_next: float32 [16, 2, 336, 128], P('slab', None, 'blk')
- residual: float32 [16, 2, 336, 128], P('slab', None, 'blk')
- hessenberg: float32 [9, 128], replicated
Inputs may be any that keep to these rules, and one draw needn't show every extreme that they name: `pair_shift`: each pair's source sphere lies in the target's slab or in one of the two slabs beside it on the periodic cycle of slabs.
All inputs are finite; a program needn't handle non-finite values.
Results may differ from a plain program's by a relative error of at most 0.004.
Values may be sent and summed in bfloat16 or wider, within the bound.
No kernel may reach another device: no remote copies, remote signals or barrier semaphores. Data moves between devices by JAX's collectives and lax.ppermute only.
A program may use at most 64 MiB of HBM per device.

v0:
```python
import jax
import jax.numpy as jnp
from jax import lax
from jax.sharding import PartitionSpec as P

two_pi = 6.283185307179586
epsilon = 1e-06
highest = lax.Precision.HIGHEST


def with_halo(cells, sides, width):
    for axis, dim in sides:
        count = lax.axis_size(axis)
        head = lax.slice_in_dim(cells, 0, width, axis=dim)
        tail = lax.slice_in_dim(cells, cells.shape[dim] - width, cells.shape[dim], axis=dim)
        cells = jnp.concatenate(
            [
                lax.ppermute(tail, axis, [(i, (i + 1) % count) for i in range(count)]),
                cells,
                lax.ppermute(head, axis, [((i + 1) % count, i) for i in range(count)]),
            ],
            axis=dim,
        )
    return cells


def complex_scale(coef_pair, basis):
    part_re = coef_pair[0] * basis[:, 0] - coef_pair[1] * basis[:, 1]
    part_im = coef_pair[0] * basis[:, 1] + coef_pair[1] * basis[:, 0]
    return jnp.stack([part_re, part_im], axis=1)


def inner_sum(left, right):
    part_re = jnp.sum(left[:, 0] * right[:, 0] + left[:, 1] * right[:, 1], axis=(0, 1))
    part_im = jnp.sum(left[:, 0] * right[:, 1] - left[:, 1] * right[:, 0], axis=(0, 1))
    return jnp.stack([part_re, part_im])


def plane_sums(projected, cos_part, sin_part):
    part_re = projected[:, 0, :, 0] - projected[:, 1, :, 1]
    part_im = projected[:, 0, :, 1] + projected[:, 1, :, 0]
    sum_re = jnp.sum(cos_part[:, :, None] * part_re + sin_part[:, :, None] * part_im, axis=1)
    sum_im = jnp.sum(cos_part[:, :, None] * part_im - sin_part[:, :, None] * part_re, axis=1)
    return jnp.stack([sum_re, sum_im], axis=1)


def plane_field(totals, coef_full, cos_part, sin_part, weights):
    total_re = totals[:, 0][:, None, :]
    total_im = totals[:, 1][:, None, :]
    turn_re = weights[:, None, None] * (
        cos_part[:, :, None] * total_re - sin_part[:, :, None] * total_im
    )
    turn_im = weights[:, None, None] * (
        cos_part[:, :, None] * total_im + sin_part[:, :, None] * total_re
    )
    turned = jnp.stack([turn_re, turn_im], axis=1)
    projected = jnp.einsum("gac,gbjn->jabcn", coef_full, turned, precision=highest)
    return jnp.stack(
        [projected[:, 0, 0] + projected[:, 1, 1], projected[:, 0, 1] - projected[:, 1, 0]], axis=1
    )


def apply_operator(
    vector, mie_coef, translation, source_rows, cos_part, sin_part, plane_coef, ewald_weight
):
    sphere_count = vector.shape[0]
    row_count = vector.shape[2]
    wave_count = plane_coef.shape[0]
    rounded = vector.astype(jnp.bfloat16)
    full_field = lax.all_gather(rounded, "blk", axis=2, tiled=True)
    extended = with_halo(full_field, (("slab", 0),), sphere_count)
    pair_count = translation.shape[0] * translation.shape[1]
    flat_trans = translation.reshape(pair_count, 2, row_count, translation.shape[4])
    sources = jnp.take(extended, source_rows, axis=0)
    product = jnp.einsum(
        "parc,pzcn->pazrn", flat_trans, sources, preferred_element_type=jnp.float32
    )
    near_re = product[:, 0, 0] - product[:, 1, 1]
    near_im = product[:, 0, 1] + product[:, 1, 0]
    near = (
        jnp.stack([near_re, near_im], axis=1)
        .reshape(sphere_count, translation.shape[1], 2, row_count, vector.shape[3])
        .sum(axis=1)
    )
    row_start = lax.axis_index("blk") * row_count
    coef_rows = lax.dynamic_slice_in_dim(plane_coef, row_start, row_count, 2)
    slice_count = wave_count // lax.axis_size("blk")
    wave_start = lax.axis_index("blk") * slice_count
    coef_slice = lax.dynamic_slice_in_dim(plane_coef, wave_start, slice_count, 0)
    cos_slice = lax.dynamic_slice_in_dim(cos_part, wave_start, slice_count, 0)
    sin_slice = lax.dynamic_slice_in_dim(sin_part, wave_start, slice_count, 0)
    projected = jnp.einsum(
        "gac,jbcn->gajbn", coef_slice, full_field, preferred_element_type=jnp.float32
    )
    partial_sums = plane_sums(projected, cos_slice, sin_slice)
    slice_total = lax.psum(partial_sums, "slab")
    totals = lax.all_gather(slice_total, "blk", axis=0, tiled=True)
    far = plane_field(totals, coef_rows.astype(jnp.float32), cos_part, sin_part, ewald_weight)
    summed = near + far
    scaled_re = (
        mie_coef[:, 0][:, :, None] * summed[:, 0] - mie_coef[:, 1][:, :, None] * summed[:, 1]
    )
    scaled_im = (
        mie_coef[:, 0][:, :, None] * summed[:, 1] + mie_coef[:, 1][:, :, None] * summed[:, 0]
    )
    return vector - jnp.stack([scaled_re, scaled_im], axis=1)


def squared(field):
    return jnp.sum(field * field, axis=(0, 1, 2))


def per_device(
    incident,
    mie_coef,
    translation,
    pair_shift,
    pair_member,
    positions,
    wave_index,
    plane_coef,
    ewald_weight,
):
    sphere_count = incident.shape[0]
    entries = sphere_count * lax.axis_size("slab") * incident.shape[2] * lax.axis_size("blk")
    source_rows = ((pair_shift + 1) * sphere_count + pair_member).reshape(-1)
    angles = two_pi * jnp.sum(
        wave_index.astype(jnp.float32)[:, None, :] * positions[None, :, :], axis=-1
    )
    cos_part = jnp.cos(angles)
    sin_part = jnp.sin(angles)

    def operator(vector):
        return apply_operator(
            vector, mie_coef, translation, source_rows, cos_part, sin_part, plane_coef, ewald_weight
        )

    start_total = lax.psum(squared(incident), ("slab", "blk"))
    beta = jnp.sqrt(start_total / entries + epsilon)
    first = incident / beta
    image = operator(first)
    proj_sum = lax.psum(inner_sum(first, image), ("slab", "blk"))
    h_one_one = proj_sum / entries
    image = image - complex_scale(h_one_one, first)
    first_total = lax.psum(squared(image), ("slab", "blk"))
    h_two_one = jnp.sqrt(first_total / entries + epsilon)
    basis_next = image / h_two_one
    image = operator(basis_next)
    h_one_two = lax.psum(inner_sum(first, image), ("slab", "blk")) / entries
    image = image - complex_scale(h_one_two, first)
    h_two_two = lax.psum(inner_sum(basis_next, image), ("slab", "blk")) / entries
    residual = image - complex_scale(h_two_two, basis_next)
    last_total = lax.psum(squared(residual), ("slab", "blk"))
    h_three_two = jnp.sqrt(last_total / entries + epsilon)
    hessenberg = jnp.stack(
        [
            beta,
            h_one_one[0],
            h_one_one[1],
            h_two_one,
            h_one_two[0],
            h_one_two[1],
            h_two_two[0],
            h_two_two[1],
            h_three_two,
        ]
    )
    return (basis_next, residual, hessenberg)


def solution(mesh):
    placed = (
        P("slab", None, "blk", None),
        P("slab", None, "blk"),
        P("slab", None, None, "blk", None),
        P("slab", None),
        P("slab", None),
        P("slab", None),
        P(),
        P(),
        P(),
    )
    return jax.shard_map(
        per_device,
        mesh=mesh,
        in_specs=placed,
        out_specs=(P("slab", None, "blk", None), P("slab", None, "blk", None), P()),
        check_vma=False,
    )
```

profile of v0, /device:TPU:0, one launch (start us, length us, event | category | flops | bytes accessed | tf_op | source)
XLA Modules:
  0.0 478.5 jit_solution(5836638708583548738)
XLA Ops:
  7.2 1.2 multiply_reduce_fusion.2
  8.5 42.0 %psum.56 = f32[128]{0:T(128)S(1)} all-reduce(f32[128]{0:T(128)S(1)} %multiply_reduce_fusion.2), channel_id=1, replica_groups=mesh['slab'=8,'blk'=4] {'slab','blk'}, use_global_device_ids=true, to_apply=%region_1.0 | all-reduce | flops 128 | bytes 1024 | tf_op jit(solution)/shard_map/psum | solution.py:138
  50.5 0.5 fusion.51
  51.0 0.9 copy_divide_fusion
  51.9 0.1 copy.52
  52.0 7.0 %all_gather.12 = bf16[2,2,336,128]{3,1,0,2:T(2,128)(2,1)S(1)} all-gather(bf16[2,2,84,128]{3,1,0,2:T(2,128)(2,1)S(1)} %copy.52), channel_id=1, replica_groups=mesh['slab'=8,'blk'=4] {'blk'}, dimensions={2}, use_global_device_ids=true | all-gather | bytes 430080 | tf_op jit(solution)/shard_map/all_gather | solution.py:70
  59.0 1.3 collective-permute-start
  60.3 3.4 collective-permute-start.1
  63.7 0.7 convert_element_type.12
  64.4 0.8 copy.55
  65.2 0.1 multiply_reduce_fusion.3
  65.3 0.1 multiply_cosine_fusion
  65.3 1.3 fusion.24
  66.6 0.1 constant_dynamic-slice_fusion
  66.7 0.1 add_reduce_fusion.4
  66.8 0.6 pad_maximum_fusion.2
  67.5 0.7 multiply_add_fusion.5
  68.2 0.1 reshape.268
  68.3 0.8 fusion.55
  69.1 65.3 %all-reduce.3.cloned.1.call-done = f32[64,2,128]{2,0,1:T(8,128)} async-done(((f32[64,2,128]{2,0,1:T(8,128)}), f32[64,2,128]{2,0,1:T(8,128)}) %all-reduce.3.cloned.1.call-update) | async-done | bytes 65552 | tf_op jit(solution)/shard_map/psum | solution.py:96
  134.3 6.0 %all_gather.13 = f32[256,2,128]{2,0,1:T(8,128)S(1)} all-gather(f32[64,2,128]{2,0,1:T(8,128)} %all-reduce.3.cloned.1.call-done), channel_id=1, replica_groups=mesh['slab'=8,'blk'=4] {'blk'}, dimensions={0}, use_global_device_ids=true | all-gather | bytes 327680 | tf_op jit(solution)/shard_map/all_gather | solution.py:97
  140.3 0.2 subtract_multiply_fusion.1
  140.6 1.3 convolution_bitcast_fusion.1
  141.9 0.7 copy-done.6
  142.7 2.5 pad_maximum_fusion
  145.2 8.9 %gather_fusion = bf16[16,2,336,128]{3,1,2,0:T(2,128)(2,1)} fusion(bf16[6,2,336,128]{3,1,0,2:T(2,128)(2,1)S(1)} %pad_maximum_fusion, s32[1024]{0:T(1024)S(1)} %pad_clamp_fusion), kind=kCustom, calls=%fused_computation.clone | custom fusion | bytes 5505088 | tf_op jit(solution)/shard_map/jit(_take)/gather | solution.py:74
  154.1 4.2 fusion.4
  158.3 0.9 fusion.8
  159.3 0.1 slice_subtract_fusion.1
  159.4 0.1 maximum_reduce_fusion
  159.5 0.1 multiply_subtract_fusion.4
  159.7 0.5 copy-done.1
  160.2 0.1 add_reduce_fusion.2
  160.3 40.3 %psum.58 = f32[2,128]{1,0:T(2,128)S(1)} all-reduce(f32[2,128]{1,0:T(2,128)S(1)} %pad_maximum_fusion.4), channel_id=1, replica_groups=mesh['slab'=8,'blk'=4] {'slab','blk'}, use_global_device_ids=true, to_apply=%region_9.11 | all-reduce | flops 256 | bytes 2048 | tf_op jit(solution)/shard_map/psum | solution.py:142
  200.6 0.1 multiply_reduce_fusion.1
  200.7 39.1 %psum.59 = f32[128]{0:T(128)S(1)} all-reduce(f32[128]{0:T(128)S(1)} %multiply_reduce_fusion.1), channel_id=1, replica_groups=mesh['slab'=8,'blk'=4] {'slab','blk'}, use_global_device_ids=true, to_apply=%region_11.13 | all-reduce | flops 128 | bytes 1024 | tf_op jit(solution)/shard_map/psum | solution.py:145
  239.8 0.5 fusion.52
  240.4 0.1 copy.62
  240.5 7.0 %all_gather.14 = bf16[2,2,336,128]{3,1,0,2:T(2,128)(2,1)S(1)} all-gather(bf16[2,2,84,128]{3,1,0,2:T(2,128)(2,1)S(1)} %copy.62), channel_id=1, replica_groups=mesh['slab'=8,'blk'=4] {'blk'}, dimensions={2}, use_global_device_ids=true | all-gather | bytes 430080 | tf_op jit(solution)/shard_map/all_gather | solution.py:70
  247.4 0.3 fusion.22
  247.8 0.1 add_reduce_fusion.3
  247.9 0.6 pad_maximum_fusion.3
  248.5 1.5 collective-permute-start.2
  250.0 3.3 collective-permute-start.3
  253.3 0.8 copy.71
  254.1 69.9 %all-reduce.5.cloned.1.call-done = f32[64,2,128]{2,0,1:T(8,128)} async-done(((f32[64,2,128]{2,0,1:T(8,128)}), f32[64,2,128]{2,0,1:T(8,128)}) %all-reduce.5.cloned.1.call-update) | async-done | bytes 65552 | tf_op jit(solution)/shard_map/psum | solution.py:96
  323.9 6.0 %all_gather.15 = f32[256,2,128]{2,0,1:T(8,128)S(1)} all-gather(f32[64,2,128]{2,0,1:T(8,128)} %all-reduce.5.cloned.1.call-done), channel_id=1, replica_groups=mesh['slab'=8,'blk'=4] {'blk'}, dimensions={0}, use_global_device_ids=true | all-gather | bytes 327680 | tf_op jit(solution)/shard_map/all_gather | solution.py:97
  329.9 0.2 subtract_multiply_fusion
  330.2 0.4 convolution_bitcast_fusion
  330.6 0.7 fusion.32
  331.2 2.6 pad_maximum_fusion.1
  333.8 9.0 %gather_fusion.1 = bf16[16,2,336,128]{3,1,2,0:T(2,128)(2,1)} fusion(bf16[6,2,336,128]{3,1,0,2:T(2,128)(2,1)S(1)} %pad_maximum_fusion.1, s32[1024]{0:T(1024)} %copy-done.9), kind=kCustom, calls=%fused_computation.1.clone | custom fusion | bytes 5505088 | tf_op jit(solution)/shard_map/jit(_take)/gather | solution.py:74
  342.8 4.2 fusion.5
  347.0 0.9 fusion.13
  348.0 0.1 slice_subtract_fusion
  348.1 0.1 maximum_reduce_fusion.1
  348.2 0.6 copy-done.5
  348.9 0.1 multiply_subtract_fusion.2
  349.1 40.4 %psum.61 = f32[2,128]{1,0:T(2,128)S(1)} all-reduce(f32[2,128]{1,0:T(2,128)S(1)} %pad_maximum_fusion.5), channel_id=1, replica_groups=mesh['slab'=8,'blk'=4] {'slab','blk'}, use_global_device_ids=true, to_apply=%region_18.20 | all-reduce | flops 256 | bytes 2048 | tf_op jit(solution)/shard_map/psum | solution.py:149
  389.6 39.1 %psum.62 = f32[2,128]{1,0:T(2,128)S(1)} all-reduce(f32[2,128]{1,0:T(2,128)S(1)} %pad_maximum_fusion.6), channel_id=1, replica_groups=mesh['slab'=8,'blk'=4] {'slab','blk'}, use_global_device_ids=true, to_apply=%region_21.23 | all-reduce | flops 256 | bytes 2048 | tf_op jit(solution)/shard_map/psum | solution.py:151
  428.7 0.1 multiply_reduce_fusion
  428.8 40.9 %psum.63 = f32[128]{0:T(128)S(1)} all-reduce(f32[128]{0:T(128)S(1)} %get-tuple-element.23), channel_id=1, replica_groups=mesh['slab'=8,'blk'=4] {'slab','blk'}, use_global_device_ids=true, to_apply=%region_23.25 | all-reduce | flops 128 | bytes 1024 | tf_op jit(solution)/shard_map/psum | solution.py:153
  469.7 0.8 copy.72
  470.5 1.2 stack.142
  (61 shorter events, 0.7 us)
Async XLA Ops:
  7.2 151.1 %copy-start = (bf16[2,8,2,84,336]{4,2,3,1,0:T(2,128)(2,1)S(1)}, bf16[2,8,2,84,336]{4,2,3,1,0:T(2,128)(2,1)}, u32[]{:S(2)}) copy-start(bf16[2,8,2,84,336]{4,2,3,1,0:T(2,128)(2,1)} %param.13) | copy-start | bytes 5419012
  7.2 133.1 %copy-start.10 = (f32[256]{0:T(256)S(1)}, f32[256]{0:T(256)}, u32[]{:S(2)}) copy-start(f32[256]{0:T(256)} %param.19) | copy-start | bytes 3076
  7.2 127.1 %all-reduce.3.cloned.1.call-start = ((), (), s32[]{:S(2)}) async-start(), calls=%async_computation | async-start | bytes 131072 | tf_op jit(solution)/shard_map/psum | solution.py:96
  59.0 82.9 %copy-start.2 = (bf16[2,2,336,128]{3,1,0,2:T(2,128)(2,1)}, bf16[2,2,336,128]{3,1,0,2:T(2,128)(2,1)S(1)}, u32[]{:S(2)}) copy-start(bf16[2,2,336,128]{3,1,0,2:T(2,128)(2,1)S(1)} %all_gather.12) | copy-start | bytes 1032196
  59.0 82.9 %collective-permute-start = (bf16[2,2,336,128]{3,1,0,2:T(2,128)(2,1)S(1)}, bf16[2,2,336,128]{3,1,0,2:T(2,128)(2,1)S(1)}, u32[]{:S(2)}, u32[]{:S(2)}) collective-permute-start(bf16[2,2,336,128]{3,1,0,2:T(2,128)(2,1)S(1)} %all_gather.12), channel_id=1, source_target_pairs={{0,4},{4,8},{8,12},{12,16},{16,20},{20,24},{24,28},{28,0},{1,5},{5... | collective-permute-start | bytes 1032200 | tf_op jit(solution)/shard_map/ppermute | solution.py:18
  60.3 82.4 %collective-permute-start.1 = (bf16[2,2,336,128]{3,1,0,2:T(2,128)(2,1)S(1)}, bf16[2,2,336,128]{3,1,0,2:T(2,128)(2,1)}, u32[]{:S(2)}, u32[]{:S(2)}) collective-permute-start(bf16[2,2,336,128]{3,1,0,2:T(2,128)(2,1)S(1)} %all_gather.12), channel_id=1, source_target_pairs={{4,0},{8,4},{12,8},{16,12},{20,16},{24,20},{28,24},{0,28},{5,1},{9... | collective-permute-start | bytes 1032200 | tf_op jit(solution)/shard_map/ppermute | solution.py:20
  67.4 256.5 %all-reduce.5.cloned.1.call-start = ((), (), s32[]{:S(2)}) async-start(), calls=%async_computation.1 | async-start | bytes 131072 | tf_op jit(solution)/shard_map/psum | solution.py:96
  68.3 85.8 %copy-start.11 = (pred[16]{0:T(512)(128)(4,1)}, pred[16]{0:T(512)(128)(4,1)S(1)}, u32[]{:S(2)}) copy-start(pred[16]{0:T(512)(128)(4,1)S(1)} %compare_and_fusion) | copy-start | bytes 52
  69.1 85.0 %copy-start.9 = (s32[1024]{0:T(1024)}, s32[1024]{0:T(1024)S(1)}, u32[]{:S(2)}) copy-start(s32[1024]{0:T(1024)S(1)} %pad_clamp_fusion) | copy-start | bytes 12292
  141.9 0.7 copy-start.6
  159.2 0.9 copy-start.1
  159.4 88.0 %copy-start.4 = (bf16[256,2,336]{0,2,1:T(8,128)(2,1)S(1)}, bf16[256,2,336]{0,2,1:T(8,128)(2,1)}, u32[]{:S(2)}) copy-start(bf16[256,2,336]{0,2,1:T(8,128)(2,1)} %param.18) | copy-start | bytes 1032196
  200.6 129.6 %copy-start.7 = (f32[2,128]{1,0:T(2,128)}, f32[2,128]{1,0:T(2,128)S(1)}, u32[]{:S(2)}) copy-start(f32[2,128]{1,0:T(2,128)S(1)} %broadcast_multiply_fusion.2) | copy-start | bytes 3076
  247.4 83.8 %copy-start.3 = (bf16[2,2,336,128]{3,1,0,2:T(2,128)(2,1)}, bf16[2,2,336,128]{3,1,0,2:T(2,128)(2,1)S(1)}, u32[]{:S(2)}) copy-start(bf16[2,2,336,128]{3,1,0,2:T(2,128)(2,1)S(1)} %all_gather.14) | copy-start | bytes 1032196
  248.5 82.7 %collective-permute-start.2 = (bf16[2,2,336,128]{3,1,0,2:T(2,128)(2,1)S(1)}, bf16[2,2,336,128]{3,1,0,2:T(2,128)(2,1)}, u32[]{:S(2)}, u32[]{:S(2)}) collective-permute-start(bf16[2,2,336,128]{3,1,0,2:T(2,128)(2,1)S(1)} %all_gather.14), channel_id=1, source_target_pairs={{0,4},{4,8},{8,12},{12,16},{16,20},{20,24},{24,28},{28,0},{1,5},{5... | collective-permute-start | bytes 1032200 | tf_op jit(solution)/shard_map/ppermute | solution.py:18
  250.0 81.2 %collective-permute-start.3 = (bf16[2,2,336,128]{3,1,0,2:T(2,128)(2,1)S(1)}, bf16[2,2,336,128]{3,1,0,2:T(2,128)(2,1)}, u32[]{:S(2)}, u32[]{:S(2)}) collective-permute-start(bf16[2,2,336,128]{3,1,0,2:T(2,128)(2,1)S(1)} %all_gather.14), channel_id=1, source_target_pairs={{4,0},{8,4},{12,8},{16,12},{20,16},{24,20},{28,24},{0,28},{5,1},{9... | collective-permute-start | bytes 1032200 | tf_op jit(solution)/shard_map/ppermute | solution.py:20
  347.9 0.9 copy-start.5
  348.2 122.3 %copy-start.8 = (f32[2,128]{1,0:T(2,128)S(1)}, f32[2,128]{1,0:T(2,128)}, u32[]{:S(2)}) copy-start(f32[2,128]{1,0:T(2,128)} %copy-done.7) | copy-start | bytes 3076
  348.2 122.3 %copy-start.12 = (f32[1,128]{1,0:T(1,128)S(1)}, f32[1,128]{1,0:T(1,128)}, u32[]{:S(2)}) copy-start(f32[1,128]{1,0:T(1,128)} %get-tuple-element.65) | copy-start | bytes 1540
  348.2 122.3 %copy-start.13 = (f32[1,128]{1,0:T(1,128)S(1)}, f32[1,128]{1,0:T(1,128)}, u32[]{:S(2)}) copy-start(f32[1,128]{1,0:T(1,128)} %get-tuple-element.63) | copy-start | bytes 1540
Sparse Core Ops, SparseCore 0:
  67.5 66.7 all-reduce.2
  248.7 75.2 all-reduce.4
where the time goes:
time: 480 us; the launch traced here: 479 us
  blocking collectives  268 us (56%)
  waiting for transfers between devices  135 us (28%)
  local copies, waits for them, and re-layouts  24.4 us (5%)
  other arithmetic  22.3 us (5%)
  between operations  14.4 us (3%)
  starting transfers between devices  9.58 us (2%)
  matrix products  5.1 us (1%)
    psum x2, waiting for transfers between devices, apply_operator(): slice_total = lax.psum(partial_sums, 'slab')  135 us
    psum x1, blocking collectives, per_device(): start_total = lax.psum(squared(incident), ('slab', 'blk'))  42 us
    psum x1, blocking collectives, per_device(): last_total = lax.psum(squared(residual), ('slab', 'blk'))  40.9 us
    psum x1, blocking collectives, per_device(): h_one_two = lax.psum(inner_sum(first, image), ('slab', 'blk')) / entries  40.4 us
    psum x1, blocking collectives, per_device(): proj_sum = lax.psum(inner_sum(first, image), ('slab', 'blk'))  40.3 us
    psum x1, blocking collectives, per_device(): lax.psum(inner_sum(basis_next, image), ('slab', 'blk')) / entries  39.1 us
    psum x1, blocking collectives, per_device(): first_total = lax.psum(squared(image), ('slab', 'blk'))  39.1 us
    gather x2, local copies, waits for them, and re-layouts, apply_operator(): sources = jnp.take(extended, source_rows, axis=0)  17.8 us
  transfers between devices with their start and end apart: 6, of which 2 were waited for; matrix products, arithmetic and copies ran while one was open for 2% of the time, Pallas kernels for 0%

commit v1 on v0

v1 whole, which is shorter than its diff:
```python
import jax
import jax.numpy as jnp
from jax import lax
from jax.experimental import pallas as pl
from jax.experimental.pallas import tpu as pltpu
from jax.sharding import PartitionSpec as P

two_pi = 6.283185307179586
epsilon = 1e-06
f32 = jnp.float32
bf16 = jnp.bfloat16

VM = pl.BlockSpec(memory_space=pltpu.VMEM)
SM = pl.BlockSpec(memory_space=pltpu.SMEM)


def call(body, outs, specs, name):
    return pl.pallas_call(
        body,
        out_shape=outs,
        in_specs=specs,
        out_specs=jax.tree.map(lambda _: VM, outs),
        name=name,
    )


def shape(dims, dtype=f32):
    return jax.ShapeDtypeStruct(dims, dtype)


def round_body(x_ref, out_ref):
    count = out_ref.shape[2]
    for s in range(out_ref.shape[0]):
        for z in range(2):
            out_ref[s, z] = x_ref[s, pl.ds(z, count, stride=2), :].astype(bf16)


def project(field, plane_ref, cos, sin):
    sum_re = sum_im = None
    lead = (((0,), (0,)), ((), ()))
    for s in range(len(field)):
        both = jnp.concatenate(field[s], axis=1)
        with_re = lax.dot_general(plane_ref[0], both, lead, preferred_element_type=f32)
        with_im = lax.dot_general(plane_ref[1], both, lead, preferred_element_type=f32)
        n = both.shape[1] // 2
        part_re = with_re[:, :n] - with_im[:, n:]
        part_im = with_re[:, n:] + with_im[:, :n]
        c, d = cos[:, s : s + 1], sin[:, s : s + 1]
        turn_re = c * part_re + d * part_im
        turn_im = c * part_im - d * part_re
        sum_re = turn_re if sum_re is None else sum_re + turn_re
        sum_im = turn_im if sum_im is None else sum_im + turn_im
    return sum_re, sum_im


def split_halves(sum_re, sum_im, send_ref, keep_ref):
    half = sum_re.shape[0] // 2
    odd = lax.rem(lax.axis_index("blk"), 2) == 1
    n = sum_re.shape[1]
    for z, part in enumerate((sum_re, sum_im)):
        low, high = part[:half], part[half:]
        at = slice(z * n, (z + 1) * n)
        send_ref[:, at] = jnp.where(odd, low, high).astype(bf16)
        keep_ref[:, at] = jnp.where(odd, high, low)


def first_sums_body(x_ref, plane_ref, wave_ref, pos_ref, send_ref, keep_ref, cos_ref, sin_ref):
    spheres = x_ref.shape[0]
    lane = lax.broadcasted_iota(jnp.int32, (1, spheres), 1)
    turns = None
    for d in range(3):
        row = jnp.zeros((1, spheres), f32)
        for s in range(spheres):
            row = jnp.where(lane == s, pos_ref[s, d], row)
        term = wave_ref[:, d : d + 1].astype(f32) * row
        turns = term if turns is None else turns + term
    angles = two_pi * (turns - jnp.floor(turns + 0.5))
    cos, sin = jnp.cos(angles), jnp.sin(angles)
    cos_ref[...] = cos
    sin_ref[...] = sin
    field = [[x_ref[s, 0], x_ref[s, 1]] for s in range(spheres)]
    split_halves(*project(field, plane_ref, cos, sin), send_ref, keep_ref)


def gather_body(shift_ref, member_ref, *refs):
    *piece_refs, out_ref, held = refs
    blocks = len(piece_refs)
    slots, spheres, _, count, _ = piece_refs[0].shape
    b = lax.axis_index("blk")
    parity = lax.rem(lax.axis_index("slab"), 2)
    for slot in range(slots):
        for s in range(spheres):
            for z in range(2):
                parts = [ref[slot, s, z] for ref in piece_refs]
                bit = 1
                while bit < blocks:
                    swap = lax.rem(lax.div(b, bit), 2) == 1
                    parts = [
                        jnp.where(swap, parts[i ^ bit], parts[i]) for i in range(blocks)
                    ]
                    bit *= 2
                held[slot * spheres + s, z] = jnp.concatenate(parts, axis=0)
    for i in range(out_ref.shape[0]):
        for k in range(out_ref.shape[1]):
            shift = shift_ref[i, k]
            forward = (shift == 1) == (parity == 0)
            slot = jnp.where(shift == 0, 0, jnp.where(forward, 1, 2))
            out_ref[i, k] = held[slot * spheres + member_ref[i, k]]


def far_field(total, plane_ref, cos, sin, weight, spheres):
    total_re, total_im = total
    n = total_re.shape[1]
    fields = []
    for s in range(spheres):
        c, d = weight * cos[:, s : s + 1], weight * sin[:, s : s + 1]
        turned = jnp.concatenate(
            [c * total_re - d * total_im, c * total_im + d * total_re], axis=1
        ).astype(bf16)
        with_re = jnp.dot(plane_ref[0], turned, preferred_element_type=f32)
        with_im = jnp.dot(plane_ref[1], turned, preferred_element_type=f32)
        fields.append(
            (with_re[:, :n] + with_im[:, n:], with_re[:, n:] - with_im[:, :n])
        )
    return fields


def join_halves(mine_ref, other_ref):
    odd = lax.rem(lax.axis_index("blk"), 2) == 1
    n = mine_ref.shape[1] // 2
    out = []
    for z in range(2):
        at = slice(z * n, (z + 1) * n)
        mine, other = mine_ref[:, at], other_ref[:, at].astype(f32)
        out.append(
            jnp.concatenate([jnp.where(odd, other, mine), jnp.where(odd, mine, other)], axis=0)
        )
    return out


def image_fields(near_ref, mine_ref, other_ref, cos, sin, plane_ref, weight_ref, mie_ref):
    spheres = near_ref.shape[0]
    far = far_field(join_halves(mine_ref, other_ref), plane_ref, cos, sin, weight_ref[...], spheres)
    out = []
    for s in range(spheres):
        sum_re = near_ref[s, 0, 0] - near_ref[s, 1, 1] + far[s][0]
        sum_im = near_ref[s, 0, 1] + near_ref[s, 1, 0] + far[s][1]
        m_re, m_im = mie_ref[:, 2 * s : 2 * s + 1], mie_ref[:, 2 * s + 1 : 2 * s + 2]
        out.append((m_re * sum_re - m_im * sum_im, m_re * sum_im + m_im * sum_re))
    return out


def first_image_body(
    near_ref, mine_ref, other_ref, cos_ref, sin_ref, plane_ref, weight_ref, mie_ref,
    image_ref, round_ref, send_ref, keep_ref,
):
    cos, sin = cos_ref[...], sin_ref[...]
    images = image_fields(near_ref, mine_ref, other_ref, cos, sin, plane_ref, weight_ref, mie_ref)
    field = []
    for s, (re, im) in enumerate(images):
        image_ref[s, 0] = re
        image_ref[s, 1] = im
        field.append([re.astype(bf16), im.astype(bf16)])
        round_ref[s, 0] = field[s][0]
        round_ref[s, 1] = field[s][1]
    split_halves(*project(field, plane_ref, cos, sin), send_ref, keep_ref)


def second_image_body(
    near_ref, mine_ref, other_ref, cos_ref, sin_ref, plane_ref, weight_ref, mie_ref, x_ref, g_ref,
    image_ref, gram_ref,
):
    images = image_fields(
        near_ref, mine_ref, other_ref, cos_ref[...], sin_ref[...], plane_ref, weight_ref, mie_ref
    )
    count = g_ref.shape[2]
    sums = None
    for s, (re, im) in enumerate(images):
        image_ref[s, 0] = re
        image_ref[s, 1] = im
        x = (x_ref[s, pl.ds(0, count, stride=2), :], x_ref[s, pl.ds(1, count, stride=2), :])
        g = (g_ref[s, 0], g_ref[s, 1])
        h = (re, im)
        terms = [x[0] * x[0] + x[1] * x[1]]
        terms += [x[0] * g[0] + x[1] * g[1], x[0] * g[1] - x[1] * g[0]]
        terms += [g[0] * g[0] + g[1] * g[1]]
        terms += [x[0] * h[0] + x[1] * h[1], x[0] * h[1] - x[1] * h[0]]
        terms += [g[0] * h[0] + g[1] * h[1], g[0] * h[1] - g[1] * h[0]]
        terms += [h[0] * h[0] + h[1] * h[1]]
        rows = [jnp.sum(term, axis=0, keepdims=True) for term in terms]
        sums = rows if sums is None else [a + r for a, r in zip(sums, rows)]
    gram_ref[...] = jnp.zeros_like(gram_ref)
    for i, row in enumerate(sums):
        gram_ref[i : i + 1, :] = row


def times(a, b):
    return (a[0] * b[0] - a[1] * b[1], a[0] * b[1] + a[1] * b[0])


def conj_times(a, b):
    return (a[0] * b[0] + a[1] * b[1], a[0] * b[1] - a[1] * b[0])


def plus(*terms):
    return (sum(t[0] for t in terms), sum(t[1] for t in terms))


def scaled(a, r):
    return (a[0] * r, a[1] * r)


def finish_body(entries, gram_ref, x_ref, g_ref, h_ref, basis_ref, residual_ref, hess_ref):
    gram = gram_ref[...] / entries
    row = [gram[i : i + 1, :] for i in range(9)]
    xx, gg, hh = row[0], row[3], row[8]
    xg, xh, gh = (row[1], row[2]), (row[4], row[5]), (row[6], row[7])
    square = xx + epsilon
    beta = jnp.sqrt(square)
    inv = 1.0 / beta
    h11 = ((xx - xg[0]) / square, -xg[1] / square)
    alpha = ((epsilon + xg[0]) / square * inv, xg[1] / square * inv)
    delta = -inv
    cross = alpha[0] * xg[0] + alpha[1] * xg[1]
    norm = (alpha[0] * alpha[0] + alpha[1] * alpha[1]) * xx + delta * delta * gg + 2.0 * delta * cross
    h21 = jnp.sqrt(jnp.maximum(norm, 0.0) + epsilon)
    a = (alpha[0] / h21, alpha[1] / h21)
    d = delta / h21
    b = (d - a[0], -a[1])
    h12 = scaled(plus(scaled(a, xx), times(b, xg), scaled(xh, -d)), inv)
    e = (a[0] - h12[0] * inv, a[1] - h12[1] * inv)
    with_x = plus(scaled(e, xx), times(b, xg), scaled(xh, -d))
    with_g = plus(times(e, (xg[0], -xg[1])), scaled(b, gg), scaled(gh, -d))
    h22 = plus(conj_times(a, with_x), scaled(with_g, d))
    c0 = plus(e, scaled(times(h22, a), -1.0))
    c1 = plus(b, scaled(h22, -d))
    c2 = -d
    last = (
        (c0[0] * c0[0] + c0[1] * c0[1]) * xx
        + (c1[0] * c1[0] + c1[1] * c1[1]) * gg
        + c2 * c2 * hh
        + 2.0 * times(conj_times(c0, c1), xg)[0]
        + 2.0 * c2 * conj_times(c0, xh)[0]
        + 2.0 * c2 * conj_times(c1, gh)[0]
    )
    h32 = jnp.sqrt(jnp.maximum(last, 0.0) + epsilon)
    for i, value in enumerate((beta, h11[0], h11[1], h21, h12[0], h12[1], h22[0], h22[1], h32)):
        hess_ref[i : i + 1, :] = value
    count = g_ref.shape[2]
    for s in range(g_ref.shape[0]):
        rows = [pl.ds(z, count, stride=2) for z in range(2)]
        x = (x_ref[s, rows[0], :], x_ref[s, rows[1], :])
        g = (g_ref[s, 0], g_ref[s, 1])
        h = (h_ref[s, 0], h_ref[s, 1])
        basis = plus(times(a, x), scaled(g, d))
        residual = plus(times(c0, x), times(c1, g), scaled(h, c2))
        for z in range(2):
            basis_ref[s, rows[z], :] = basis[z]
            residual_ref[s, rows[z], :] = residual[z]


def trade(value, axis, bit):
    return lax.ppermute(value, axis, [(i, i ^ bit) for i in range(lax.axis_size(axis))])


def trade_odd(value):
    count = lax.axis_size("slab")
    pairs = []
    for i in range(count):
        pairs.append((i, (i + 1) % count if i % 2 else (i - 1) % count))
    return lax.ppermute(value, "slab", pairs)


def bits(axis, start=1):
    out, bit = [], start
    while bit < lax.axis_size(axis):
        out.append(bit)
        bit *= 2
    return out


def fetch_pieces(own):
    mine = jnp.stack([own, trade(own, "slab", 1), trade_odd(own)])
    pieces = {0: mine}
    for bit in bits("blk", 2):
        pieces.update({r | bit: trade(value, "blk", bit) for r, value in list(pieces.items())})
    for r, value in list(pieces.items()):
        pieces[r | 1] = trade(value, "blk", 1)
    return [pieces[r] for r in range(len(pieces))]


def total_sums(send, keep):
    keep = keep + trade(send, "blk", 1).astype(f32)
    steps = [("blk", bit) for bit in bits("blk", 2)] + [("slab", bit) for bit in bits("slab")]
    for axis, bit in steps:
        keep = keep + trade(keep.astype(bf16), axis, bit).astype(f32)
    return keep, trade(keep.astype(bf16), "blk", 1)


def total_gram(gram):
    for axis in ("blk", "slab"):
        for bit in bits(axis):
            gram = gram + trade(gram, axis, bit)
    return gram


def per_device(
    incident, mie_coef, translation, pair_shift, pair_member, positions, wave_index, plane_coef,
    ewald_weight,
):
    spheres, _, count, n = incident.shape
    pairs = translation.shape[1]
    blocks = lax.axis_size("blk")
    waves = plane_coef.shape[0]
    entries = spheres * lax.axis_size("slab") * count * blocks
    x = incident.transpose(0, 2, 1, 3).reshape(spheres, 2 * count, n)
    plane = lax.dynamic_slice_in_dim(
        plane_coef.transpose(1, 2, 0), lax.axis_index("blk") * count, count, 1
    )
    weight = ewald_weight.reshape(waves, 1)
    mie = mie_coef.transpose(2, 0, 1).reshape(count, spheres * 2)

    field = shape((spheres, 2, count, n))
    field_half = shape((spheres, 2, count, n), bf16)
    sums = shape((waves // 2, 2 * n))
    sums_half = shape((waves // 2, 2 * n), bf16)
    phase = shape((waves, spheres))
    sources = shape((spheres, pairs, 2, count * blocks, n), bf16)

    def near_products(own):
        pieces = fetch_pieces(own)
        slots = pieces[0].shape[0]
        gathered = pl.pallas_call(
            gather_body,
            out_shape=sources,
            in_specs=[SM, SM] + [VM] * blocks,
            out_specs=VM,
            scratch_shapes=[pltpu.VMEM((slots * spheres, 2, count * blocks, n), bf16)],
            name="gather",
        )(pair_shift, pair_member, *pieces)
        return jnp.einsum(
            "ikarc,ikzcn->iazrn", translation, gathered, preferred_element_type=f32
        )

    rounded = call(round_body, field_half, [VM], "round")(x)
    send, keep, cos, sin = call(
        first_sums_body, (sums_half, sums, phase, phase), [VM, VM, VM, SM], "first_sums"
    )(rounded, plane, wave_index, positions)
    mine, other = total_sums(send, keep)
    near = near_products(rounded)
    image, image_rounded, send, keep = call(
        first_image_body, (field, field_half, sums_half, sums), [VM] * 8, "first_image"
    )(near, mine, other, cos, sin, plane, weight, mie)

    mine, other = total_sums(send, keep)
    near = near_products(image_rounded)
    image_two, gram = call(second_image_body, (field, shape((16, n))), [VM] * 10, "second_image")(
        near, mine, other, cos, sin, plane, weight, mie, x, image
    )
    gram = total_gram(gram)
    flat = shape((spheres, 2 * count, n))
    basis, residual, hessenberg = call(
        lambda *refs: finish_body(float(entries), *refs), (flat, flat, shape((9, n))), [VM] * 4, "finish"
    )(gram, x, image, image_two)

    def unflatten(value):
        return value.reshape(spheres, count, 2, n).transpose(0, 2, 1, 3)

    return unflatten(basis), unflatten(residual), hessenberg


def solution(mesh):
    placed = (
        P("slab", None, "blk", None),
        P("slab", None, "blk"),
        P("slab", None, None, "blk", None),
        P("slab", None),
        P("slab", None),
        P("slab", None),
        P(),
        P(),
        P(),
    )
    return jax.shard_map(
        per_device,
        mesh=mesh,
        in_specs=placed,
        out_specs=(P("slab", None, "blk", None), P("slab", None, "blk", None), P()),
        check_vma=False,
    )
```

time: 480 us -> 106 us (0.22)
  blocking collectives: 268 us -> 0 us
  waiting for transfers between devices: 135 us -> 39.7 us
  Pallas kernels: 0 us -> 17.9 us
  local copies, waits for them, and re-layouts: 24.4 us -> 8.34 us
  other arithmetic: 22.3 us -> 8.32 us
  starting transfers between devices: 9.58 us -> 23.4 us
  between operations: 14.4 us -> 0.79 us
    psum x6 -> x0, blocking collectives: 242 us -> none  [the longest x1 42 us: per_device(): start_total = lax.psum(squared(incident), ('slab', 'blk'))]
    psum x2 -> x0, waiting for transfers between devices: 135 us -> none  [apply_operator(): slice_total = lax.psum(partial_sums, 'slab')]
    ppermute x4 -> x27, waiting for transfers between devices: 0.01 us -> 39.7 us  [the longest x25 35.5 us: trade(): lax.ppermute(value, axis, [(i, i ^ bit) for i in range(lax.axis_size(axis...]
    all_gather x4 -> x0, blocking collectives: 25.9 us -> none  [the longest x2 13.9 us: apply_operator(): full_field = lax.all_gather(rounded, 'blk', axis=2, tiled=True)]
    pallas_call x0 -> x7, Pallas kernels: none -> 17.9 us  [the longest x2 6.5 us: near_products(): pl.pallas_call(gather_body, out_shape=sources, in_specs=[SM, SM] + [VM] *...]
    gather x2 -> x0, local copies, waits for them, and re-layouts: 17.8 us -> none  [apply_operator(): sources = jnp.take(extended, source_rows, axis=0)]
    ppermute x4 -> x27, starting transfers between devices: 9.5 us -> 23.4 us  [the longest x25 17.4 us: trade(): lax.ppermute(value, axis, [(i, i ^ bit) for i in range(lax.axis_size(axis...]
    select_n x3 -> x0, other arithmetic: 8.45 us -> none  [apply_operator(): sources = jnp.take(extended, source_rows, axis=0)]
  transfers between devices with their start and end apart: 6 -> 27, of which waited for: 2 -> 18; matrix products, arithmetic and copies ran while one was open for 2% -> 11% of each run, Pallas kernels for 0% -> 6%
where the time goes in v1:
time: 106 us; the launch traced here: 105 us
  waiting for transfers between devices  39.7 us (37%)
  starting transfers between devices  23.4 us (22%)
  Pallas kernels  17.9 us (17%)
  local copies, waits for them, and re-layouts  8.34 us (8%)
  other arithmetic  8.32 us (8%)
  matrix products  6.79 us (6%)
    ppermute x25, waiting for transfers between devices, trade(): lax.ppermute(value, axis, [(i, i ^ bit) for i in range(lax.axis_size(axis...  35.5 us
    ppermute x25, starting transfers between devices, trade(): lax.ppermute(value, axis, [(i, i ^ bit) for i in range(lax.axis_size(axis...  17.4 us
    dot_general x2, matrix products, near_products(): jnp.einsum('ikarc,ikzcn->iazrn', translation, gathered, preferred_element...  6.79 us
    pallas_call x2, Pallas kernels, near_products(): pl.pallas_call(gather_body, out_shape=sources, in_specs=[SM, SM] + [VM] *...  6.5 us
    ppermute x2, starting transfers between devices, trade_odd(): return lax.ppermute(value, 'slab', pairs)  6.02 us
    unnamed x27, local copies, waits for them, and re-layouts  5.28 us
    ppermute x2, waiting for transfers between devices, trade_odd(): return lax.ppermute(value, 'slab', pairs)  4.18 us
    convert_element_type x8, other arithmetic, total_sums(): keep = keep + trade(keep.astype(bf16), axis, bit).astype(f32)  3.79 us
  transfers between devices with their start and end apart: 27, of which 18 were waited for; matrix products, arithmetic and copies ran while one was open for 11% of the time, Pallas kernels for 6%

profile of v1, /device:TPU:0, one launch (start us, length us, event | category | flops | bytes accessed | tf_op | source)
XLA Modules:
  0.0 105.3 jit_solution(8210148032701352376)
XLA Ops:
  0.7 1.7 %round.1.x_ref = bf16[2,2,84,128]{3,2,1,0:T(8,128)(2,1)} custom-call(f32[2,168,128]{2,1,0:T(8,128)} %bitcast.41), custom_call_target="tpu_custom_call" | custom-call | tf_op jit(solution)/shard_map/round/pallas_call | solution.py:345
  2.4 1.5 %copy.23.wave_ref = s32[256,3]{1,0:T(8,128)} copy(s32[256,3]{0,1:T(4,128)} %param.15) | data formatting | bytes 6144 | tf_op args[6]
  3.9 1.5 %dynamic-slice_bitcast_fusion.plane_ref = bf16[2,84,256]{2,1,0:T(8,128)(2,1)} fusion(bf16[256,2,336]{0,2,1:T(8,128)(2,1)} %param.16, s32[]{:T(128)S(6)} %select_n.3), kind=kLoop, calls=%fused_computation.24 | loop fusion | bytes 172036 | tf_op jit(solution)/shard_map/dynamic_slice | solution.py:317
  5.4 2.6 %first_sums.1 = (bf16[128,256]{1,0:T(8,128)(2,1)}, f32[128,256]{1,0:T(8,128)}, f32[256,2]{1,0:T(8,128)}, f32[256,2]{1,0:T(8,128)}) custom-call(bf16[2,2,84,128]{3,2,1,0:T(8,128)(2,1)} %round.1.x_ref, bf16[2,84,256]{2,1,0:T(8,128)(2,1)} %dynamic-slice_bitcast_fusion.plane_ref, s32[256,3]{1,0:T(8,128)} %copy.23.wave_ref, f32[2,3]{1,0:T(2,128)} %pos_ref.1), custom_call_target="tpu_custom_call" | custom-call | tf_op jit(solution)/shard_map/first_sums/pallas_call | solution.py:346
  8.0 0.5 collective-permute-start.5
  8.5 1.1 %collective-permute-done.5 = bf16[128,256]{1,0:T(8,128)(2,1)S(1)} collective-permute-done((bf16[128,256]{1,0:T(8,128)(2,1)}, bf16[128,256]{1,0:T(8,128)(2,1)S(1)}, u32[]{:S(2)}, u32[]{:S(2)}) %collective-permute-start.5) | collective-permute-done | bytes 65568 | tf_op jit(solution)/shard_map/ppermute | solution.py:263
  9.6 0.9 fusion.16
  10.5 2.9 %collective-permute-start.6 = (bf16[128,256]{1,0:T(8,128)(2,1)S(1)}, bf16[128,256]{1,0:T(8,128)(2,1)S(1)}, u32[]{:S(2)}, u32[]{:S(2)}) collective-permute-start(bf16[128,256]{1,0:T(8,128)(2,1)S(1)} %fusion.16), channel_id=1, source_target_pairs={{0,2},{1,3},{2,0},{3,1},{4,6},{5,7},{6,4},{7,5},{8,10},{9,11},{10,... | collective-permute-start | bytes 196616 | tf_op jit(solution)/shard_map/ppermute | solution.py:263
  13.4 2.4 %collective-permute-done.6 = bf16[128,256]{1,0:T(8,128)(2,1)S(1)} collective-permute-done((bf16[128,256]{1,0:T(8,128)(2,1)S(1)}, bf16[128,256]{1,0:T(8,128)(2,1)S(1)}, u32[]{:S(2)}, u32[]{:S(2)}) %collective-permute-start.6) | collective-permute-done | bytes 65568 | tf_op jit(solution)/shard_map/ppermute | solution.py:263
  15.9 0.9 fusion.25
  16.8 1.9 %collective-permute-start.7 = (bf16[128,256]{1,0:T(8,128)(2,1)S(1)}, bf16[128,256]{1,0:T(8,128)(2,1)S(1)}, u32[]{:S(2)}, u32[]{:S(2)}) collective-permute-start(bf16[128,256]{1,0:T(8,128)(2,1)S(1)} %get-tuple-element.35), channel_id=1, source_target_pairs={{0,4},{4,0},{8,12},{12,8},{16,20},{20,16},{24,28},{28,24},{1,5},{5... | collective-permute-start | bytes 196616 | tf_op jit(solution)/shard_map/ppermute | solution.py:263
  18.7 3.6 %collective-permute-start.1 = (bf16[2,2,84,128]{3,2,1,0:T(8,128)(2,1)}, bf16[2,2,84,128]{3,2,1,0:T(8,128)(2,1)S(1)}, u32[]{:S(2)}, u32[]{:S(2)}) collective-permute-start(bf16[2,2,84,128]{3,2,1,0:T(8,128)(2,1)} %round.1.x_ref), channel_id=1, source_target_pairs={{0,28},{4,8},{8,4},{12,16},{16,12},{20,24},{24,20},{28,0},{1,29},{... | collective-permute-start | bytes 258056 | tf_op jit(solution)/shard_map/ppermute | solution.py:271
  22.3 2.1 %collective-permute-start.8 = (bf16[128,256]{1,0:T(8,128)(2,1)S(1)}, bf16[128,256]{1,0:T(8,128)(2,1)S(1)}, u32[]{:S(2)}, u32[]{:S(2)}) collective-permute-start(bf16[128,256]{1,0:T(8,128)(2,1)S(1)} %fusion.17), channel_id=1, source_target_pairs={{0,8},{4,12},{8,0},{12,4},{16,24},{20,28},{24,16},{28,20},{1,9},{5... | collective-permute-start | bytes 196616 | tf_op jit(solution)/shard_map/ppermute | solution.py:263
  24.4 2.4 %collective-permute-done.1 = bf16[2,2,84,128]{3,2,1,0:T(8,128)(2,1)S(1)} collective-permute-done((bf16[2,2,84,128]{3,2,1,0:T(8,128)(2,1)}, bf16[2,2,84,128]{3,2,1,0:T(8,128)(2,1)S(1)}, u32[]{:S(2)}, u32[]{:S(2)}) %collective-permute-start.1) | collective-permute-done | bytes 86048 | tf_op jit(solution)/shard_map/ppermute | solution.py:271
  26.7 0.8 collective-permute-done
  27.5 0.9 pad_maximum_fusion.refs_0_
  28.5 1.6 %collective-permute-start.3 = (bf16[3,2,2,84,128]{4,3,2,1,0:T(8,128)(2,1)S(1)}, bf16[3,2,2,84,128]{4,3,2,1,0:T(8,128)(2,1)S(1)}, u32[]{:S(2)}, u32[]{:S(2)}) collective-permute-start(bf16[3,2,2,84,128]{4,3,2,1,0:T(8,128)(2,1)S(1)} %pad_maximum_fusion.refs_0_), channel_id=1, source_target_pairs={{0,2},{1,3},{2,0},{3,1},{4,6},{5,7},{6,4},{7,5},{8,10},{9,11},{10,... | collective-permute-start | bytes 774152 | tf_op jit(solution)/shard_map/ppermute | solution.py:263
  30.1 0.5 collective-permute-start.9
  30.5 4.4 %collective-permute-done.3.refs_2_ = bf16[3,2,2,84,128]{4,3,2,1,0:T(8,128)(2,1)S(1)} collective-permute-done((bf16[3,2,2,84,128]{4,3,2,1,0:T(8,128)(2,1)S(1)}, bf16[3,2,2,84,128]{4,3,2,1,0:T(8,128)(2,1)S(1)}, u32[]{:S(2)}, u32[]{:S(2)}) %collective-permute-start.3) | collective-permute-done | bytes 258080 | tf_op jit(solution)/shard_map/ppermute | solution.py:263
  35.0 0.7 copy.25.mie_ref
  35.7 0.8 copy.24.weight_ref
  36.5 0.7 fusion.24
  37.2 0.5 collective-permute-start.10
  37.8 0.7 copy-done.5
  38.4 0.7 copy-done.7
  39.1 3.3 %gather.2 = bf16[2,8,2,336,128]{4,3,2,1,0:T(8,128)(2,1)} custom-call(s32[2,8]{1,0:T(2,128)} %shift_ref.3, s32[2,8]{1,0:T(2,128)} %member_ref.3, bf16[3,2,2,84,128]{4,3,2,1,0:T(8,128)(2,1)} %copy-done.1, bf16[3,2,2,84,128]{4,3,2,1,0:T(8,128)(2,1)} %copy-done.5, bf16[3,2,2,84,128]{4,3,2,1,0:T(8,128)(2,1)} %copy-done.3, bf16[3,2,2,84,128]{4,3,2,1,0:T(8,128)(2,1)} %copy-done.7), custom_call_target="tpu_custom_call" | custom-call | tf_op jit(solution)/shard_map/gather/pallas_call | solution.py:333
  42.4 3.4 %fusion.6.near_ref = f32[2,2,2,84,128]{4,3,2,1,0:T(8,128)} fusion(bf16[2,8,2,84,336,1]{4,2,3,1,0,5:T(2,128)(2,1)S(1)} %bitcast.39, bf16[2,8,2,336,128]{4,3,2,1,0:T(8,128)(2,1)} %gather.2), kind=kOutput, calls=%fused_computation.6 | convolution fusion | flops 462422016 | bytes 4902912 | tf_op jit(solution)/shard_map/ikarc,ikzcn->iazrn/dot_general | solution.py:341
  45.8 0.6 copy-done.10
  46.4 2.6 %first_image.1 = (f32[2,2,84,128]{3,2,1,0:T(8,128)}, bf16[2,2,84,128]{3,2,1,0:T(8,128)(2,1)}, bf16[128,256]{1,0:T(8,128)(2,1)}, f32[128,256]{1,0:T(8,128)}) custom-call(f32[2,2,2,84,128]{4,3,2,1,0:T(8,128)} %fusion.6.near_ref, f32[128,256]{1,0:T(8,128)} %get-tuple-element.34.mine_ref, bf16[128,256]{1,0:T(8,128)(2,1)} %copy-done.10, ...), custom_call_target="tpu_custom_call" | custom-call | tf_op jit(solution)/shard_map/first_image/pallas_call | solution.py:351
  49.0 1.5 %collective-permute-done.16 = bf16[128,256]{1,0:T(8,128)(2,1)S(1)} collective-permute-done((bf16[128,256]{1,0:T(8,128)(2,1)}, bf16[128,256]{1,0:T(8,128)(2,1)S(1)}, u32[]{:S(2)}, u32[]{:S(2)}) %collective-permute-start.16) | collective-permute-done | bytes 65568 | tf_op jit(solution)/shard_map/ppermute | solution.py:263
  50.5 0.9 fusion.18
  51.4 1.6 %collective-permute-start.17 = (bf16[128,256]{1,0:T(8,128)(2,1)S(1)}, bf16[128,256]{1,0:T(8,128)(2,1)S(1)}, u32[]{:S(2)}, u32[]{:S(2)}) collective-permute-start(bf16[128,256]{1,0:T(8,128)(2,1)S(1)} %fusion.18), channel_id=1, source_target_pairs={{0,2},{1,3},{2,0},{3,1},{4,6},{5,7},{6,4},{7,5},{8,10},{9,11},{10,... | collective-permute-start | bytes 196616 | tf_op jit(solution)/shard_map/ppermute | solution.py:263
  53.0 2.7 %collective-permute-done.17 = bf16[128,256]{1,0:T(8,128)(2,1)S(1)} collective-permute-done((bf16[128,256]{1,0:T(8,128)(2,1)S(1)}, bf16[128,256]{1,0:T(8,128)(2,1)S(1)}, u32[]{:S(2)}, u32[]{:S(2)}) %collective-permute-start.17) | collective-permute-done | bytes 65568 | tf_op jit(solution)/shard_map/ppermute | solution.py:263
  55.8 0.9 fusion.23
  56.7 0.1 collective-permute-start.18
  56.8 2.4 %collective-permute-start.12 = (bf16[2,2,84,128]{3,2,1,0:T(8,128)(2,1)}, bf16[2,2,84,128]{3,2,1,0:T(8,128)(2,1)S(1)}, u32[]{:S(2)}, u32[]{:S(2)}) collective-permute-start(bf16[2,2,84,128]{3,2,1,0:T(8,128)(2,1)} %get-tuple-element.20), channel_id=1, source_target_pairs={{0,28},{4,8},{8,4},{12,16},{16,12},{20,24},{24,20},{28,0},{1,29},{... | collective-permute-start | bytes 258056 | tf_op jit(solution)/shard_map/ppermute | solution.py:271
  59.3 3.2 %collective-permute-done.18 = bf16[128,256]{1,0:T(8,128)(2,1)S(1)} collective-permute-done((bf16[128,256]{1,0:T(8,128)(2,1)S(1)}, bf16[128,256]{1,0:T(8,128)(2,1)S(1)}, u32[]{:S(2)}, u32[]{:S(2)}) %collective-permute-start.18) | collective-permute-done | bytes 65568 | tf_op jit(solution)/shard_map/ppermute | solution.py:263
  62.6 1.8 %collective-permute-done.12 = bf16[2,2,84,128]{3,2,1,0:T(8,128)(2,1)S(1)} collective-permute-done((bf16[2,2,84,128]{3,2,1,0:T(8,128)(2,1)}, bf16[2,2,84,128]{3,2,1,0:T(8,128)(2,1)S(1)}, u32[]{:S(2)}, u32[]{:S(2)}) %collective-permute-start.12) | collective-permute-done | bytes 86048 | tf_op jit(solution)/shard_map/ppermute | solution.py:271
  64.4 0.5 collective-permute-done.11
  64.9 0.9 pad_maximum_fusion.1.refs_0_
  65.8 1.6 %collective-permute-start.14 = (bf16[3,2,2,84,128]{4,3,2,1,0:T(8,128)(2,1)S(1)}, bf16[3,2,2,84,128]{4,3,2,1,0:T(8,128)(2,1)S(1)}, u32[]{:S(2)}, u32[]{:S(2)}) collective-permute-start(bf16[3,2,2,84,128]{4,3,2,1,0:T(8,128)(2,1)S(1)} %pad_maximum_fusion.1.refs_0_), channel_id=1, source_target_pairs={{0,2},{1,3},{2,0},{3,1},{4,6},{5,7},{6,4},{7,5},{8,10},{9,11},{10,... | collective-permute-start | bytes 774152 | tf_op jit(solution)/shard_map/ppermute | solution.py:263
  67.5 0.5 collective-permute-start.20
  68.0 4.4 %collective-permute-done.14.refs_2_ = bf16[3,2,2,84,128]{4,3,2,1,0:T(8,128)(2,1)S(1)} collective-permute-done((bf16[3,2,2,84,128]{4,3,2,1,0:T(8,128)(2,1)S(1)}, bf16[3,2,2,84,128]{4,3,2,1,0:T(8,128)(2,1)S(1)}, u32[]{:S(2)}, u32[]{:S(2)}) %collective-permute-start.14) | collective-permute-done | bytes 258080 | tf_op jit(solution)/shard_map/ppermute | solution.py:263
  72.5 0.6 collective-permute-done.20
  73.0 0.7 fusion.22
  73.7 0.3 collective-permute-done.15.refs_3_
  74.0 0.4 copy-done.6
  74.4 0.7 copy-done.8
  75.1 3.3 %gather.3 = bf16[2,8,2,336,128]{4,3,2,1,0:T(8,128)(2,1)} custom-call(s32[2,8]{1,0:T(2,128)} %shift_ref.3, s32[2,8]{1,0:T(2,128)} %member_ref.3, bf16[3,2,2,84,128]{4,3,2,1,0:T(8,128)(2,1)} %copy-done.2, bf16[3,2,2,84,128]{4,3,2,1,0:T(8,128)(2,1)} %copy-done.6, bf16[3,2,2,84,128]{4,3,2,1,0:T(8,128)(2,1)} %copy-done.4, bf16[3,2,2,84,128]{4,3,2,1,0:T(8,128)(2,1)} %copy-done.8), custom_call_target="tpu_custom_call" | custom-call | tf_op jit(solution)/shard_map/gather/pallas_call | solution.py:333
  78.4 3.4 %fusion.11.near_ref = f32[2,2,2,84,128]{4,3,2,1,0:T(8,128)} fusion(bf16[2,8,2,84,336,1]{4,2,3,1,0,5:T(2,128)(2,1)S(1)} %bitcast.40, bf16[2,8,2,336,128]{4,3,2,1,0:T(8,128)(2,1)} %gather.3), kind=kOutput, calls=%fused_computation.7 | convolution fusion | flops 462422016 | bytes 4902912 | tf_op jit(solution)/shard_map/ikarc,ikzcn->iazrn/dot_general | solution.py:341
  81.8 0.6 copy-done.9
  82.4 2.5 %second_image.1 = (f32[2,2,84,128]{3,2,1,0:T(8,128)}, f32[16,128]{1,0:T(8,128)}) custom-call(f32[2,2,2,84,128]{4,3,2,1,0:T(8,128)} %fusion.11.near_ref, f32[128,256]{1,0:T(8,128)} %get-tuple-element.30.mine_ref, bf16[128,256]{1,0:T(8,128)(2,1)} %copy-done.9, f32[256,2]{1,0:T(8,128)} %get-tuple-element.18.cos_ref, f32[256,2]{1,0:T(8,128)} %get-tuple-element.19.sin_ref, ...), custom_call_target="tpu_custom_call" | custom-call | tf_op jit(solution)/shard_map/second_image/pallas_call | solution.py:357
  85.0 0.5 collective-permute-start.22
  85.5 1.0 collective-permute-done.22
  86.5 0.7 add.59
  87.2 1.3 %collective-permute-start.23 = (f32[16,128]{1,0:T(8,128)S(1)}, f32[16,128]{1,0:T(8,128)S(1)}, u32[]{:S(2)}, u32[]{:S(2)}) collective-permute-start(f32[16,128]{1,0:T(8,128)S(1)} %add.59), channel_id=1, source_target_pairs={{0,2},{1,3},{2,0},{3,1},{4,6},{5,7},{6,4},{7,5},{8,10},{9,11},{10,... | collective-permute-start | bytes 24584 | tf_op jit(solution)/shard_map/ppermute | solution.py:263
  88.5 2.4 %collective-permute-done.23 = f32[16,128]{1,0:T(8,128)S(1)} collective-permute-done((f32[16,128]{1,0:T(8,128)S(1)}, f32[16,128]{1,0:T(8,128)S(1)}, u32[]{:S(2)}, u32[]{:S(2)}) %collective-permute-start.23) | collective-permute-done | bytes 8224 | tf_op jit(solution)/shard_map/ppermute | solution.py:263
  90.9 0.4 collective-permute-start.24
  91.2 3.3 %collective-permute-done.24 = f32[16,128]{1,0:T(8,128)S(1)} collective-permute-done((f32[16,128]{1,0:T(8,128)S(1)}, f32[16,128]{1,0:T(8,128)S(1)}, u32[]{:S(2)}, u32[]{:S(2)}) %collective-permute-start.24) | collective-permute-done | bytes 8224 | tf_op jit(solution)/shard_map/ppermute | solution.py:263
  94.5 3.6 %collective-permute-done.25 = f32[16,128]{1,0:T(8,128)S(1)} collective-permute-done((f32[16,128]{1,0:T(8,128)S(1)}, f32[16,128]{1,0:T(8,128)S(1)}, u32[]{:S(2)}, u32[]{:S(2)}) %collective-permute-start.25) | collective-permute-done | bytes 8224 | tf_op jit(solution)/shard_map/ppermute | solution.py:263
  98.2 1.4 %collective-permute-start.26 = (f32[16,128]{1,0:T(8,128)S(1)}, f32[16,128]{1,0:T(8,128)S(1)}, u32[]{:S(2)}, u32[]{:S(2)}) collective-permute-start(f32[16,128]{1,0:T(8,128)S(1)} %add.62), channel_id=1, source_target_pairs={{0,16},{4,20},{8,24},{12,28},{16,0},{20,4},{24,8},{28,12},{1,17},{... | collective-permute-start | bytes 24584 | tf_op jit(solution)/shard_map/ppermute | solution.py:263
  99.6 3.2 %collective-permute-done.26 = f32[16,128]{1,0:T(8,128)S(1)} collective-permute-done((f32[16,128]{1,0:T(8,128)S(1)}, f32[16,128]{1,0:T(8,128)S(1)}, u32[]{:S(2)}, u32[]{:S(2)}) %collective-permute-start.26) | collective-permute-done | bytes 8224 | tf_op jit(solution)/shard_map/ppermute | solution.py:263
  102.7 0.6 add.63.refs_0_
  103.3 2.0 %finish.1 = (f32[2,168,128]{2,1,0:T(8,128)}, f32[2,168,128]{2,1,0:T(8,128)}, f32[9,128]{1,0:T(8,128)}) custom-call(f32[16,128]{1,0:T(8,128)} %add.63.refs_0_, f32[2,168,128]{2,1,0:T(8,128)} %bitcast.43, f32[2,2,84,128]{3,2,1,0:T(8,128)} %get-tuple-element.23.g_ref.refs_2_, f32[2,2,84,128]{3,2,1,0:T(8,128)} %get-tuple-element.25.refs_3_), custom_call_target="tpu_custom_call" | custom-call | tf_op jit(solution)/shard_map/finish/pallas_call | solution.py:362
  (46 shorter events, 0.3 us)
Async XLA Ops:
  0.6 41.8 %copy-start = (bf16[2,8,2,84,336]{4,2,3,1,0:T(2,128)(2,1)S(1)}, bf16[2,8,2,84,336]{4,2,3,1,0:T(2,128)(2,1)}, u32[]{:S(2)}) copy-start(bf16[2,8,2,84,336]{4,2,3,1,0:T(2,128)(2,1)} %param.11) | copy-start | bytes 5419012
  0.6 34.4 %copy-start.11 = (f32[2,2,84]{2,1,0:T(2,128)S(1)}, f32[2,2,84]{2,1,0:T(2,128)}, u32[]{:S(2)}) copy-start(f32[2,2,84]{2,1,0:T(2,128)} %param.10) | copy-start | bytes 4036
  0.7 35.1 %copy-start.12 = (f32[256]{0:T(256)S(1)}, f32[256]{0:T(256)}, u32[]{:S(2)}) copy-start(f32[256]{0:T(256)} %param.17) | copy-start | bytes 3076
  8.0 1.6 %collective-permute-start.5 = (bf16[128,256]{1,0:T(8,128)(2,1)}, bf16[128,256]{1,0:T(8,128)(2,1)S(1)}, u32[]{:S(2)}, u32[]{:S(2)}) collective-permute-start(bf16[128,256]{1,0:T(8,128)(2,1)} %get-tuple-element.17), channel_id=1, source_target_pairs={{0,1},{1,0},{2,3},{3,2},{4,5},{5,4},{6,7},{7,6},{8,9},{9,8},{10,11... | collective-permute-start | bytes 196616 | tf_op jit(solution)/shard_map/ppermute | solution.py:263
  10.5 5.3 %collective-permute-start.6 = (bf16[128,256]{1,0:T(8,128)(2,1)S(1)}, bf16[128,256]{1,0:T(8,128)(2,1)S(1)}, u32[]{:S(2)}, u32[]{:S(2)}) collective-permute-start(bf16[128,256]{1,0:T(8,128)(2,1)S(1)} %fusion.16), channel_id=1, source_target_pairs={{0,2},{1,3},{2,0},{3,1},{4,6},{5,7},{6,4},{7,5},{8,10},{9,11},{10,... | collective-permute-start | bytes 196616 | tf_op jit(solution)/shard_map/ppermute | solution.py:263
  16.8 5.5 %collective-permute-start.7 = (bf16[128,256]{1,0:T(8,128)(2,1)S(1)}, bf16[128,256]{1,0:T(8,128)(2,1)S(1)}, u32[]{:S(2)}, u32[]{:S(2)}) collective-permute-start(bf16[128,256]{1,0:T(8,128)(2,1)S(1)} %get-tuple-element.35), channel_id=1, source_target_pairs={{0,4},{4,0},{8,12},{12,8},{16,20},{20,16},{24,28},{28,24},{1,5},{5... | collective-permute-start | bytes 196616 | tf_op jit(solution)/shard_map/ppermute | solution.py:263
  18.7 8.0 %collective-permute-start.1 = (bf16[2,2,84,128]{3,2,1,0:T(8,128)(2,1)}, bf16[2,2,84,128]{3,2,1,0:T(8,128)(2,1)S(1)}, u32[]{:S(2)}, u32[]{:S(2)}) collective-permute-start(bf16[2,2,84,128]{3,2,1,0:T(8,128)(2,1)} %round.1.x_ref), channel_id=1, source_target_pairs={{0,28},{4,8},{8,4},{12,16},{16,12},{20,24},{24,20},{28,0},{1,29},{... | collective-permute-start | bytes 258056 | tf_op jit(solution)/shard_map/ppermute | solution.py:271
  22.3 5.3 %collective-permute-start = (bf16[2,2,84,128]{3,2,1,0:T(8,128)(2,1)}, bf16[2,2,84,128]{3,2,1,0:T(8,128)(2,1)S(1)}, u32[]{:S(2)}, u32[]{:S(2)}) collective-permute-start(bf16[2,2,84,128]{3,2,1,0:T(8,128)(2,1)} %round.1.x_ref), channel_id=1, source_target_pairs={{0,4},{4,0},{8,12},{12,8},{16,20},{20,16},{24,28},{28,24},{1,5},{5... | collective-permute-start | bytes 258056 | tf_op jit(solution)/shard_map/ppermute | solution.py:263
  22.3 7.8 %collective-permute-start.8 = (bf16[128,256]{1,0:T(8,128)(2,1)S(1)}, bf16[128,256]{1,0:T(8,128)(2,1)S(1)}, u32[]{:S(2)}, u32[]{:S(2)}) collective-permute-start(bf16[128,256]{1,0:T(8,128)(2,1)S(1)} %fusion.17), channel_id=1, source_target_pairs={{0,8},{4,12},{8,0},{12,4},{16,24},{20,28},{24,16},{28,20},{1,9},{5... | collective-permute-start | bytes 196616 | tf_op jit(solution)/shard_map/ppermute | solution.py:263
  28.5 9.3 %copy-start.1 = (bf16[3,2,2,84,128]{4,3,2,1,0:T(8,128)(2,1)}, bf16[3,2,2,84,128]{4,3,2,1,0:T(8,128)(2,1)S(1)}, u32[]{:S(2)}) copy-start(bf16[3,2,2,84,128]{4,3,2,1,0:T(8,128)(2,1)S(1)} %pad_maximum_fusion.refs_0_) | copy-start | bytes 774148
  28.5 6.5 %collective-permute-start.3 = (bf16[3,2,2,84,128]{4,3,2,1,0:T(8,128)(2,1)S(1)}, bf16[3,2,2,84,128]{4,3,2,1,0:T(8,128)(2,1)S(1)}, u32[]{:S(2)}, u32[]{:S(2)}) collective-permute-start(bf16[3,2,2,84,128]{4,3,2,1,0:T(8,128)(2,1)S(1)} %pad_maximum_fusion.refs_0_), channel_id=1, source_target_pairs={{0,2},{1,3},{2,0},{3,1},{4,6},{5,7},{6,4},{7,5},{8,10},{9,11},{10,... | collective-permute-start | bytes 774152 | tf_op jit(solution)/shard_map/ppermute | solution.py:263
  30.1 6.4 %collective-permute-start.9 = (bf16[128,256]{1,0:T(8,128)(2,1)S(1)}, bf16[128,256]{1,0:T(8,128)(2,1)S(1)}, u32[]{:S(2)}, u32[]{:S(2)}) collective-permute-start(bf16[128,256]{1,0:T(8,128)(2,1)S(1)} %fusion.20), channel_id=1, source_target_pairs={{0,16},{4,20},{8,24},{12,28},{16,0},{20,4},{24,8},{28,12},{1,17},{... | collective-permute-start | bytes 196616 | tf_op jit(solution)/shard_map/ppermute | solution.py:263
  30.5 7.2 %collective-permute-start.2 = (bf16[3,2,2,84,128]{4,3,2,1,0:T(8,128)(2,1)S(1)}, bf16[3,2,2,84,128]{4,3,2,1,0:T(8,128)(2,1)S(1)}, u32[]{:S(2)}, u32[]{:S(2)}) collective-permute-start(bf16[3,2,2,84,128]{4,3,2,1,0:T(8,128)(2,1)S(1)} %pad_maximum_fusion.refs_0_), channel_id=1, source_target_pairs={{0,1},{1,0},{2,3},{3,2},{4,5},{5,4},{6,7},{7,6},{8,9},{9,8},{10,11... | collective-permute-start | bytes 774152 | tf_op jit(solution)/shard_map/ppermute | solution.py:263
  35.0 2.8 %copy-start.3 = (bf16[3,2,2,84,128]{4,3,2,1,0:T(8,128)(2,1)}, bf16[3,2,2,84,128]{4,3,2,1,0:T(8,128)(2,1)S(1)}, u32[]{:S(2)}) copy-start(bf16[3,2,2,84,128]{4,3,2,1,0:T(8,128)(2,1)S(1)} %collective-permute-done.3.refs_2_) | copy-start | bytes 774148
  35.0 2.7 %collective-permute-start.4 = (bf16[3,2,2,84,128]{4,3,2,1,0:T(8,128)(2,1)S(1)}, bf16[3,2,2,84,128]{4,3,2,1,0:T(8,128)(2,1)S(1)}, u32[]{:S(2)}, u32[]{:S(2)}) collective-permute-start(bf16[3,2,2,84,128]{4,3,2,1,0:T(8,128)(2,1)S(1)} %collective-permute-done.3.refs_2_), channel_id=1, source_target_pairs={{0,1},{1,0},{2,3},{3,2},{4,5},{5,4},{6,7},{7,6},{8,9},{9,8},{10,11... | collective-permute-start | bytes 774152 | tf_op jit(solution)/shard_map/ppermute | solution.py:263
  37.2 8.6 %collective-permute-start.10 = (bf16[128,256]{1,0:T(8,128)(2,1)S(1)}, bf16[128,256]{1,0:T(8,128)(2,1)S(1)}, u32[]{:S(2)}, u32[]{:S(2)}) collective-permute-start(bf16[128,256]{1,0:T(8,128)(2,1)S(1)} %get-tuple-element.33), channel_id=1, source_target_pairs={{0,1},{1,0},{2,3},{3,2},{4,5},{5,4},{6,7},{7,6},{8,9},{9,8},{10,11... | collective-permute-start | bytes 196616 | tf_op jit(solution)/shard_map/ppermute | solution.py:263
  37.7 0.7 copy-start.5
  38.4 0.7 copy-start.7
  45.8 0.6 copy-start.10
  49.0 1.5 %collective-permute-start.16 = (bf16[128,256]{1,0:T(8,128)(2,1)}, bf16[128,256]{1,0:T(8,128)(2,1)S(1)}, u32[]{:S(2)}, u32[]{:S(2)}) collective-permute-start(bf16[128,256]{1,0:T(8,128)(2,1)} %get-tuple-element.22), channel_id=1, source_target_pairs={{0,1},{1,0},{2,3},{3,2},{4,5},{5,4},{6,7},{7,6},{8,9},{9,8},{10,11... | collective-permute-start | bytes 196616 | tf_op jit(solution)/shard_map/ppermute | solution.py:263
  51.4 4.3 %collective-permute-start.17 = (bf16[128,256]{1,0:T(8,128)(2,1)S(1)}, bf16[128,256]{1,0:T(8,128)(2,1)S(1)}, u32[]{:S(2)}, u32[]{:S(2)}) collective-permute-start(bf16[128,256]{1,0:T(8,128)(2,1)S(1)} %fusion.18), channel_id=1, source_target_pairs={{0,2},{1,3},{2,0},{3,1},{4,6},{5,7},{6,4},{7,5},{8,10},{9,11},{10,... | collective-permute-start | bytes 196616 | tf_op jit(solution)/shard_map/ppermute | solution.py:263
  56.7 5.8 %collective-permute-start.18 = (bf16[128,256]{1,0:T(8,128)(2,1)S(1)}, bf16[128,256]{1,0:T(8,128)(2,1)S(1)}, u32[]{:S(2)}, u32[]{:S(2)}) collective-permute-start(bf16[128,256]{1,0:T(8,128)(2,1)S(1)} %get-tuple-element.31), channel_id=1, source_target_pairs={{0,4},{4,0},{8,12},{12,8},{16,20},{20,16},{24,28},{28,24},{1,5},{5... | collective-permute-start | bytes 196616 | tf_op jit(solution)/shard_map/ppermute | solution.py:263
  56.8 7.6 %collective-permute-start.12 = (bf16[2,2,84,128]{3,2,1,0:T(8,128)(2,1)}, bf16[2,2,84,128]{3,2,1,0:T(8,128)(2,1)S(1)}, u32[]{:S(2)}, u32[]{:S(2)}) collective-permute-start(bf16[2,2,84,128]{3,2,1,0:T(8,128)(2,1)} %get-tuple-element.20), channel_id=1, source_target_pairs={{0,28},{4,8},{8,4},{12,16},{16,12},{20,24},{24,20},{28,0},{1,29},{... | collective-permute-start | bytes 258056 | tf_op jit(solution)/shard_map/ppermute | solution.py:271
  59.2 5.7 %collective-permute-start.11 = (bf16[2,2,84,128]{3,2,1,0:T(8,128)(2,1)}, bf16[2,2,84,128]{3,2,1,0:T(8,128)(2,1)S(1)}, u32[]{:S(2)}, u32[]{:S(2)}) collective-permute-start(bf16[2,2,84,128]{3,2,1,0:T(8,128)(2,1)} %get-tuple-element.20), channel_id=1, source_target_pairs={{0,4},{4,0},{8,12},{12,8},{16,20},{20,16},{24,28},{28,24},{1,5},{5... | collective-permute-start | bytes 258056 | tf_op jit(solution)/shard_map/ppermute | solution.py:263
  62.5 5.0 %collective-permute-start.19 = (bf16[128,256]{1,0:T(8,128)(2,1)S(1)}, bf16[128,256]{1,0:T(8,128)(2,1)S(1)}, u32[]{:S(2)}, u32[]{:S(2)}) collective-permute-start(bf16[128,256]{1,0:T(8,128)(2,1)S(1)} %fusion.19), channel_id=1, source_target_pairs={{0,8},{4,12},{8,0},{12,4},{16,24},{20,28},{24,16},{28,20},{1,9},{5... | collective-permute-start | bytes 196616 | tf_op jit(solution)/shard_map/ppermute | solution.py:263
  65.8 8.2 %copy-start.2 = (bf16[3,2,2,84,128]{4,3,2,1,0:T(8,128)(2,1)}, bf16[3,2,2,84,128]{4,3,2,1,0:T(8,128)(2,1)S(1)}, u32[]{:S(2)}) copy-start(bf16[3,2,2,84,128]{4,3,2,1,0:T(8,128)(2,1)S(1)} %pad_maximum_fusion.1.refs_0_) | copy-start | bytes 774148
  65.8 6.6 %collective-permute-start.14 = (bf16[3,2,2,84,128]{4,3,2,1,0:T(8,128)(2,1)S(1)}, bf16[3,2,2,84,128]{4,3,2,1,0:T(8,128)(2,1)S(1)}, u32[]{:S(2)}, u32[]{:S(2)}) collective-permute-start(bf16[3,2,2,84,128]{4,3,2,1,0:T(8,128)(2,1)S(1)} %pad_maximum_fusion.1.refs_0_), channel_id=1, source_target_pairs={{0,2},{1,3},{2,0},{3,1},{4,6},{5,7},{6,4},{7,5},{8,10},{9,11},{10,... | collective-permute-start | bytes 774152 | tf_op jit(solution)/shard_map/ppermute | solution.py:263
  67.5 5.5 %collective-permute-start.20 = (bf16[128,256]{1,0:T(8,128)(2,1)S(1)}, bf16[128,256]{1,0:T(8,128)(2,1)S(1)}, u32[]{:S(2)}, u32[]{:S(2)}) collective-permute-start(bf16[128,256]{1,0:T(8,128)(2,1)S(1)} %fusion.21), channel_id=1, source_target_pairs={{0,16},{4,20},{8,24},{12,28},{16,0},{20,4},{24,8},{28,12},{1,17},{... | collective-permute-start | bytes 196616 | tf_op jit(solution)/shard_map/ppermute | solution.py:263
  68.0 5.7 %collective-permute-start.13 = (bf16[3,2,2,84,128]{4,3,2,1,0:T(8,128)(2,1)S(1)}, bf16[3,2,2,84,128]{4,3,2,1,0:T(8,128)(2,1)S(1)}, u32[]{:S(2)}, u32[]{:S(2)}) collective-permute-start(bf16[3,2,2,84,128]{4,3,2,1,0:T(8,128)(2,1)S(1)} %pad_maximum_fusion.1.refs_0_), channel_id=1, source_target_pairs={{0,1},{1,0},{2,3},{3,2},{4,5},{5,4},{6,7},{7,6},{8,9},{9,8},{10,11... | collective-permute-start | bytes 774152 | tf_op jit(solution)/shard_map/ppermute | solution.py:263
  72.5 1.6 %copy-start.4 = (bf16[3,2,2,84,128]{4,3,2,1,0:T(8,128)(2,1)}, bf16[3,2,2,84,128]{4,3,2,1,0:T(8,128)(2,1)S(1)}, u32[]{:S(2)}) copy-start(bf16[3,2,2,84,128]{4,3,2,1,0:T(8,128)(2,1)S(1)} %collective-permute-done.14.refs_2_) | copy-start | bytes 774148
  72.5 1.5 %collective-permute-start.15 = (bf16[3,2,2,84,128]{4,3,2,1,0:T(8,128)(2,1)S(1)}, bf16[3,2,2,84,128]{4,3,2,1,0:T(8,128)(2,1)S(1)}, u32[]{:S(2)}, u32[]{:S(2)}) collective-permute-start(bf16[3,2,2,84,128]{4,3,2,1,0:T(8,128)(2,1)S(1)} %collective-permute-done.14.refs_2_), channel_id=1, source_target_pairs={{0,1},{1,0},{2,3},{3,2},{4,5},{5,4},{6,7},{7,6},{8,9},{9,8},{10,11... | collective-permute-start | bytes 774152 | tf_op jit(solution)/shard_map/ppermute | solution.py:263
  73.7 8.1 %collective-permute-start.21 = (bf16[128,256]{1,0:T(8,128)(2,1)S(1)}, bf16[128,256]{1,0:T(8,128)(2,1)S(1)}, u32[]{:S(2)}, u32[]{:S(2)}) collective-permute-start(bf16[128,256]{1,0:T(8,128)(2,1)S(1)} %get-tuple-element.29), channel_id=1, source_target_pairs={{0,1},{1,0},{2,3},{3,2},{4,5},{5,4},{6,7},{7,6},{8,9},{9,8},{10,11... | collective-permute-start | bytes 196616 | tf_op jit(solution)/shard_map/ppermute | solution.py:263
  73.7 0.7 copy-start.6
  74.4 0.7 copy-start.8
  81.8 0.6 copy-start.9
  85.0 1.5 %collective-permute-start.22 = (f32[16,128]{1,0:T(8,128)}, f32[16,128]{1,0:T(8,128)S(1)}, u32[]{:S(2)}, u32[]{:S(2)}) collective-permute-start(f32[16,128]{1,0:T(8,128)} %get-tuple-element.24), channel_id=1, source_target_pairs={{0,1},{1,0},{2,3},{3,2},{4,5},{5,4},{6,7},{7,6},{8,9},{9,8},{10,11... | collective-permute-start | bytes 24584 | tf_op jit(solution)/shard_map/ppermute | solution.py:263
  87.2 3.7 %collective-permute-start.23 = (f32[16,128]{1,0:T(8,128)S(1)}, f32[16,128]{1,0:T(8,128)S(1)}, u32[]{:S(2)}, u32[]{:S(2)}) collective-permute-start(f32[16,128]{1,0:T(8,128)S(1)} %add.59), channel_id=1, source_target_pairs={{0,2},{1,3},{2,0},{3,1},{4,6},{5,7},{6,4},{7,5},{8,10},{9,11},{10,... | collective-permute-start | bytes 24584 | tf_op jit(solution)/shard_map/ppermute | solution.py:263
  90.9 3.7 %collective-permute-start.24 = (f32[16,128]{1,0:T(8,128)S(1)}, f32[16,128]{1,0:T(8,128)S(1)}, u32[]{:S(2)}, u32[]{:S(2)}) collective-permute-start(f32[16,128]{1,0:T(8,128)S(1)} %add.60), channel_id=1, source_target_pairs={{0,4},{4,0},{8,12},{12,8},{16,20},{20,16},{24,28},{28,24},{1,5},{5... | collective-permute-start | bytes 24584 | tf_op jit(solution)/shard_map/ppermute | solution.py:263
  94.5 3.7 %collective-permute-start.25 = (f32[16,128]{1,0:T(8,128)S(1)}, f32[16,128]{1,0:T(8,128)S(1)}, u32[]{:S(2)}, u32[]{:S(2)}) collective-permute-start(f32[16,128]{1,0:T(8,128)S(1)} %add.61), channel_id=1, source_target_pairs={{0,8},{4,12},{8,0},{12,4},{16,24},{20,28},{24,16},{28,20},{1,9},{5... | collective-permute-start | bytes 24584 | tf_op jit(solution)/shard_map/ppermute | solution.py:263
  98.2 4.5 %collective-permute-start.26 = (f32[16,128]{1,0:T(8,128)S(1)}, f32[16,128]{1,0:T(8,128)S(1)}, u32[]{:S(2)}, u32[]{:S(2)}) collective-permute-start(f32[16,128]{1,0:T(8,128)S(1)} %add.62), channel_id=1, source_target_pairs={{0,16},{4,20},{8,24},{12,28},{16,0},{20,4},{24,8},{28,12},{1,17},{... | collective-permute-start | bytes 24584 | tf_op jit(solution)/shard_map/ppermute | solution.py:263

commit v2 on v1

--- a/solution.py
+++ b/solution.py
@@ -14,12 +14,14 @@
 SM = pl.BlockSpec(memory_space=pltpu.SMEM)
 
 
-def call(body, outs, specs, name):
+def call(body, outs, specs, name, scratch=()):
     return pl.pallas_call(
         body,
         out_shape=outs,
         in_specs=specs,
         out_specs=jax.tree.map(lambda _: VM, outs),
+        scratch_shapes=scratch,
+        compiler_params=pltpu.CompilerParams(vmem_limit_bytes=16 << 20),
         name=name,
     )
 
@@ -35,7 +37,7 @@
             out_ref[s, z] = x_ref[s, pl.ds(z, count, stride=2), :].astype(bf16)
 
 
-def project(field, plane_ref, cos, sin):
+def project(field, plane_ref, columns, spheres):
     sum_re = sum_im = None
     lead = (((0,), (0,)), ((), ()))
     for s in range(len(field)):
@@ -45,7 +47,7 @@
         n = both.shape[1] // 2
         part_re = with_re[:, :n] - with_im[:, n:]
         part_im = with_re[:, n:] + with_im[:, :n]
-        c, d = cos[:, s : s + 1], sin[:, s : s + 1]
+        c, d = columns[:, s : s + 1], columns[:, spheres + s : spheres + s + 1]
         turn_re = c * part_re + d * part_im
         turn_im = c * part_im - d * part_re
         sum_re = turn_re if sum_re is None else sum_re + turn_re
@@ -64,22 +66,40 @@
         keep_ref[:, at] = jnp.where(odd, high, low)
 
 
-def first_sums_body(x_ref, plane_ref, wave_ref, pos_ref, send_ref, keep_ref, cos_ref, sin_ref):
-    spheres = x_ref.shape[0]
-    lane = lax.broadcasted_iota(jnp.int32, (1, spheres), 1)
+def first_sums_body(
+    x_ref, plane_ref, wave_ref, pos_ref, weight_ref, mie_ref,
+    send_ref, keep_ref, column_ref, part_ref, held,
+):
+    spheres, _, count, _ = x_ref.shape
+    waves = wave_ref.shape[1]
+    b = lax.axis_index("blk")
+    for a in range(2):
+        part = plane_ref[a, 0:count, :]
+        for p in range(1, plane_ref.shape[1] // count):
+            part = jnp.where(b == p, plane_ref[a, p * count : (p + 1) * count, :], part)
+        part_ref[a] = part
+    row = lax.broadcasted_iota(jnp.int32, (spheres, 1), 0)
     turns = None
     for d in range(3):
-        row = jnp.zeros((1, spheres), f32)
+        place = jnp.zeros((spheres, 1), f32)
         for s in range(spheres):
-            row = jnp.where(lane == s, pos_ref[s, d], row)
-        term = wave_ref[:, d : d + 1].astype(f32) * row
+            place = jnp.where(row == s, pos_ref[s, d], place)
+        term = wave_ref[d : d + 1, :].astype(f32) * place
         turns = term if turns is None else turns + term
     angles = two_pi * (turns - jnp.floor(turns + 0.5))
     cos, sin = jnp.cos(angles), jnp.sin(angles)
-    cos_ref[...] = cos
-    sin_ref[...] = sin
+    weight = weight_ref[...]
+    held[...] = jnp.zeros_like(held)
+    for i, value in enumerate((cos, sin, weight * cos, weight * sin)):
+        held[i * spheres : (i + 1) * spheres, :] = value
+    for s in range(spheres):
+        for z in range(2):
+            at = 4 * spheres + 2 * s + z
+            held[at : at + 1, 0:count] = mie_ref[s, z : z + 1, :]
+    columns = held[...].T
+    column_ref[...] = columns
     field = [[x_ref[s, 0], x_ref[s, 1]] for s in range(spheres)]
-    split_halves(*project(field, plane_ref, cos, sin), send_ref, keep_ref)
+    split_halves(*project(field, part_ref, columns, spheres), send_ref, keep_ref)
 
 
 def gather_body(shift_ref, member_ref, *refs):
@@ -108,12 +128,13 @@
             out_ref[i, k] = held[slot * spheres + member_ref[i, k]]
 
 
-def far_field(total, plane_ref, cos, sin, weight, spheres):
+def far_field(total, plane_ref, columns, spheres):
     total_re, total_im = total
     n = total_re.shape[1]
     fields = []
     for s in range(spheres):
-        c, d = weight * cos[:, s : s + 1], weight * sin[:, s : s + 1]
+        at = 2 * spheres + s
+        c, d = columns[:, at : at + 1], columns[:, at + spheres : at + spheres + 1]
         turned = jnp.concatenate(
             [c * total_re - d * total_im, c * total_im + d * total_re], axis=1
         ).astype(bf16)
@@ -138,24 +159,27 @@
     return out
 
 
-def image_fields(near_ref, mine_ref, other_ref, cos, sin, plane_ref, weight_ref, mie_ref):
-    spheres = near_ref.shape[0]
-    far = far_field(join_halves(mine_ref, other_ref), plane_ref, cos, sin, weight_ref[...], spheres)
+def image_fields(near_ref, mine_ref, other_ref, column_ref, plane_ref):
+    spheres, pairs, _, _, count, _ = near_ref.shape
+    far = far_field(join_halves(mine_ref, other_ref), plane_ref, column_ref[...], spheres)
     out = []
     for s in range(spheres):
-        sum_re = near_ref[s, 0, 0] - near_ref[s, 1, 1] + far[s][0]
-        sum_im = near_ref[s, 0, 1] + near_ref[s, 1, 0] + far[s][1]
-        m_re, m_im = mie_ref[:, 2 * s : 2 * s + 1], mie_ref[:, 2 * s + 1 : 2 * s + 2]
+        sum_re, sum_im = far[s]
+        for k in range(pairs):
+            sum_re = sum_re + (near_ref[s, k, 0, 0] - near_ref[s, k, 1, 1])
+            sum_im = sum_im + (near_ref[s, k, 0, 1] + near_ref[s, k, 1, 0])
+        at = 4 * spheres + 2 * s
+        m_re = column_ref[0:count, at : at + 1]
+        m_im = column_ref[0:count, at + 1 : at + 2]
         out.append((m_re * sum_re - m_im * sum_im, m_re * sum_im + m_im * sum_re))
     return out
 
 
 def first_image_body(
-    near_ref, mine_ref, other_ref, cos_ref, sin_ref, plane_ref, weight_ref, mie_ref,
+    near_ref, mine_ref, other_ref, column_ref, plane_ref,
     image_ref, round_ref, send_ref, keep_ref,
 ):
-    cos, sin = cos_ref[...], sin_ref[...]
-    images = image_fields(near_ref, mine_ref, other_ref, cos, sin, plane_ref, weight_ref, mie_ref)
+    images = image_fields(near_ref, mine_ref, other_ref, column_ref, plane_ref)
     field = []
     for s, (re, im) in enumerate(images):
         image_ref[s, 0] = re
@@ -163,16 +187,14 @@
         field.append([re.astype(bf16), im.astype(bf16)])
         round_ref[s, 0] = field[s][0]
         round_ref[s, 1] = field[s][1]
-    split_halves(*project(field, plane_ref, cos, sin), send_ref, keep_ref)
+    sums = project(field, plane_ref, column_ref[...], len(images))
+    split_halves(*sums, send_ref, keep_ref)
 
 
 def second_image_body(
-    near_ref, mine_ref, other_ref, cos_ref, sin_ref, plane_ref, weight_ref, mie_ref, x_ref, g_ref,
-    image_ref, gram_ref,
+    near_ref, mine_ref, other_ref, column_ref, plane_ref, x_ref, g_ref, image_ref, gram_ref,
 ):
-    images = image_fields(
-        near_ref, mine_ref, other_ref, cos_ref[...], sin_ref[...], plane_ref, weight_ref, mie_ref
-    )
+    images = image_fields(near_ref, mine_ref, other_ref, column_ref, plane_ref)
     count = g_ref.shape[2]
     sums = None
     for s, (re, im) in enumerate(images):
@@ -314,48 +336,46 @@
     waves = plane_coef.shape[0]
     entries = spheres * lax.axis_size("slab") * count * blocks
     x = incident.transpose(0, 2, 1, 3).reshape(spheres, 2 * count, n)
-    plane = lax.dynamic_slice_in_dim(
-        plane_coef.transpose(1, 2, 0), lax.axis_index("blk") * count, count, 1
-    )
-    weight = ewald_weight.reshape(waves, 1)
-    mie = mie_coef.transpose(2, 0, 1).reshape(count, spheres * 2)
+    plane = plane_coef.transpose(1, 2, 0)
 
     field = shape((spheres, 2, count, n))
     field_half = shape((spheres, 2, count, n), bf16)
     sums = shape((waves // 2, 2 * n))
     sums_half = shape((waves // 2, 2 * n), bf16)
-    phase = shape((waves, spheres))
     sources = shape((spheres, pairs, 2, count * blocks, n), bf16)
+    held_rows = -(-6 * spheres // 8) * 8
+    column = shape((waves, held_rows))
+    part = shape((2, count, waves), bf16)
 
     def near_products(own):
         pieces = fetch_pieces(own)
         slots = pieces[0].shape[0]
-        gathered = pl.pallas_call(
-            gather_body,
-            out_shape=sources,
-            in_specs=[SM, SM] + [VM] * blocks,
-            out_specs=VM,
-            scratch_shapes=[pltpu.VMEM((slots * spheres, 2, count * blocks, n), bf16)],
-            name="gather",
-        )(pair_shift, pair_member, *pieces)
+        held = pltpu.VMEM((slots * spheres, 2, count * blocks, n), bf16)
+        gathered = call(gather_body, sources, [SM, SM] + [VM] * blocks, "gather", [held])(
+            pair_shift, pair_member, *pieces
+        )
         return jnp.einsum(
-            "ikarc,ikzcn->iazrn", translation, gathered, preferred_element_type=f32
+            "ikarc,ikzcn->ikazrn", translation, gathered, preferred_element_type=f32
         )
 
     rounded = call(round_body, field_half, [VM], "round")(x)
-    send, keep, cos, sin = call(
-        first_sums_body, (sums_half, sums, phase, phase), [VM, VM, VM, SM], "first_sums"
-    )(rounded, plane, wave_index, positions)
+    send, keep, columns, plane = call(
+        first_sums_body,
+        (sums_half, sums, column, part),
+        [VM, VM, VM, SM, VM, VM],
+        "first_sums",
+        [pltpu.VMEM((held_rows, waves), f32)],
+    )(rounded, plane, wave_index.T, positions, ewald_weight.reshape(1, waves), mie_coef)
     mine, other = total_sums(send, keep)
     near = near_products(rounded)
     image, image_rounded, send, keep = call(
-        first_image_body, (field, field_half, sums_half, sums), [VM] * 8, "first_image"
-    )(near, mine, other, cos, sin, plane, weight, mie)
+        first_image_body, (field, field_half, sums_half, sums), [VM] * 5, "first_image"
+    )(near, mine, other, columns, plane)
 
     mine, other = total_sums(send, keep)
     near = near_products(image_rounded)
-    image_two, gram = call(second_image_body, (field, shape((16, n))), [VM] * 10, "second_image")(
-        near, mine, other, cos, sin, plane, weight, mie, x, image
+    image_two, gram = call(second_image_body, (field, shape((16, n))), [VM] * 7, "second_image")(
+        near, mine, other, columns, plane, x, image
     )
     gram = total_gram(gram)
     flat = shape((spheres, 2 * count, n))

time: 106 us -> 77.6 us (0.73)
  Pallas kernels: 17.9 us -> 5.42 us
  other arithmetic: 8.32 us -> 0.32 us
  matrix products: 6.79 us -> 1.82 us
  starting transfers between devices: 23.4 us -> 28.3 us
  waiting for transfers between devices: 39.7 us -> 35.9 us
  local copies, waits for them, and re-layouts: 8.34 us -> 4.79 us
    pallas_call x5, Pallas kernels: 14.3 us -> 4.54 us  [the longest x2 2.17 us: near_products(): call(gather_body, sources, [SM, SM] + [VM] * blocks, 'gather', [held])]
    dot_general x2, matrix products: 6.79 us -> 1.82 us  [near_products(): jnp.einsum('ikarc,ikzcn->ikazrn', translation, gathered, preferred_elemen...]
    ppermute x25, starting transfers between devices: 17.4 us -> 21.6 us  [trade(): lax.ppermute(value, axis, [(i, i ^ bit) for i in range(lax.axis_size(axis...]
    ppermute x25, waiting for transfers between devices: 35.5 us -> 31.5 us  [trade(): lax.ppermute(value, axis, [(i, i ^ bit) for i in range(lax.axis_size(axis...]
    convert_element_type x8, other arithmetic: 3.79 us -> 0.16 us  [total_sums(): keep = keep + trade(keep.astype(bf16), axis, bit).astype(f32)]
    another operation x2, other arithmetic: 1.84 us -> 0.07 us  [fetch_pieces(): mine = jnp.stack([own, trade(own, 'slab', 1), trade_odd(own)])]
    pallas_call x1, Pallas kernels: 1.7 us -> 0.01 us  [per_device(): rounded = call(round_body, field_half, [VM], 'round')(x)]
    dynamic_slice x1 -> x0, local copies, waits for them, and re-layouts: 1.55 us -> none  [per_device(): lax.dynamic_slice_in_dim(plane_coef.transpose(1, 2, 0), lax.axis_index('b...]
  transfers between devices with their start and end apart: 27 -> 27, of which waited for: 18 -> 20; matrix products, arithmetic and copies ran while one was open for 11% -> 3% of each run, Pallas kernels for 6% -> 3%
where the time goes in v2:
time: 77.6 us; the launch traced here: 77.3 us
  waiting for transfers between devices  35.9 us (46%)
  starting transfers between devices  28.3 us (36%)
  Pallas kernels  5.42 us (7%)
  local copies, waits for them, and re-layouts  4.79 us (6%)
  matrix products  1.82 us (2%)
  between operations  0.84 us (1%)
    ppermute x25, waiting for transfers between devices, trade(): lax.ppermute(value, axis, [(i, i ^ bit) for i in range(lax.axis_size(axis...  31.5 us
    ppermute x25, starting transfers between devices, trade(): lax.ppermute(value, axis, [(i, i ^ bit) for i in range(lax.axis_size(axis...  21.6 us
    ppermute x2, starting transfers between devices, trade_odd(): return lax.ppermute(value, 'slab', pairs)  6.65 us
    unnamed x20, local copies, waits for them, and re-layouts  4.79 us
    ppermute x2, waiting for transfers between devices, trade_odd(): return lax.ppermute(value, 'slab', pairs)  4.34 us
    pallas_call x2, Pallas kernels, near_products(): call(gather_body, sources, [SM, SM] + [VM] * blocks, 'gather', [held])  2.17 us
    dot_general x2, matrix products, near_products(): jnp.einsum('ikarc,ikzcn->ikazrn', translation, gathered, preferred_elemen...  1.82 us
  transfers between devices with their start and end apart: 27, of which 20 were waited for; matrix products, arithmetic and copies ran while one was open for 3% of the time, Pallas kernels for 3%

profile of v2, /device:TPU:0, one launch (start us, length us, event | category | flops | bytes accessed | tf_op | source)
XLA Modules:
  0.0 77.3 jit_solution(5299239455082727567)
XLA Ops:
  0.6 0.0 copy-start
  0.7 0.0 copy-start.1
  0.7 1.1 %copy-done.1 = f32[2,2,84,128]{3,1,2,0:T(2,128)S(1)} copy-done((f32[2,2,84,128]{3,1,2,0:T(2,128)S(1)}, f32[2,2,84,128]{3,1,2,0:T(2,128)}, u32[]{:S(2)}) %copy-start.1) | copy-done | bytes 172056
  1.7 0.0 copy-start.3
  1.8 1.0 %copy-done.3 = bf16[256,2,336]{0,2,1:T(8,128)(2,1)S(1)} copy-done((bf16[256,2,336]{0,2,1:T(8,128)(2,1)S(1)}, bf16[256,2,336]{0,2,1:T(8,128)(2,1)}, u32[]{:S(2)}) %copy-start.3) | copy-done | bytes 344088
  2.7 0.7 copy-done.4
  3.4 0.7 copy-done.7
  4.1 0.7 copy-done.8
  4.8 0.7 copy-done.9
  5.5 1.0 %first_sums.1 = (bf16[128,256]{1,0:T(8,128)(2,1)S(1)}, f32[128,256]{1,0:T(8,128)S(1)}, f32[256,16]{1,0:T(8,128)S(1)}, bf16[2,84,256]{2,1,0:T(8,128)(2,1)S(1)}) custom-call(bf16[2,2,84,128]{3,2,1,0:T(8,128)(2,1)S(1)} %round.1.x_ref, bf16[2,336,256]{2,1,0:T(8,128)(2,1)S(1)} %bitcast.44, s32[3,256]{1,0:T(4,128)S(1)} %bitcast.46, f32[2,3]{1,0:T(2,128)S(1)} %copy-done.8, ...), custom_call_target="tpu_custom_call" | custom-call | tf_op jit(solution)/shard_map/first_sums/pallas_call | solution.py:362
  6.5 0.6 collective-permute-start.5
  7.0 0.9 %collective-permute-done.5 = bf16[128,256]{1,0:T(8,128)(2,1)S(1)} collective-permute-done((bf16[128,256]{1,0:T(8,128)(2,1)S(1)}, bf16[128,256]{1,0:T(8,128)(2,1)S(1)}, u32[]{:S(2)}, u32[]{:S(2)}) %collective-permute-start.5) | collective-permute-done | bytes 65568 | tf_op jit(solution)/shard_map/ppermute | solution.py:285
  8.0 2.9 %collective-permute-start.6 = (bf16[128,256]{1,0:T(8,128)(2,1)S(1)}, bf16[128,256]{1,0:T(8,128)(2,1)S(1)}, u32[]{:S(2)}, u32[]{:S(2)}) collective-permute-start(bf16[128,256]{1,0:T(8,128)(2,1)S(1)} %fusion.16), channel_id=1, source_target_pairs={{0,2},{1,3},{2,0},{3,1},{4,6},{5,7},{6,4},{7,5},{8,10},{9,11},{10,... | collective-permute-start | bytes 196616 | tf_op jit(solution)/shard_map/ppermute | solution.py:285
  10.9 2.4 %collective-permute-done.6 = bf16[128,256]{1,0:T(8,128)(2,1)S(1)} collective-permute-done((bf16[128,256]{1,0:T(8,128)(2,1)S(1)}, bf16[128,256]{1,0:T(8,128)(2,1)S(1)}, u32[]{:S(2)}, u32[]{:S(2)}) %collective-permute-start.6) | collective-permute-done | bytes 65568 | tf_op jit(solution)/shard_map/ppermute | solution.py:285
  13.3 1.9 %collective-permute-start.7 = (bf16[128,256]{1,0:T(8,128)(2,1)S(1)}, bf16[128,256]{1,0:T(8,128)(2,1)S(1)}, u32[]{:S(2)}, u32[]{:S(2)}) collective-permute-start(bf16[128,256]{1,0:T(8,128)(2,1)S(1)} %get-tuple-element.35), channel_id=1, source_target_pairs={{0,4},{4,0},{8,12},{12,8},{16,20},{20,16},{24,28},{28,24},{1,5},{5... | collective-permute-start | bytes 196616 | tf_op jit(solution)/shard_map/ppermute | solution.py:285
  15.2 3.6 %collective-permute-start.1 = (bf16[2,2,84,128]{3,2,1,0:T(8,128)(2,1)S(1)}, bf16[2,2,84,128]{3,2,1,0:T(8,128)(2,1)S(1)}, u32[]{:S(2)}, u32[]{:S(2)}) collective-permute-start(bf16[2,2,84,128]{3,2,1,0:T(8,128)(2,1)S(1)} %round.1.x_ref), channel_id=1, source_target_pairs={{0,28},{4,8},{8,4},{12,16},{16,12},{20,24},{24,20},{28,0},{1,29},{... | collective-permute-start | bytes 258056 | tf_op jit(solution)/shard_map/ppermute | solution.py:293
  18.8 0.0 collective-permute-start
  18.8 0.0 collective-permute-done.7
  18.8 2.3 %collective-permute-start.8 = (bf16[128,256]{1,0:T(8,128)(2,1)S(1)}, bf16[128,256]{1,0:T(8,128)(2,1)S(1)}, u32[]{:S(2)}, u32[]{:S(2)}) collective-permute-start(bf16[128,256]{1,0:T(8,128)(2,1)S(1)} %fusion.17), channel_id=1, source_target_pairs={{0,8},{4,12},{8,0},{12,4},{16,24},{20,28},{24,16},{28,20},{1,9},{5... | collective-permute-start | bytes 196616 | tf_op jit(solution)/shard_map/ppermute | solution.py:285
  21.1 2.2 %collective-permute-done.1 = bf16[2,2,84,128]{3,2,1,0:T(8,128)(2,1)S(1)} collective-permute-done((bf16[2,2,84,128]{3,2,1,0:T(8,128)(2,1)S(1)}, bf16[2,2,84,128]{3,2,1,0:T(8,128)(2,1)S(1)}, u32[]{:S(2)}, u32[]{:S(2)}) %collective-permute-start.1) | collective-permute-done | bytes 86048 | tf_op jit(solution)/shard_map/ppermute | solution.py:293
  23.2 0.6 collective-permute-done
  23.9 1.6 %collective-permute-start.3 = (bf16[3,2,2,84,128]{4,3,2,1,0:T(8,128)(2,1)S(1)}, bf16[3,2,2,84,128]{4,3,2,1,0:T(8,128)(2,1)S(1)}, u32[]{:S(2)}, u32[]{:S(2)}) collective-permute-start(bf16[3,2,2,84,128]{4,3,2,1,0:T(8,128)(2,1)S(1)} %pad_maximum_fusion.refs_0_), channel_id=1, source_target_pairs={{0,2},{1,3},{2,0},{3,1},{4,6},{5,7},{6,4},{7,5},{8,10},{9,11},{10,... | collective-permute-start | bytes 774152 | tf_op jit(solution)/shard_map/ppermute | solution.py:285
  25.5 0.0 collective-permute-done.8
  25.5 0.9 %collective-permute-start.9 = (bf16[128,256]{1,0:T(8,128)(2,1)S(1)}, bf16[128,256]{1,0:T(8,128)(2,1)S(1)}, u32[]{:S(2)}, u32[]{:S(2)}) collective-permute-start(bf16[128,256]{1,0:T(8,128)(2,1)S(1)} %fusion.20), channel_id=1, source_target_pairs={{0,16},{4,20},{8,24},{12,28},{16,0},{20,4},{24,8},{28,12},{1,17},{... | collective-permute-start | bytes 196616 | tf_op jit(solution)/shard_map/ppermute | solution.py:285
  26.4 0.0 collective-permute-start.2
  26.4 4.0 %collective-permute-done.3.refs_2_ = bf16[3,2,2,84,128]{4,3,2,1,0:T(8,128)(2,1)S(1)} collective-permute-done((bf16[3,2,2,84,128]{4,3,2,1,0:T(8,128)(2,1)S(1)}, bf16[3,2,2,84,128]{4,3,2,1,0:T(8,128)(2,1)S(1)}, u32[]{:S(2)}, u32[]{:S(2)}) %collective-permute-start.3) | collective-permute-done | bytes 258080 | tf_op jit(solution)/shard_map/ppermute | solution.py:285
  30.4 0.3 collective-permute-done.9
  30.8 0.3 collective-permute-start.10
  31.0 0.9 %collective-permute-done.4.refs_3_ = bf16[3,2,2,84,128]{4,3,2,1,0:T(8,128)(2,1)S(1)} collective-permute-done((bf16[3,2,2,84,128]{4,3,2,1,0:T(8,128)(2,1)S(1)}, bf16[3,2,2,84,128]{4,3,2,1,0:T(8,128)(2,1)S(1)}, u32[]{:S(2)}, u32[]{:S(2)}) %collective-permute-start.4) | collective-permute-done | bytes 258080 | tf_op jit(solution)/shard_map/ppermute | solution.py:285
  32.0 1.1 %gather.2 = bf16[2,8,2,336,128]{4,3,2,1,0:T(8,128)(2,1)S(1)} custom-call(s32[2,8]{1,0:T(2,128)S(1)} %copy-done.5, s32[2,8]{1,0:T(2,128)S(1)} %copy-done.6, bf16[3,2,2,84,128]{4,3,2,1,0:T(8,128)(2,1)S(1)} %pad_maximum_fusion.refs_0_, bf16[3,2,2,84,128]{4,3,2,1,0:T(8,128)(2,1)S(1)} %collective-permute-done.2.refs_1_, ...), custom_call_target="tpu_custom_call" | custom-call | tf_op jit(solution)/shard_map/gather/pallas_call | solution.py:354
  33.1 0.9 %fusion.6.near_ref = f32[2,8,2,2,84,128]{5,4,3,2,1,0:T(8,128)S(1)} fusion(bf16[2,8,2,84,336,1]{4,2,3,1,0,5:T(2,128)(2,1)S(1)} %bitcast.38, bf16[2,8,2,336,128]{4,3,2,1,0:T(8,128)(2,1)S(1)} %gather.2), kind=kOutput, calls=%fused_computation.6 | convolution fusion | flops 462422016 | bytes 7311360 | tf_op jit(solution)/shard_map/ikarc,ikzcn->ikazrn/dot_general | solution.py:357
  34.0 0.8 %first_image.1 = (f32[2,2,84,128]{3,2,1,0:T(8,128)S(1)}, bf16[2,2,84,128]{3,2,1,0:T(8,128)(2,1)S(1)}, bf16[128,256]{1,0:T(8,128)(2,1)S(1)}, f32[128,256]{1,0:T(8,128)S(1)}) custom-call(f32[2,8,2,2,84,128]{5,4,3,2,1,0:T(8,128)S(1)} %fusion.6.near_ref, f32[128,256]{1,0:T(8,128)S(1)} %get-tuple-element.34.mine_ref, ...), custom_call_target="tpu_custom_call" | custom-call | tf_op jit(solution)/shard_map/first_image/pallas_call | solution.py:371
  34.8 0.2 collective-permute-start.16
  35.0 1.1 %collective-permute-done.16 = bf16[128,256]{1,0:T(8,128)(2,1)S(1)} collective-permute-done((bf16[128,256]{1,0:T(8,128)(2,1)S(1)}, bf16[128,256]{1,0:T(8,128)(2,1)S(1)}, u32[]{:S(2)}, u32[]{:S(2)}) %collective-permute-start.16) | collective-permute-done | bytes 65568 | tf_op jit(solution)/shard_map/ppermute | solution.py:285
  36.1 1.6 %collective-permute-start.17 = (bf16[128,256]{1,0:T(8,128)(2,1)S(1)}, bf16[128,256]{1,0:T(8,128)(2,1)S(1)}, u32[]{:S(2)}, u32[]{:S(2)}) collective-permute-start(bf16[128,256]{1,0:T(8,128)(2,1)S(1)} %fusion.18), channel_id=1, source_target_pairs={{0,2},{1,3},{2,0},{3,1},{4,6},{5,7},{6,4},{7,5},{8,10},{9,11},{10,... | collective-permute-start | bytes 196616 | tf_op jit(solution)/shard_map/ppermute | solution.py:285
  37.7 2.7 %collective-permute-done.17 = bf16[128,256]{1,0:T(8,128)(2,1)S(1)} collective-permute-done((bf16[128,256]{1,0:T(8,128)(2,1)S(1)}, bf16[128,256]{1,0:T(8,128)(2,1)S(1)}, u32[]{:S(2)}, u32[]{:S(2)}) %collective-permute-start.17) | collective-permute-done | bytes 65568 | tf_op jit(solution)/shard_map/ppermute | solution.py:285
  40.5 0.1 collective-permute-start.18
  40.6 3.1 %collective-permute-start.12 = (bf16[2,2,84,128]{3,2,1,0:T(8,128)(2,1)S(1)}, bf16[2,2,84,128]{3,2,1,0:T(8,128)(2,1)S(1)}, u32[]{:S(2)}, u32[]{:S(2)}) collective-permute-start(bf16[2,2,84,128]{3,2,1,0:T(8,128)(2,1)S(1)} %get-tuple-element.20), channel_id=1, source_target_pairs={{0,28},{4,8},{8,4},{12,16},{16,12},{20,24},{24,20},{28,0},{1,29},{... | collective-permute-start | bytes 258056 | tf_op jit(solution)/shard_map/ppermute | solution.py:293
  43.6 1.2 %collective-permute-done.18 = bf16[128,256]{1,0:T(8,128)(2,1)S(1)} collective-permute-done((bf16[128,256]{1,0:T(8,128)(2,1)S(1)}, bf16[128,256]{1,0:T(8,128)(2,1)S(1)}, u32[]{:S(2)}, u32[]{:S(2)}) %collective-permute-start.18) | collective-permute-done | bytes 65568 | tf_op jit(solution)/shard_map/ppermute | solution.py:285
  44.8 1.1 %collective-permute-start.19 = (bf16[128,256]{1,0:T(8,128)(2,1)S(1)}, bf16[128,256]{1,0:T(8,128)(2,1)S(1)}, u32[]{:S(2)}, u32[]{:S(2)}) collective-permute-start(bf16[128,256]{1,0:T(8,128)(2,1)S(1)} %fusion.19), channel_id=1, source_target_pairs={{0,8},{4,12},{8,0},{12,4},{16,24},{20,28},{24,16},{28,20},{1,9},{5... | collective-permute-start | bytes 196616 | tf_op jit(solution)/shard_map/ppermute | solution.py:285
  46.0 2.2 %collective-permute-done.12 = bf16[2,2,84,128]{3,2,1,0:T(8,128)(2,1)S(1)} collective-permute-done((bf16[2,2,84,128]{3,2,1,0:T(8,128)(2,1)S(1)}, bf16[2,2,84,128]{3,2,1,0:T(8,128)(2,1)S(1)}, u32[]{:S(2)}, u32[]{:S(2)}) %collective-permute-start.12) | collective-permute-done | bytes 86048 | tf_op jit(solution)/shard_map/ppermute | solution.py:293
  48.1 0.8 %collective-permute-done.11 = bf16[2,2,84,128]{3,2,1,0:T(8,128)(2,1)S(1)} collective-permute-done((bf16[2,2,84,128]{3,2,1,0:T(8,128)(2,1)S(1)}, bf16[2,2,84,128]{3,2,1,0:T(8,128)(2,1)S(1)}, u32[]{:S(2)}, u32[]{:S(2)}) %collective-permute-start.11) | collective-permute-done | bytes 86048 | tf_op jit(solution)/shard_map/ppermute | solution.py:285
  49.0 1.6 %collective-permute-start.14 = (bf16[3,2,2,84,128]{4,3,2,1,0:T(8,128)(2,1)S(1)}, bf16[3,2,2,84,128]{4,3,2,1,0:T(8,128)(2,1)S(1)}, u32[]{:S(2)}, u32[]{:S(2)}) collective-permute-start(bf16[3,2,2,84,128]{4,3,2,1,0:T(8,128)(2,1)S(1)} %pad_maximum_fusion.1.refs_0_), channel_id=1, source_target_pairs={{0,2},{1,3},{2,0},{3,1},{4,6},{5,7},{6,4},{7,5},{8,10},{9,11},{10,... | collective-permute-start | bytes 774152 | tf_op jit(solution)/shard_map/ppermute | solution.py:285
  50.6 0.0 collective-permute-done.19
  50.6 2.6 %collective-permute-start.20 = (bf16[128,256]{1,0:T(8,128)(2,1)S(1)}, bf16[128,256]{1,0:T(8,128)(2,1)S(1)}, u32[]{:S(2)}, u32[]{:S(2)}) collective-permute-start(bf16[128,256]{1,0:T(8,128)(2,1)S(1)} %fusion.21), channel_id=1, source_target_pairs={{0,16},{4,20},{8,24},{12,28},{16,0},{20,4},{24,8},{28,12},{1,17},{... | collective-permute-start | bytes 196616 | tf_op jit(solution)/shard_map/ppermute | solution.py:285
  53.2 2.3 %collective-permute-done.14.refs_2_ = bf16[3,2,2,84,128]{4,3,2,1,0:T(8,128)(2,1)S(1)} collective-permute-done((bf16[3,2,2,84,128]{4,3,2,1,0:T(8,128)(2,1)S(1)}, bf16[3,2,2,84,128]{4,3,2,1,0:T(8,128)(2,1)S(1)}, u32[]{:S(2)}, u32[]{:S(2)}) %collective-permute-start.14) | collective-permute-done | bytes 258080 | tf_op jit(solution)/shard_map/ppermute | solution.py:285
  55.5 0.3 collective-permute-done.20
  55.9 0.3 collective-permute-start.21
  56.2 0.9 %collective-permute-done.15.refs_3_ = bf16[3,2,2,84,128]{4,3,2,1,0:T(8,128)(2,1)S(1)} collective-permute-done((bf16[3,2,2,84,128]{4,3,2,1,0:T(8,128)(2,1)S(1)}, bf16[3,2,2,84,128]{4,3,2,1,0:T(8,128)(2,1)S(1)}, u32[]{:S(2)}, u32[]{:S(2)}) %collective-permute-start.15) | collective-permute-done | bytes 258080 | tf_op jit(solution)/shard_map/ppermute | solution.py:285
  57.1 1.1 %gather.3 = bf16[2,8,2,336,128]{4,3,2,1,0:T(8,128)(2,1)S(1)} custom-call(s32[2,8]{1,0:T(2,128)S(1)} %copy-done.5, s32[2,8]{1,0:T(2,128)S(1)} %copy-done.6, bf16[3,2,2,84,128]{4,3,2,1,0:T(8,128)(2,1)S(1)} %pad_maximum_fusion.1.refs_0_, bf16[3,2,2,84,128]{4,3,2,1,0:T(8,128)(2,1)S(1)} %collective-permute-done.13.refs_1_, ...), custom_call_target="tpu_custom_call" | custom-call | tf_op jit(solution)/shard_map/gather/pallas_call | solution.py:354
  58.2 0.0 copy-start.2
  58.2 0.9 %fusion.11.near_ref = f32[2,8,2,2,84,128]{5,4,3,2,1,0:T(8,128)S(1)} fusion(bf16[2,8,2,84,336,1]{4,2,3,1,0,5:T(2,128)(2,1)S(1)} %bitcast.39, bf16[2,8,2,336,128]{4,3,2,1,0:T(8,128)(2,1)S(1)} %gather.3), kind=kOutput, calls=%fused_computation.7 | convolution fusion | flops 462422016 | bytes 7311360 | tf_op jit(solution)/shard_map/ikarc,ikzcn->ikazrn/dot_general | solution.py:357
  59.1 0.6 second_image.1
  59.7 0.2 collective-permute-start.22
  59.9 1.0 %collective-permute-done.22 = f32[16,128]{1,0:T(8,128)S(1)} collective-permute-done((f32[16,128]{1,0:T(8,128)S(1)}, f32[16,128]{1,0:T(8,128)S(1)}, u32[]{:S(2)}, u32[]{:S(2)}) %collective-permute-start.22) | collective-permute-done | bytes 8224 | tf_op jit(solution)/shard_map/ppermute | solution.py:285
  60.9 1.5 %collective-permute-start.23 = (f32[16,128]{1,0:T(8,128)S(1)}, f32[16,128]{1,0:T(8,128)S(1)}, u32[]{:S(2)}, u32[]{:S(2)}) collective-permute-start(f32[16,128]{1,0:T(8,128)S(1)} %add.55), channel_id=1, source_target_pairs={{0,2},{1,3},{2,0},{3,1},{4,6},{5,7},{6,4},{7,5},{8,10},{9,11},{10,... | collective-permute-start | bytes 24584 | tf_op jit(solution)/shard_map/ppermute | solution.py:285
  62.5 2.1 %collective-permute-done.23 = f32[16,128]{1,0:T(8,128)S(1)} collective-permute-done((f32[16,128]{1,0:T(8,128)S(1)}, f32[16,128]{1,0:T(8,128)S(1)}, u32[]{:S(2)}, u32[]{:S(2)}) %collective-permute-start.23) | collective-permute-done | bytes 8224 | tf_op jit(solution)/shard_map/ppermute | solution.py:285
  64.6 0.1 collective-permute-start.24
  64.7 3.6 %collective-permute-done.24 = f32[16,128]{1,0:T(8,128)S(1)} collective-permute-done((f32[16,128]{1,0:T(8,128)S(1)}, f32[16,128]{1,0:T(8,128)S(1)}, u32[]{:S(2)}, u32[]{:S(2)}) %collective-permute-start.24) | collective-permute-done | bytes 8224 | tf_op jit(solution)/shard_map/ppermute | solution.py:285
  68.3 0.4 collective-permute-start.25
  68.6 3.3 %collective-permute-done.25 = f32[16,128]{1,0:T(8,128)S(1)} collective-permute-done((f32[16,128]{1,0:T(8,128)S(1)}, f32[16,128]{1,0:T(8,128)S(1)}, u32[]{:S(2)}, u32[]{:S(2)}) %collective-permute-start.25) | collective-permute-done | bytes 8224 | tf_op jit(solution)/shard_map/ppermute | solution.py:285
  71.9 1.6 %collective-permute-start.26 = (f32[16,128]{1,0:T(8,128)S(1)}, f32[16,128]{1,0:T(8,128)S(1)}, u32[]{:S(2)}, u32[]{:S(2)}) collective-permute-start(f32[16,128]{1,0:T(8,128)S(1)} %add.58), channel_id=1, source_target_pairs={{0,16},{4,20},{8,24},{12,28},{16,0},{20,4},{24,8},{28,12},{1,17},{... | collective-permute-start | bytes 24584 | tf_op jit(solution)/shard_map/ppermute | solution.py:285
  73.5 2.9 %collective-permute-done.26 = f32[16,128]{1,0:T(8,128)S(1)} collective-permute-done((f32[16,128]{1,0:T(8,128)S(1)}, f32[16,128]{1,0:T(8,128)S(1)}, u32[]{:S(2)}, u32[]{:S(2)}) %collective-permute-start.26) | collective-permute-done | bytes 8224 | tf_op jit(solution)/shard_map/ppermute | solution.py:285
  76.5 0.9 %finish.1 = (f32[2,168,128]{2,1,0:T(8,128)}, f32[2,168,128]{2,1,0:T(8,128)}, f32[9,128]{1,0:T(8,128)}) custom-call(f32[16,128]{1,0:T(8,128)S(1)} %add.59.refs_0_, f32[2,168,128]{2,1,0:T(8,128)S(1)} %bitcast.42, f32[2,2,84,128]{3,2,1,0:T(8,128)S(1)} %get-tuple-element.23.g_ref.refs_2_, f32[2,2,84,128]{3,2,1,0:T(8,128)S(1)} %get-tuple-element.25.refs_3_), custom_call_target="tpu_custom_call" | custom-call | tf_op jit(solution)/shard_map/finish/pallas_call | solution.py:382
  (36 shorter events, 0.4 us)
Async XLA Ops:
  0.6 32.4 %copy-start = (bf16[2,8,2,84,336]{4,2,3,1,0:T(2,128)(2,1)S(1)}, bf16[2,8,2,84,336]{4,2,3,1,0:T(2,128)(2,1)}, u32[]{:S(2)}) copy-start(bf16[2,8,2,84,336]{4,2,3,1,0:T(2,128)(2,1)} %param.11) | copy-start | bytes 5419012
  0.6 31.3 %copy-start.5 = (s32[2,8]{1,0:T(2,128)S(1)}, s32[2,8]{1,0:T(2,128)}, u32[]{:S(2)}) copy-start(s32[2,8]{1,0:T(2,128)} %shift_ref.3) | copy-start | bytes 196
  0.7 1.1 %copy-start.1 = (f32[2,2,84,128]{3,1,2,0:T(2,128)S(1)}, f32[2,2,84,128]{3,1,2,0:T(2,128)}, u32[]{:S(2)}) copy-start(f32[2,2,84,128]{3,1,2,0:T(2,128)} %param.9) | copy-start | bytes 516100
  1.7 30.2 %copy-start.6 = (s32[2,8]{1,0:T(2,128)S(1)}, s32[2,8]{1,0:T(2,128)}, u32[]{:S(2)}) copy-start(s32[2,8]{1,0:T(2,128)} %member_ref.3) | copy-start | bytes 196
  1.7 1.0 %copy-start.3 = (bf16[256,2,336]{0,2,1:T(8,128)(2,1)S(1)}, bf16[256,2,336]{0,2,1:T(8,128)(2,1)}, u32[]{:S(2)}) copy-start(bf16[256,2,336]{0,2,1:T(8,128)(2,1)} %param.16) | copy-start | bytes 1032196
  2.7 0.7 copy-start.4
  3.4 0.7 copy-start.7
  4.1 0.7 copy-start.8
  4.8 0.7 copy-start.9
  6.5 1.5 %collective-permute-start.5 = (bf16[128,256]{1,0:T(8,128)(2,1)S(1)}, bf16[128,256]{1,0:T(8,128)(2,1)S(1)}, u32[]{:S(2)}, u32[]{:S(2)}) collective-permute-start(bf16[128,256]{1,0:T(8,128)(2,1)S(1)} %get-tuple-element.17), channel_id=1, source_target_pairs={{0,1},{1,0},{2,3},{3,2},{4,5},{5,4},{6,7},{7,6},{8,9},{9,8},{10,11... | collective-permute-start | bytes 196616 | tf_op jit(solution)/shard_map/ppermute | solution.py:285
  8.0 5.3 %collective-permute-start.6 = (bf16[128,256]{1,0:T(8,128)(2,1)S(1)}, bf16[128,256]{1,0:T(8,128)(2,1)S(1)}, u32[]{:S(2)}, u32[]{:S(2)}) collective-permute-start(bf16[128,256]{1,0:T(8,128)(2,1)S(1)} %fusion.16), channel_id=1, source_target_pairs={{0,2},{1,3},{2,0},{3,1},{4,6},{5,7},{6,4},{7,5},{8,10},{9,11},{10,... | collective-permute-start | bytes 196616 | tf_op jit(solution)/shard_map/ppermute | solution.py:285
  13.3 5.5 %collective-permute-start.7 = (bf16[128,256]{1,0:T(8,128)(2,1)S(1)}, bf16[128,256]{1,0:T(8,128)(2,1)S(1)}, u32[]{:S(2)}, u32[]{:S(2)}) collective-permute-start(bf16[128,256]{1,0:T(8,128)(2,1)S(1)} %get-tuple-element.35), channel_id=1, source_target_pairs={{0,4},{4,0},{8,12},{12,8},{16,20},{20,16},{24,28},{28,24},{1,5},{5... | collective-permute-start | bytes 196616 | tf_op jit(solution)/shard_map/ppermute | solution.py:285
  15.2 8.0 %collective-permute-start.1 = (bf16[2,2,84,128]{3,2,1,0:T(8,128)(2,1)S(1)}, bf16[2,2,84,128]{3,2,1,0:T(8,128)(2,1)S(1)}, u32[]{:S(2)}, u32[]{:S(2)}) collective-permute-start(bf16[2,2,84,128]{3,2,1,0:T(8,128)(2,1)S(1)} %round.1.x_ref), channel_id=1, source_target_pairs={{0,28},{4,8},{8,4},{12,16},{16,12},{20,24},{24,20},{28,0},{1,29},{... | collective-permute-start | bytes 258056 | tf_op jit(solution)/shard_map/ppermute | solution.py:293
  18.8 5.1 %collective-permute-start = (bf16[2,2,84,128]{3,2,1,0:T(8,128)(2,1)S(1)}, bf16[2,2,84,128]{3,2,1,0:T(8,128)(2,1)S(1)}, u32[]{:S(2)}, u32[]{:S(2)}) collective-permute-start(bf16[2,2,84,128]{3,2,1,0:T(8,128)(2,1)S(1)} %round.1.x_ref), channel_id=1, source_target_pairs={{0,4},{4,0},{8,12},{12,8},{16,20},{20,16},{24,28},{28,24},{1,5},{5... | collective-permute-start | bytes 258056 | tf_op jit(solution)/shard_map/ppermute | solution.py:285
  18.8 6.7 %collective-permute-start.8 = (bf16[128,256]{1,0:T(8,128)(2,1)S(1)}, bf16[128,256]{1,0:T(8,128)(2,1)S(1)}, u32[]{:S(2)}, u32[]{:S(2)}) collective-permute-start(bf16[128,256]{1,0:T(8,128)(2,1)S(1)} %fusion.17), channel_id=1, source_target_pairs={{0,8},{4,12},{8,0},{12,4},{16,24},{20,28},{24,16},{28,20},{1,9},{5... | collective-permute-start | bytes 196616 | tf_op jit(solution)/shard_map/ppermute | solution.py:285
  23.9 6.5 %collective-permute-start.3 = (bf16[3,2,2,84,128]{4,3,2,1,0:T(8,128)(2,1)S(1)}, bf16[3,2,2,84,128]{4,3,2,1,0:T(8,128)(2,1)S(1)}, u32[]{:S(2)}, u32[]{:S(2)}) collective-permute-start(bf16[3,2,2,84,128]{4,3,2,1,0:T(8,128)(2,1)S(1)} %pad_maximum_fusion.refs_0_), channel_id=1, source_target_pairs={{0,2},{1,3},{2,0},{3,1},{4,6},{5,7},{6,4},{7,5},{8,10},{9,11},{10,... | collective-permute-start | bytes 774152 | tf_op jit(solution)/shard_map/ppermute | solution.py:285
  25.5 5.2 %collective-permute-start.9 = (bf16[128,256]{1,0:T(8,128)(2,1)S(1)}, bf16[128,256]{1,0:T(8,128)(2,1)S(1)}, u32[]{:S(2)}, u32[]{:S(2)}) collective-permute-start(bf16[128,256]{1,0:T(8,128)(2,1)S(1)} %fusion.20), channel_id=1, source_target_pairs={{0,16},{4,20},{8,24},{12,28},{16,0},{20,4},{24,8},{28,12},{1,17},{... | collective-permute-start | bytes 196616 | tf_op jit(solution)/shard_map/ppermute | solution.py:285
  26.4 4.6 %collective-permute-start.2 = (bf16[3,2,2,84,128]{4,3,2,1,0:T(8,128)(2,1)S(1)}, bf16[3,2,2,84,128]{4,3,2,1,0:T(8,128)(2,1)S(1)}, u32[]{:S(2)}, u32[]{:S(2)}) collective-permute-start(bf16[3,2,2,84,128]{4,3,2,1,0:T(8,128)(2,1)S(1)} %pad_maximum_fusion.refs_0_), channel_id=1, source_target_pairs={{0,1},{1,0},{2,3},{3,2},{4,5},{5,4},{6,7},{7,6},{8,9},{9,8},{10,11... | collective-permute-start | bytes 774152 | tf_op jit(solution)/shard_map/ppermute | solution.py:285
  30.4 1.5 %collective-permute-start.4 = (bf16[3,2,2,84,128]{4,3,2,1,0:T(8,128)(2,1)S(1)}, bf16[3,2,2,84,128]{4,3,2,1,0:T(8,128)(2,1)S(1)}, u32[]{:S(2)}, u32[]{:S(2)}) collective-permute-start(bf16[3,2,2,84,128]{4,3,2,1,0:T(8,128)(2,1)S(1)} %collective-permute-done.3.refs_2_), channel_id=1, source_target_pairs={{0,1},{1,0},{2,3},{3,2},{4,5},{5,4},{6,7},{7,6},{8,9},{9,8},{10,11... | collective-permute-start | bytes 774152 | tf_op jit(solution)/shard_map/ppermute | solution.py:285
  30.8 3.2 %collective-permute-start.10 = (bf16[128,256]{1,0:T(8,128)(2,1)S(1)}, bf16[128,256]{1,0:T(8,128)(2,1)S(1)}, u32[]{:S(2)}, u32[]{:S(2)}) collective-permute-start(bf16[128,256]{1,0:T(8,128)(2,1)S(1)} %get-tuple-element.33), channel_id=1, source_target_pairs={{0,1},{1,0},{2,3},{3,2},{4,5},{5,4},{6,7},{7,6},{8,9},{9,8},{10,11... | collective-permute-start | bytes 196616 | tf_op jit(solution)/shard_map/ppermute | solution.py:285
  34.8 1.3 %collective-permute-start.16 = (bf16[128,256]{1,0:T(8,128)(2,1)S(1)}, bf16[128,256]{1,0:T(8,128)(2,1)S(1)}, u32[]{:S(2)}, u32[]{:S(2)}) collective-permute-start(bf16[128,256]{1,0:T(8,128)(2,1)S(1)} %get-tuple-element.22), channel_id=1, source_target_pairs={{0,1},{1,0},{2,3},{3,2},{4,5},{5,4},{6,7},{7,6},{8,9},{9,8},{10,11... | collective-permute-start | bytes 196616 | tf_op jit(solution)/shard_map/ppermute | solution.py:285
  36.1 4.3 %collective-permute-start.17 = (bf16[128,256]{1,0:T(8,128)(2,1)S(1)}, bf16[128,256]{1,0:T(8,128)(2,1)S(1)}, u32[]{:S(2)}, u32[]{:S(2)}) collective-permute-start(bf16[128,256]{1,0:T(8,128)(2,1)S(1)} %fusion.18), channel_id=1, source_target_pairs={{0,2},{1,3},{2,0},{3,1},{4,6},{5,7},{6,4},{7,5},{8,10},{9,11},{10,... | collective-permute-start | bytes 196616 | tf_op jit(solution)/shard_map/ppermute | solution.py:285
  40.5 4.3 %collective-permute-start.18 = (bf16[128,256]{1,0:T(8,128)(2,1)S(1)}, bf16[128,256]{1,0:T(8,128)(2,1)S(1)}, u32[]{:S(2)}, u32[]{:S(2)}) collective-permute-start(bf16[128,256]{1,0:T(8,128)(2,1)S(1)} %get-tuple-element.31), channel_id=1, source_target_pairs={{0,4},{4,0},{8,12},{12,8},{16,20},{20,16},{24,28},{28,24},{1,5},{5... | collective-permute-start | bytes 196616 | tf_op jit(solution)/shard_map/ppermute | solution.py:285
  40.6 7.6 %collective-permute-start.12 = (bf16[2,2,84,128]{3,2,1,0:T(8,128)(2,1)S(1)}, bf16[2,2,84,128]{3,2,1,0:T(8,128)(2,1)S(1)}, u32[]{:S(2)}, u32[]{:S(2)}) collective-permute-start(bf16[2,2,84,128]{3,2,1,0:T(8,128)(2,1)S(1)} %get-tuple-element.20), channel_id=1, source_target_pairs={{0,28},{4,8},{8,4},{12,16},{16,12},{20,24},{24,20},{28,0},{1,29},{... | collective-permute-start | bytes 258056 | tf_op jit(solution)/shard_map/ppermute | solution.py:293
  43.6 5.3 %collective-permute-start.11 = (bf16[2,2,84,128]{3,2,1,0:T(8,128)(2,1)S(1)}, bf16[2,2,84,128]{3,2,1,0:T(8,128)(2,1)S(1)}, u32[]{:S(2)}, u32[]{:S(2)}) collective-permute-start(bf16[2,2,84,128]{3,2,1,0:T(8,128)(2,1)S(1)} %get-tuple-element.20), channel_id=1, source_target_pairs={{0,4},{4,0},{8,12},{12,8},{16,20},{20,16},{24,28},{28,24},{1,5},{5... | collective-permute-start | bytes 258056 | tf_op jit(solution)/shard_map/ppermute | solution.py:285
  44.8 5.8 %collective-permute-start.19 = (bf16[128,256]{1,0:T(8,128)(2,1)S(1)}, bf16[128,256]{1,0:T(8,128)(2,1)S(1)}, u32[]{:S(2)}, u32[]{:S(2)}) collective-permute-start(bf16[128,256]{1,0:T(8,128)(2,1)S(1)} %fusion.19), channel_id=1, source_target_pairs={{0,8},{4,12},{8,0},{12,4},{16,24},{20,28},{24,16},{28,20},{1,9},{5... | collective-permute-start | bytes 196616 | tf_op jit(solution)/shard_map/ppermute | solution.py:285
  49.0 6.5 %collective-permute-start.14 = (bf16[3,2,2,84,128]{4,3,2,1,0:T(8,128)(2,1)S(1)}, bf16[3,2,2,84,128]{4,3,2,1,0:T(8,128)(2,1)S(1)}, u32[]{:S(2)}, u32[]{:S(2)}) collective-permute-start(bf16[3,2,2,84,128]{4,3,2,1,0:T(8,128)(2,1)S(1)} %pad_maximum_fusion.1.refs_0_), channel_id=1, source_target_pairs={{0,2},{1,3},{2,0},{3,1},{4,6},{5,7},{6,4},{7,5},{8,10},{9,11},{10,... | collective-permute-start | bytes 774152 | tf_op jit(solution)/shard_map/ppermute | solution.py:285
  50.6 5.2 %collective-permute-start.20 = (bf16[128,256]{1,0:T(8,128)(2,1)S(1)}, bf16[128,256]{1,0:T(8,128)(2,1)S(1)}, u32[]{:S(2)}, u32[]{:S(2)}) collective-permute-start(bf16[128,256]{1,0:T(8,128)(2,1)S(1)} %fusion.21), channel_id=1, source_target_pairs={{0,16},{4,20},{8,24},{12,28},{16,0},{20,4},{24,8},{28,12},{1,17},{... | collective-permute-start | bytes 196616 | tf_op jit(solution)/shard_map/ppermute | solution.py:285
  53.2 3.0 %collective-permute-start.13 = (bf16[3,2,2,84,128]{4,3,2,1,0:T(8,128)(2,1)S(1)}, bf16[3,2,2,84,128]{4,3,2,1,0:T(8,128)(2,1)S(1)}, u32[]{:S(2)}, u32[]{:S(2)}) collective-permute-start(bf16[3,2,2,84,128]{4,3,2,1,0:T(8,128)(2,1)S(1)} %pad_maximum_fusion.1.refs_0_), channel_id=1, source_target_pairs={{0,1},{1,0},{2,3},{3,2},{4,5},{5,4},{6,7},{7,6},{8,9},{9,8},{10,11... | collective-permute-start | bytes 774152 | tf_op jit(solution)/shard_map/ppermute | solution.py:285
  55.5 1.5 %collective-permute-start.15 = (bf16[3,2,2,84,128]{4,3,2,1,0:T(8,128)(2,1)S(1)}, bf16[3,2,2,84,128]{4,3,2,1,0:T(8,128)(2,1)S(1)}, u32[]{:S(2)}, u32[]{:S(2)}) collective-permute-start(bf16[3,2,2,84,128]{4,3,2,1,0:T(8,128)(2,1)S(1)} %collective-permute-done.14.refs_2_), channel_id=1, source_target_pairs={{0,1},{1,0},{2,3},{3,2},{4,5},{5,4},{6,7},{7,6},{8,9},{9,8},{10,11... | collective-permute-start | bytes 774152 | tf_op jit(solution)/shard_map/ppermute | solution.py:285
  55.9 3.2 %collective-permute-start.21 = (bf16[128,256]{1,0:T(8,128)(2,1)S(1)}, bf16[128,256]{1,0:T(8,128)(2,1)S(1)}, u32[]{:S(2)}, u32[]{:S(2)}) collective-permute-start(bf16[128,256]{1,0:T(8,128)(2,1)S(1)} %get-tuple-element.29), channel_id=1, source_target_pairs={{0,1},{1,0},{2,3},{3,2},{4,5},{5,4},{6,7},{7,6},{8,9},{9,8},{10,11... | collective-permute-start | bytes 196616 | tf_op jit(solution)/shard_map/ppermute | solution.py:285
  58.2 0.9 %copy-start.2 = (f32[2,2,84,128]{3,1,2,0:T(2,128)S(1)}, f32[2,2,84,128]{3,1,2,0:T(2,128)}, u32[]{:S(2)}) copy-start(f32[2,2,84,128]{3,1,2,0:T(2,128)} %param.9) | copy-start | bytes 516100
  59.7 1.2 %collective-permute-start.22 = (f32[16,128]{1,0:T(8,128)S(1)}, f32[16,128]{1,0:T(8,128)S(1)}, u32[]{:S(2)}, u32[]{:S(2)}) collective-permute-start(f32[16,128]{1,0:T(8,128)S(1)} %get-tuple-element.24), channel_id=1, source_target_pairs={{0,1},{1,0},{2,3},{3,2},{4,5},{5,4},{6,7},{7,6},{8,9},{9,8},{10,11... | collective-permute-start | bytes 24584 | tf_op jit(solution)/shard_map/ppermute | solution.py:285
  60.9 3.7 %collective-permute-start.23 = (f32[16,128]{1,0:T(8,128)S(1)}, f32[16,128]{1,0:T(8,128)S(1)}, u32[]{:S(2)}, u32[]{:S(2)}) collective-permute-start(f32[16,128]{1,0:T(8,128)S(1)} %add.55), channel_id=1, source_target_pairs={{0,2},{1,3},{2,0},{3,1},{4,6},{5,7},{6,4},{7,5},{8,10},{9,11},{10,... | collective-permute-start | bytes 24584 | tf_op jit(solution)/shard_map/ppermute | solution.py:285
  64.6 3.7 %collective-permute-start.24 = (f32[16,128]{1,0:T(8,128)S(1)}, f32[16,128]{1,0:T(8,128)S(1)}, u32[]{:S(2)}, u32[]{:S(2)}) collective-permute-start(f32[16,128]{1,0:T(8,128)S(1)} %add.56), channel_id=1, source_target_pairs={{0,4},{4,0},{8,12},{12,8},{16,20},{20,16},{24,28},{28,24},{1,5},{5... | collective-permute-start | bytes 24584 | tf_op jit(solution)/shard_map/ppermute | solution.py:285
  68.3 3.7 %collective-permute-start.25 = (f32[16,128]{1,0:T(8,128)S(1)}, f32[16,128]{1,0:T(8,128)S(1)}, u32[]{:S(2)}, u32[]{:S(2)}) collective-permute-start(f32[16,128]{1,0:T(8,128)S(1)} %add.57), channel_id=1, source_target_pairs={{0,8},{4,12},{8,0},{12,4},{16,24},{20,28},{24,16},{28,20},{1,9},{5... | collective-permute-start | bytes 24584 | tf_op jit(solution)/shard_map/ppermute | solution.py:285
  71.9 4.5 %collective-permute-start.26 = (f32[16,128]{1,0:T(8,128)S(1)}, f32[16,128]{1,0:T(8,128)S(1)}, u32[]{:S(2)}, u32[]{:S(2)}) collective-permute-start(f32[16,128]{1,0:T(8,128)S(1)} %add.58), channel_id=1, source_target_pairs={{0,16},{4,20},{8,24},{12,28},{16,0},{20,4},{24,8},{28,12},{1,17},{... | collective-permute-start | bytes 24584 | tf_op jit(solution)/shard_map/ppermute | solution.py:285

commit v3 on v2

--- a/solution.py
+++ b/solution.py
@@ -12,9 +12,10 @@
 
 VM = pl.BlockSpec(memory_space=pltpu.VMEM)
 SM = pl.BlockSpec(memory_space=pltpu.SMEM)
-
-
-def call(body, outs, specs, name, scratch=()):
+HB = pl.BlockSpec(memory_space=pltpu.HBM)
+
+
+def call(body, outs, specs, scratch=()):
     return pl.pallas_call(
         body,
         out_shape=outs,
@@ -22,19 +23,15 @@
         out_specs=jax.tree.map(lambda _: VM, outs),
         scratch_shapes=scratch,
         compiler_params=pltpu.CompilerParams(vmem_limit_bytes=16 << 20),
-        name=name,
     )
+
+
+def in_hbm(arrays):
+    return [pltpu.with_memory_space_constraint(v, pltpu.HBM) for v in arrays]
 
 
 def shape(dims, dtype=f32):
     return jax.ShapeDtypeStruct(dims, dtype)
-
-
-def round_body(x_ref, out_ref):
-    count = out_ref.shape[2]
-    for s in range(out_ref.shape[0]):
-        for z in range(2):
-            out_ref[s, z] = x_ref[s, pl.ds(z, count, stride=2), :].astype(bf16)
 
 
 def project(field, plane_ref, columns, spheres):
@@ -67,24 +64,27 @@
 
 
 def first_sums_body(
-    x_ref, plane_ref, wave_ref, pos_ref, weight_ref, mie_ref,
-    send_ref, keep_ref, column_ref, part_ref, held,
+    x_hbm, plane_hbm, wave_hbm, pos_hbm, weight_hbm, mie_hbm,
+    round_ref, send_ref, keep_ref, column_ref, part_ref,
+    x_ref, plane_ref, wave_ref, pos_ref, weight_ref, mie_ref, held, sems,
 ):
-    spheres, _, count, _ = x_ref.shape
-    waves = wave_ref.shape[1]
+    moves = ((wave_hbm, wave_ref), (pos_hbm, pos_ref), (weight_hbm, weight_ref), (mie_hbm, mie_ref))
+    moves += ((plane_hbm, plane_ref), (x_hbm, x_ref))
+    copies = [pltpu.make_async_copy(*move, sems.at[i]) for i, move in enumerate(moves)]
+    for copy in copies:
+        copy.start()
+    for copy in copies:
+        copy.wait()
+    spheres, _, count, _ = round_ref.shape
     b = lax.axis_index("blk")
     for a in range(2):
         part = plane_ref[a, 0:count, :]
         for p in range(1, plane_ref.shape[1] // count):
             part = jnp.where(b == p, plane_ref[a, p * count : (p + 1) * count, :], part)
         part_ref[a] = part
-    row = lax.broadcasted_iota(jnp.int32, (spheres, 1), 0)
     turns = None
     for d in range(3):
-        place = jnp.zeros((spheres, 1), f32)
-        for s in range(spheres):
-            place = jnp.where(row == s, pos_ref[s, d], place)
-        term = wave_ref[d : d + 1, :].astype(f32) * place
+        term = wave_ref[d : d + 1, :].astype(f32) * pos_ref[:, d : d + 1]
         turns = term if turns is None else turns + term
     angles = two_pi * (turns - jnp.floor(turns + 0.5))
     cos, sin = jnp.cos(angles), jnp.sin(angles)
@@ -98,20 +98,34 @@
             held[at : at + 1, 0:count] = mie_ref[s, z : z + 1, :]
     columns = held[...].T
     column_ref[...] = columns
-    field = [[x_ref[s, 0], x_ref[s, 1]] for s in range(spheres)]
+    field = []
+    for s in range(spheres):
+        field.append([x_ref[s, pl.ds(z, count, stride=2), :].astype(bf16) for z in range(2)])
+        round_ref[s, 0] = field[s][0]
+        round_ref[s, 1] = field[s][1]
     split_halves(*project(field, part_ref, columns, spheres), send_ref, keep_ref)
 
 
-def gather_body(shift_ref, member_ref, *refs):
-    *piece_refs, out_ref, held = refs
-    blocks = len(piece_refs)
-    slots, spheres, _, count, _ = piece_refs[0].shape
+def gather_body(shift_hbm, member_hbm, *refs):
+    *piece_refs, out_ref, held, shift_ref, member_ref, sems = refs
+    copies = [
+        pltpu.make_async_copy(shift_hbm, shift_ref, sems.at[0]),
+        pltpu.make_async_copy(member_hbm, member_ref, sems.at[1]),
+    ]
+    for copy in copies:
+        copy.start()
+    blocks = len(piece_refs) // 2
+    near_refs, odd_refs = piece_refs[:blocks], piece_refs[blocks:]
+    spheres, _, _, _ = odd_refs[0].shape
     b = lax.axis_index("blk")
     parity = lax.rem(lax.axis_index("slab"), 2)
-    for slot in range(slots):
+    for slot in range(3):
         for s in range(spheres):
             for z in range(2):
-                parts = [ref[slot, s, z] for ref in piece_refs]
+                if slot < 2:
+                    parts = [ref[slot, s, z] for ref in near_refs]
+                else:
+                    parts = [ref[s, z] for ref in odd_refs]
                 bit = 1
                 while bit < blocks:
                     swap = lax.rem(lax.div(b, bit), 2) == 1
@@ -120,6 +134,8 @@
                     ]
                     bit *= 2
                 held[slot * spheres + s, z] = jnp.concatenate(parts, axis=0)
+    for copy in copies:
+        copy.wait()
     for i in range(out_ref.shape[0]):
         for k in range(out_ref.shape[1]):
             shift = shift_ref[i, k]
@@ -293,6 +309,15 @@
     return lax.ppermute(value, "slab", pairs)
 
 
+def trade_mixed(value, even, odd):
+    blocks = lax.axis_size("blk")
+    pairs = []
+    for i in range(blocks * lax.axis_size("slab")):
+        axis, bit = odd if i % 2 else even
+        pairs.append((i, i ^ (bit if axis == "blk" else bit * blocks)))
+    return lax.ppermute(value, ("slab", "blk"), pairs)
+
+
 def bits(axis, start=1):
     out, bit = [], start
     while bit < lax.axis_size(axis):
@@ -302,20 +327,25 @@
 
 
 def fetch_pieces(own):
-    mine = jnp.stack([own, trade(own, "slab", 1), trade_odd(own)])
-    pieces = {0: mine}
-    for bit in bits("blk", 2):
-        pieces.update({r | bit: trade(value, "blk", bit) for r, value in list(pieces.items())})
-    for r, value in list(pieces.items()):
-        pieces[r | 1] = trade(value, "blk", 1)
-    return [pieces[r] for r in range(len(pieces))]
+    out = []
+    even = trade(own, "slab", 1)
+    groups = [jnp.stack([own, even]), trade_odd(own)]
+    for group in groups:
+        pieces = {0: group}
+        for bit in bits("blk", 2):
+            pieces.update({r | bit: trade(value, "blk", bit) for r, value in list(pieces.items())})
+        for r, value in list(pieces.items()):
+            pieces[r | 1] = trade(value, "blk", 1)
+        out += [pieces[r] for r in range(len(pieces))]
+    return out
 
 
 def total_sums(send, keep):
     keep = keep + trade(send, "blk", 1).astype(f32)
     steps = [("blk", bit) for bit in bits("blk", 2)] + [("slab", bit) for bit in bits("slab")]
-    for axis, bit in steps:
-        keep = keep + trade(keep.astype(bf16), axis, bit).astype(f32)
+    crossed = steps[1::-1] + steps[2:] if len(steps) > 1 else steps
+    for even, odd in zip(steps, crossed):
+        keep = keep + trade_mixed(keep.astype(bf16), even, odd).astype(f32)
     return keep, trade(keep.astype(bf16), "blk", 1)
 
 
@@ -349,38 +379,39 @@
 
     def near_products(own):
         pieces = fetch_pieces(own)
-        slots = pieces[0].shape[0]
-        held = pltpu.VMEM((slots * spheres, 2, count * blocks, n), bf16)
-        gathered = call(gather_body, sources, [SM, SM] + [VM] * blocks, "gather", [held])(
-            pair_shift, pair_member, *pieces
+        table = pltpu.SMEM((spheres, pairs), jnp.int32)
+        buffers = [pltpu.VMEM((3 * spheres, 2, count * blocks, n), bf16), table, table]
+        buffers.append(pltpu.SemaphoreType.DMA((2,)))
+        return near_work(pieces, buffers)
+
+    def near_work(pieces, buffers):
+        gathered = call(gather_body, sources, [HB, HB] + [VM] * (2 * blocks), buffers)(
+            *in_hbm((pair_shift, pair_member)), *pieces
         )
         return jnp.einsum(
             "ikarc,ikzcn->ikazrn", translation, gathered, preferred_element_type=f32
         )
 
-    rounded = call(round_body, field_half, [VM], "round")(x)
-    send, keep, columns, plane = call(
-        first_sums_body,
-        (sums_half, sums, column, part),
-        [VM, VM, VM, SM, VM, VM],
-        "first_sums",
-        [pltpu.VMEM((held_rows, waves), f32)],
-    )(rounded, plane, wave_index.T, positions, ewald_weight.reshape(1, waves), mie_coef)
+    operands = (x, plane, wave_index.T, positions, ewald_weight.reshape(1, waves), mie_coef)
+    buffers = [pltpu.VMEM(v.shape, v.dtype) for v in operands]
+    buffers += [pltpu.VMEM((held_rows, waves), f32), pltpu.SemaphoreType.DMA((len(operands),))]
+    rounded, send, keep, columns, plane = call(
+        first_sums_body, (field_half, sums_half, sums, column, part), [HB] * len(operands), buffers
+    )(*in_hbm(operands))
     mine, other = total_sums(send, keep)
     near = near_products(rounded)
     image, image_rounded, send, keep = call(
-        first_image_body, (field, field_half, sums_half, sums), [VM] * 5, "first_image"
+        first_image_body, (field, field_half, sums_half, sums), [VM] * 5
     )(near, mine, other, columns, plane)
-
     mine, other = total_sums(send, keep)
     near = near_products(image_rounded)
-    image_two, gram = call(second_image_body, (field, shape((16, n))), [VM] * 7, "second_image")(
+    image_two, gram = call(second_image_body, (field, shape((16, n))), [VM] * 7)(
         near, mine, other, columns, plane, x, image
     )
     gram = total_gram(gram)
     flat = shape((spheres, 2 * count, n))
     basis, residual, hessenberg = call(
-        lambda *refs: finish_body(float(entries), *refs), (flat, flat, shape((9, n))), [VM] * 4, "finish"
+        lambda *refs: finish_body(float(entries), *refs), (flat, flat, shape((9, n))), [VM] * 4
     )(gram, x, image, image_two)
 
     def unflatten(value):

time: 77.6 us -> 74 us (0.954)
  local copies, waits for them, and re-layouts: 4.79 us -> 0.02 us
  starting transfers between devices: 28.3 us -> 31.4 us
  waiting for transfers between devices: 35.9 us -> 33.6 us
    ppermute x0 -> x8, starting transfers between devices: none -> 12.3 us  [trade_mixed(): return lax.ppermute(value, ('slab', 'blk'), pairs)]
    ppermute x25 -> x23, starting transfers between devices: 21.6 us -> 11.4 us  [trade(): lax.ppermute(value, axis, [(i, i ^ bit) for i in range(lax.axis_size(axis...]
    ppermute x0 -> x8, waiting for transfers between devices: none -> 6.37 us  [trade_mixed(): return lax.ppermute(value, ('slab', 'blk'), pairs)]
    unnamed x20 -> x4, local copies, waits for them, and re-layouts: 4.79 us -> 0.02 us
    ppermute x2, waiting for transfers between devices: 4.34 us -> 0.01 us  [trade_odd(): return lax.ppermute(value, 'slab', pairs)]
    ppermute x25 -> x23, waiting for transfers between devices: 31.5 us -> 27.2 us  [trade(): lax.ppermute(value, axis, [(i, i ^ bit) for i in range(lax.axis_size(axis...]
    ppermute x2, starting transfers between devices: 6.65 us -> 7.69 us  [trade_odd(): return lax.ppermute(value, 'slab', pairs)]
    pallas_call x6 -> x5, Pallas kernels: 4.55 us -> 4.97 us  [the longest x2 1.82 us: near_work(): call(gather_body, sources, [HB, HB] + [VM] * (2 * blocks), buffers)]
  transfers between devices with their start and end apart: 27 -> 33, of which waited for: 20 -> 18; matrix products, arithmetic and copies ran while one was open for 3% -> 3% of each run, Pallas kernels for 3% -> 2%
where the time goes in v3:
time: 74 us; the launch traced here: 73.8 us
  waiting for transfers between devices  33.6 us (45%)
  starting transfers between devices  31.4 us (42%)
  Pallas kernels  5.83 us (8%)
  matrix products  1.84 us (2%)
  between operations  0.86 us (1%)
    ppermute x23, waiting for transfers between devices, trade(): lax.ppermute(value, axis, [(i, i ^ bit) for i in range(lax.axis_size(axis...  27.2 us
    ppermute x8, starting transfers between devices, trade_mixed(): return lax.ppermute(value, ('slab', 'blk'), pairs)  12.3 us
    ppermute x23, starting transfers between devices, trade(): lax.ppermute(value, axis, [(i, i ^ bit) for i in range(lax.axis_size(axis...  11.4 us
    ppermute x2, starting transfers between devices, trade_odd(): return lax.ppermute(value, 'slab', pairs)  7.69 us
    ppermute x8, waiting for transfers between devices, trade_mixed(): return lax.ppermute(value, ('slab', 'blk'), pairs)  6.37 us
    dot_general x2, matrix products, near_work(): jnp.einsum('ikarc,ikzcn->ikazrn', translation, gathered, preferred_elemen...  1.84 us
    pallas_call x2, Pallas kernels, near_work(): call(gather_body, sources, [HB, HB] + [VM] * (2 * blocks), buffers)  1.82 us
    pallas_call x1, Pallas kernels, per_device(): call(first_sums_body, (field_half, sums_half, sums, column, part), [HB] *...  1.79 us
  transfers between devices with their start and end apart: 33, of which 18 were waited for; matrix products, arithmetic and copies ran while one was open for 3% of the time, Pallas kernels for 2%

profile of v3, /device:TPU:0, one launch (start us, length us, event | category | flops | bytes accessed | tf_op | source)
XLA Modules:
  0.0 73.8 jit_solution(16008971536104527243)
XLA Ops:
  0.6 0.0 copy-start
  0.6 1.8 %shard_map.112 = (bf16[2,2,84,128]{3,2,1,0:T(8,128)(2,1)S(1)}, bf16[128,256]{1,0:T(8,128)(2,1)S(1)}, f32[128,256]{1,0:T(8,128)S(1)}, f32[256,16]{1,0:T(8,128)S(1)}, bf16[2,84,256]{2,1,0:T(8,128)(2,1)S(1)}) custom-call(f32[2,168,128]{2,1,0:T(8,128)} %bitcast.38, bf16[2,336,256]{2,1,0:T(8,128)(2,1)} %bitcast.43, s32[3,256]{1,0:T(4,128)} %bitcast.46, ...), custom_call_target="tpu_custom_call" | custom-call | tf_op jit(solution)/shard_map/pallas_call | solution.py:398
  2.4 0.6 collective-permute-start.8
  3.0 0.9 %collective-permute-done.8 = bf16[128,256]{1,0:T(8,128)(2,1)S(1)} collective-permute-done((bf16[128,256]{1,0:T(8,128)(2,1)S(1)}, bf16[128,256]{1,0:T(8,128)(2,1)S(1)}, u32[]{:S(2)}, u32[]{:S(2)}) %collective-permute-start.8) | collective-permute-done | bytes 65568 | tf_op jit(solution)/shard_map/ppermute | solution.py:301
  3.9 2.9 %collective-permute-start.9 = (bf16[128,256]{1,0:T(8,128)(2,1)S(1)}, bf16[128,256]{1,0:T(8,128)(2,1)S(1)}, u32[]{:S(2)}, u32[]{:S(2)}) collective-permute-start(bf16[128,256]{1,0:T(8,128)(2,1)S(1)} %fusion.16), channel_id=1, source_target_pairs={{0,2},{1,5},{2,0},{3,7},{4,6},{5,1},{6,4},{7,3},{8,10},{9,13},{10,... | collective-permute-start | bytes 196616 | tf_op jit(solution)/shard_map/ppermute | solution.py:318
  6.8 2.2 %collective-permute-done.9 = bf16[128,256]{1,0:T(8,128)(2,1)S(1)} collective-permute-done((bf16[128,256]{1,0:T(8,128)(2,1)S(1)}, bf16[128,256]{1,0:T(8,128)(2,1)S(1)}, u32[]{:S(2)}, u32[]{:S(2)}) %collective-permute-start.9) | collective-permute-done | bytes 65568 | tf_op jit(solution)/shard_map/ppermute | solution.py:318
  9.1 2.1 %collective-permute-start.10 = (bf16[128,256]{1,0:T(8,128)(2,1)S(1)}, bf16[128,256]{1,0:T(8,128)(2,1)S(1)}, u32[]{:S(2)}, u32[]{:S(2)}) collective-permute-start(bf16[128,256]{1,0:T(8,128)(2,1)S(1)} %get-tuple-element.37), channel_id=1, source_target_pairs={{0,4},{1,3},{2,6},{3,1},{4,0},{5,7},{6,2},{7,5},{8,12},{9,11},{10,... | collective-permute-start | bytes 196616 | tf_op jit(solution)/shard_map/ppermute | solution.py:318
  11.2 3.6 %collective-permute-start.4 = (bf16[2,2,84,128]{3,2,1,0:T(8,128)(2,1)S(1)}, bf16[2,2,84,128]{3,2,1,0:T(8,128)(2,1)S(1)}, u32[]{:S(2)}, u32[]{:S(2)}) collective-permute-start(bf16[2,2,84,128]{3,2,1,0:T(8,128)(2,1)S(1)} %get-tuple-element.17), channel_id=1, source_target_pairs={{0,28},{4,8},{8,4},{12,16},{16,12},{20,24},{24,20},{28,0},{1,29},{... | collective-permute-start | bytes 258056 | tf_op jit(solution)/shard_map/ppermute | solution.py:309
  14.7 0.0 collective-permute-start
  14.8 0.3 collective-permute-done.10
  15.1 1.9 %collective-permute-start.11 = (bf16[128,256]{1,0:T(8,128)(2,1)S(1)}, bf16[128,256]{1,0:T(8,128)(2,1)S(1)}, u32[]{:S(2)}, u32[]{:S(2)}) collective-permute-start(bf16[128,256]{1,0:T(8,128)(2,1)S(1)} %fusion.17), channel_id=1, source_target_pairs={{0,8},{1,9},{2,10},{3,11},{4,12},{5,13},{6,14},{7,15},{8,0},{9,1},... | collective-permute-start | bytes 196616 | tf_op jit(solution)/shard_map/ppermute | solution.py:318
  17.0 2.8 %collective-permute-done = bf16[2,2,84,128]{3,2,1,0:T(8,128)(2,1)S(1)} collective-permute-done((bf16[2,2,84,128]{3,2,1,0:T(8,128)(2,1)S(1)}, bf16[2,2,84,128]{3,2,1,0:T(8,128)(2,1)S(1)}, u32[]{:S(2)}, u32[]{:S(2)}) %collective-permute-start) | collective-permute-done | bytes 86048 | tf_op jit(solution)/shard_map/ppermute | solution.py:301
  19.8 1.6 %collective-permute-start.2 = (bf16[2,2,2,84,128]{4,3,2,1,0:T(8,128)(2,1)S(1)}, bf16[2,2,2,84,128]{4,3,2,1,0:T(8,128)(2,1)S(1)}, u32[]{:S(2)}, u32[]{:S(2)}) collective-permute-start(bf16[2,2,2,84,128]{4,3,2,1,0:T(8,128)(2,1)S(1)} %pad_maximum_fusion.refs_0_), channel_id=1, source_target_pairs={{0,2},{1,3},{2,0},{3,1},{4,6},{5,7},{6,4},{7,5},{8,10},{9,11},{10,... | collective-permute-start | bytes 516104 | tf_op jit(solution)/shard_map/ppermute | solution.py:301
  21.4 0.5 collective-permute-start.6
  22.0 0.7 collective-permute-start.12
  22.6 0.0 collective-permute-start.1
  22.6 0.5 collective-permute-start.5
  23.1 3.5 %collective-permute-done.6.refs_6_ = bf16[2,2,84,128]{3,2,1,0:T(8,128)(2,1)S(1)} collective-permute-done((bf16[2,2,84,128]{3,2,1,0:T(8,128)(2,1)S(1)}, bf16[2,2,84,128]{3,2,1,0:T(8,128)(2,1)S(1)}, u32[]{:S(2)}, u32[]{:S(2)}) %collective-permute-start.6) | collective-permute-done | bytes 86048 | tf_op jit(solution)/shard_map/ppermute | solution.py:301
  26.6 0.0 collective-permute-start.7
  26.6 0.5 collective-permute-start.3
  27.2 0.0 collective-permute-done.12
  27.2 0.1 collective-permute-start.13
  27.3 0.0 collective-permute-done.5.refs_5_
  27.3 0.6 collective-permute-done.7.refs_7_
  27.9 0.0 collective-permute-done.1.refs_1_
  27.9 0.3 collective-permute-done.3.refs_3_
  28.2 0.9 %shard_map.113 = bf16[2,8,2,336,128]{4,3,2,1,0:T(8,128)(2,1)S(1)} custom-call(s32[2,8]{1,0:T(2,128)} %shift_hbm.3, s32[2,8]{1,0:T(2,128)} %member_hbm.3, bf16[2,2,2,84,128]{4,3,2,1,0:T(8,128)(2,1)S(1)} %pad_maximum_fusion.refs_0_, bf16[2,2,2,84,128]{4,3,2,1,0:T(8,128)(2,1)S(1)} %collective-permute-done.1.refs_1_, ...), custom_call_target="tpu_custom_call" | custom-call | tf_op jit(solution)/shard_map/pallas_call | solution.py:388
  29.1 0.9 %fusion.6.near_ref = f32[2,8,2,2,84,128]{5,4,3,2,1,0:T(8,128)S(1)} fusion(bf16[2,8,2,84,336,1]{4,2,3,1,0,5:T(2,128)(2,1)S(1)} %bitcast.36, bf16[2,8,2,336,128]{4,3,2,1,0:T(8,128)(2,1)S(1)} %shard_map.113), kind=kOutput, calls=%fused_computation.6 | convolution fusion | flops 462422016 | bytes 7311360 | tf_op jit(solution)/shard_map/ikarc,ikzcn->ikazrn/dot_general | solution.py:391
  30.1 0.0 collective-permute-done.13.other_ref
  30.1 0.8 %shard_map.114 = (f32[2,2,84,128]{3,2,1,0:T(8,128)S(1)}, bf16[2,2,84,128]{3,2,1,0:T(8,128)(2,1)S(1)}, bf16[128,256]{1,0:T(8,128)(2,1)S(1)}, f32[128,256]{1,0:T(8,128)S(1)}) custom-call(f32[2,8,2,2,84,128]{5,4,3,2,1,0:T(8,128)S(1)} %fusion.6.near_ref, f32[128,256]{1,0:T(8,128)S(1)} %get-tuple-element.36.mine_ref, ...), custom_call_target="tpu_custom_call" | custom-call | tf_op jit(solution)/shard_map/pallas_call | solution.py:403
  30.9 0.4 collective-permute-start.22
  31.3 0.9 %collective-permute-done.22 = bf16[128,256]{1,0:T(8,128)(2,1)S(1)} collective-permute-done((bf16[128,256]{1,0:T(8,128)(2,1)S(1)}, bf16[128,256]{1,0:T(8,128)(2,1)S(1)}, u32[]{:S(2)}, u32[]{:S(2)}) %collective-permute-start.22) | collective-permute-done | bytes 65568 | tf_op jit(solution)/shard_map/ppermute | solution.py:301
  32.2 1.3 %collective-permute-start.23 = (bf16[128,256]{1,0:T(8,128)(2,1)S(1)}, bf16[128,256]{1,0:T(8,128)(2,1)S(1)}, u32[]{:S(2)}, u32[]{:S(2)}) collective-permute-start(bf16[128,256]{1,0:T(8,128)(2,1)S(1)} %fusion.18), channel_id=1, source_target_pairs={{0,2},{1,5},{2,0},{3,7},{4,6},{5,1},{6,4},{7,3},{8,10},{9,13},{10,... | collective-permute-start | bytes 196616 | tf_op jit(solution)/shard_map/ppermute | solution.py:318
  33.5 3.0 %collective-permute-done.23 = bf16[128,256]{1,0:T(8,128)(2,1)S(1)} collective-permute-done((bf16[128,256]{1,0:T(8,128)(2,1)S(1)}, bf16[128,256]{1,0:T(8,128)(2,1)S(1)}, u32[]{:S(2)}, u32[]{:S(2)}) %collective-permute-start.23) | collective-permute-done | bytes 65568 | tf_op jit(solution)/shard_map/ppermute | solution.py:318
  36.6 0.4 collective-permute-start.24
  36.9 4.1 %collective-permute-start.18 = (bf16[2,2,84,128]{3,2,1,0:T(8,128)(2,1)S(1)}, bf16[2,2,84,128]{3,2,1,0:T(8,128)(2,1)S(1)}, u32[]{:S(2)}, u32[]{:S(2)}) collective-permute-start(bf16[2,2,84,128]{3,2,1,0:T(8,128)(2,1)S(1)} %get-tuple-element.22), channel_id=1, source_target_pairs={{0,28},{4,8},{8,4},{12,16},{16,12},{20,24},{24,20},{28,0},{1,29},{... | collective-permute-start | bytes 258056 | tf_op jit(solution)/shard_map/ppermute | solution.py:309
  41.0 0.0 collective-permute-done.24
  41.1 1.8 %collective-permute-start.25 = (bf16[128,256]{1,0:T(8,128)(2,1)S(1)}, bf16[128,256]{1,0:T(8,128)(2,1)S(1)}, u32[]{:S(2)}, u32[]{:S(2)}) collective-permute-start(bf16[128,256]{1,0:T(8,128)(2,1)S(1)} %fusion.19), channel_id=1, source_target_pairs={{0,8},{1,9},{2,10},{3,11},{4,12},{5,13},{6,14},{7,15},{8,0},{9,1},... | collective-permute-start | bytes 196616 | tf_op jit(solution)/shard_map/ppermute | solution.py:318
  42.9 2.7 %collective-permute-done.14 = bf16[2,2,84,128]{3,2,1,0:T(8,128)(2,1)S(1)} collective-permute-done((bf16[2,2,84,128]{3,2,1,0:T(8,128)(2,1)S(1)}, bf16[2,2,84,128]{3,2,1,0:T(8,128)(2,1)S(1)}, u32[]{:S(2)}, u32[]{:S(2)}) %collective-permute-start.14) | collective-permute-done | bytes 86048 | tf_op jit(solution)/shard_map/ppermute | solution.py:301
  45.6 0.9 %collective-permute-start.16 = (bf16[2,2,2,84,128]{4,3,2,1,0:T(8,128)(2,1)S(1)}, bf16[2,2,2,84,128]{4,3,2,1,0:T(8,128)(2,1)S(1)}, u32[]{:S(2)}, u32[]{:S(2)}) collective-permute-start(bf16[2,2,2,84,128]{4,3,2,1,0:T(8,128)(2,1)S(1)} %pad_maximum_fusion.1.refs_0_), channel_id=1, source_target_pairs={{0,2},{1,3},{2,0},{3,1},{4,6},{5,7},{6,4},{7,5},{8,10},{9,11},{10,... | collective-permute-start | bytes 516104 | tf_op jit(solution)/shard_map/ppermute | solution.py:301
  46.5 0.0 collective-permute-done.18.refs_4_
  46.5 1.2 %collective-permute-start.20 = (bf16[2,2,84,128]{3,2,1,0:T(8,128)(2,1)S(1)}, bf16[2,2,84,128]{3,2,1,0:T(8,128)(2,1)S(1)}, u32[]{:S(2)}, u32[]{:S(2)}) collective-permute-start(bf16[2,2,84,128]{3,2,1,0:T(8,128)(2,1)S(1)} %collective-permute-done.18.refs_4_), channel_id=1, source_target_pairs={{0,2},{1,3},{2,0},{3,1},{4,6},{5,7},{6,4},{7,5},{8,10},{9,11},{10,... | collective-permute-start | bytes 258056 | tf_op jit(solution)/shard_map/ppermute | solution.py:301
  47.7 1.3 %collective-permute-start.26 = (bf16[128,256]{1,0:T(8,128)(2,1)S(1)}, bf16[128,256]{1,0:T(8,128)(2,1)S(1)}, u32[]{:S(2)}, u32[]{:S(2)}) collective-permute-start(bf16[128,256]{1,0:T(8,128)(2,1)S(1)} %fusion.21), channel_id=1, source_target_pairs={{0,16},{1,17},{2,18},{3,19},{4,20},{5,21},{6,22},{7,23},{8,24},{9,... | collective-permute-start | bytes 196616 | tf_op jit(solution)/shard_map/ppermute | solution.py:318
  49.0 0.5 collective-permute-start.19
  49.5 2.6 %collective-permute-done.20.refs_6_ = bf16[2,2,84,128]{3,2,1,0:T(8,128)(2,1)S(1)} collective-permute-done((bf16[2,2,84,128]{3,2,1,0:T(8,128)(2,1)S(1)}, bf16[2,2,84,128]{3,2,1,0:T(8,128)(2,1)S(1)}, u32[]{:S(2)}, u32[]{:S(2)}) %collective-permute-start.20) | collective-permute-done | bytes 86048 | tf_op jit(solution)/shard_map/ppermute | solution.py:301
  52.1 0.5 collective-permute-start.17
  52.6 0.7 %collective-permute-done.26 = bf16[128,256]{1,0:T(8,128)(2,1)S(1)} collective-permute-done((bf16[128,256]{1,0:T(8,128)(2,1)S(1)}, bf16[128,256]{1,0:T(8,128)(2,1)S(1)}, u32[]{:S(2)}, u32[]{:S(2)}) %collective-permute-start.26) | collective-permute-done | bytes 65568 | tf_op jit(solution)/shard_map/ppermute | solution.py:318
  53.4 0.1 collective-permute-start.27
  53.5 0.1 collective-permute-done.17.refs_3_
  53.7 0.9 %shard_map.115 = bf16[2,8,2,336,128]{4,3,2,1,0:T(8,128)(2,1)S(1)} custom-call(s32[2,8]{1,0:T(2,128)} %shift_hbm.3, s32[2,8]{1,0:T(2,128)} %member_hbm.3, bf16[2,2,2,84,128]{4,3,2,1,0:T(8,128)(2,1)S(1)} %pad_maximum_fusion.1.refs_0_, bf16[2,2,2,84,128]{4,3,2,1,0:T(8,128)(2,1)S(1)} %collective-permute-done.15.refs_1_, ...), custom_call_target="tpu_custom_call" | custom-call | tf_op jit(solution)/shard_map/pallas_call | solution.py:388
  54.6 0.0 copy-start.1
  54.6 0.9 %fusion.11.near_ref = f32[2,8,2,2,84,128]{5,4,3,2,1,0:T(8,128)S(1)} fusion(bf16[2,8,2,84,336,1]{4,2,3,1,0,5:T(2,128)(2,1)S(1)} %bitcast.37, bf16[2,8,2,336,128]{4,3,2,1,0:T(8,128)(2,1)S(1)} %shard_map.115), kind=kOutput, calls=%fused_computation.7 | convolution fusion | flops 462422016 | bytes 7311360 | tf_op jit(solution)/shard_map/ikarc,ikzcn->ikazrn/dot_general | solution.py:391
  55.6 0.6 shard_map.116
  56.2 0.4 collective-permute-start.28
  56.6 0.8 %collective-permute-done.28 = f32[16,128]{1,0:T(8,128)S(1)} collective-permute-done((f32[16,128]{1,0:T(8,128)S(1)}, f32[16,128]{1,0:T(8,128)S(1)}, u32[]{:S(2)}, u32[]{:S(2)}) %collective-permute-start.28) | collective-permute-done | bytes 8224 | tf_op jit(solution)/shard_map/ppermute | solution.py:301
  57.4 1.7 %collective-permute-start.29 = (f32[16,128]{1,0:T(8,128)S(1)}, f32[16,128]{1,0:T(8,128)S(1)}, u32[]{:S(2)}, u32[]{:S(2)}) collective-permute-start(f32[16,128]{1,0:T(8,128)S(1)} %add.55), channel_id=1, source_target_pairs={{0,2},{1,3},{2,0},{3,1},{4,6},{5,7},{6,4},{7,5},{8,10},{9,11},{10,... | collective-permute-start | bytes 24584 | tf_op jit(solution)/shard_map/ppermute | solution.py:301
  59.2 1.9 %collective-permute-done.29 = f32[16,128]{1,0:T(8,128)S(1)} collective-permute-done((f32[16,128]{1,0:T(8,128)S(1)}, f32[16,128]{1,0:T(8,128)S(1)}, u32[]{:S(2)}, u32[]{:S(2)}) %collective-permute-start.29) | collective-permute-done | bytes 8224 | tf_op jit(solution)/shard_map/ppermute | solution.py:301
  61.1 0.1 collective-permute-start.30
  61.2 3.6 %collective-permute-done.30 = f32[16,128]{1,0:T(8,128)S(1)} collective-permute-done((f32[16,128]{1,0:T(8,128)S(1)}, f32[16,128]{1,0:T(8,128)S(1)}, u32[]{:S(2)}, u32[]{:S(2)}) %collective-permute-start.30) | collective-permute-done | bytes 8224 | tf_op jit(solution)/shard_map/ppermute | solution.py:301
  64.7 0.2 collective-permute-start.31
  64.9 3.5 %collective-permute-done.31 = f32[16,128]{1,0:T(8,128)S(1)} collective-permute-done((f32[16,128]{1,0:T(8,128)S(1)}, f32[16,128]{1,0:T(8,128)S(1)}, u32[]{:S(2)}, u32[]{:S(2)}) %collective-permute-start.31) | collective-permute-done | bytes 8224 | tf_op jit(solution)/shard_map/ppermute | solution.py:301
  68.4 1.6 %collective-permute-start.32 = (f32[16,128]{1,0:T(8,128)S(1)}, f32[16,128]{1,0:T(8,128)S(1)}, u32[]{:S(2)}, u32[]{:S(2)}) collective-permute-start(f32[16,128]{1,0:T(8,128)S(1)} %add.58), channel_id=1, source_target_pairs={{0,16},{4,20},{8,24},{12,28},{16,0},{20,4},{24,8},{28,12},{1,17},{... | collective-permute-start | bytes 24584 | tf_op jit(solution)/shard_map/ppermute | solution.py:301
  70.0 3.0 %collective-permute-done.32 = f32[16,128]{1,0:T(8,128)S(1)} collective-permute-done((f32[16,128]{1,0:T(8,128)S(1)}, f32[16,128]{1,0:T(8,128)S(1)}, u32[]{:S(2)}, u32[]{:S(2)}) %collective-permute-start.32) | collective-permute-done | bytes 8224 | tf_op jit(solution)/shard_map/ppermute | solution.py:301
  72.9 0.9 %shard_map.117 = (f32[2,168,128]{2,1,0:T(8,128)}, f32[2,168,128]{2,1,0:T(8,128)}, f32[9,128]{1,0:T(8,128)}) custom-call(f32[16,128]{1,0:T(8,128)S(1)} %add.59.refs_0_, f32[2,168,128]{2,1,0:T(8,128)S(1)} %bitcast.40, f32[2,2,84,128]{3,2,1,0:T(8,128)S(1)} %get-tuple-element.25.g_ref.refs_2_, f32[2,2,84,128]{3,2,1,0:T(8,128)S(1)} %get-tuple-element.27.refs_3_), custom_call_target="tpu_custom_call" | custom-call | tf_op jit(solution)/shard_map/pallas_call | solution.py:413
  (31 shorter events, 0.3 us)
Async XLA Ops:
  0.6 28.5 %copy-start = (bf16[2,8,2,84,336]{4,2,3,1,0:T(2,128)(2,1)S(1)}, bf16[2,8,2,84,336]{4,2,3,1,0:T(2,128)(2,1)}, u32[]{:S(2)}) copy-start(bf16[2,8,2,84,336]{4,2,3,1,0:T(2,128)(2,1)} %param.11) | copy-start | bytes 5419012
  2.4 1.5 %collective-permute-start.8 = (bf16[128,256]{1,0:T(8,128)(2,1)S(1)}, bf16[128,256]{1,0:T(8,128)(2,1)S(1)}, u32[]{:S(2)}, u32[]{:S(2)}) collective-permute-start(bf16[128,256]{1,0:T(8,128)(2,1)S(1)} %get-tuple-element.19), channel_id=1, source_target_pairs={{0,1},{1,0},{2,3},{3,2},{4,5},{5,4},{6,7},{7,6},{8,9},{9,8},{10,11... | collective-permute-start | bytes 196616 | tf_op jit(solution)/shard_map/ppermute | solution.py:301
  3.9 5.2 %collective-permute-start.9 = (bf16[128,256]{1,0:T(8,128)(2,1)S(1)}, bf16[128,256]{1,0:T(8,128)(2,1)S(1)}, u32[]{:S(2)}, u32[]{:S(2)}) collective-permute-start(bf16[128,256]{1,0:T(8,128)(2,1)S(1)} %fusion.16), channel_id=1, source_target_pairs={{0,2},{1,5},{2,0},{3,7},{4,6},{5,1},{6,4},{7,3},{8,10},{9,13},{10,... | collective-permute-start | bytes 196616 | tf_op jit(solution)/shard_map/ppermute | solution.py:318
  9.1 5.9 %collective-permute-start.10 = (bf16[128,256]{1,0:T(8,128)(2,1)S(1)}, bf16[128,256]{1,0:T(8,128)(2,1)S(1)}, u32[]{:S(2)}, u32[]{:S(2)}) collective-permute-start(bf16[128,256]{1,0:T(8,128)(2,1)S(1)} %get-tuple-element.37), channel_id=1, source_target_pairs={{0,4},{1,3},{2,6},{3,1},{4,0},{5,7},{6,2},{7,5},{8,12},{9,11},{10,... | collective-permute-start | bytes 196616 | tf_op jit(solution)/shard_map/ppermute | solution.py:318
  11.2 10.2 %collective-permute-start.4 = (bf16[2,2,84,128]{3,2,1,0:T(8,128)(2,1)S(1)}, bf16[2,2,84,128]{3,2,1,0:T(8,128)(2,1)S(1)}, u32[]{:S(2)}, u32[]{:S(2)}) collective-permute-start(bf16[2,2,84,128]{3,2,1,0:T(8,128)(2,1)S(1)} %get-tuple-element.17), channel_id=1, source_target_pairs={{0,28},{4,8},{8,4},{12,16},{16,12},{20,24},{24,20},{28,0},{1,29},{... | collective-permute-start | bytes 258056 | tf_op jit(solution)/shard_map/ppermute | solution.py:309
  14.7 5.0 %collective-permute-start = (bf16[2,2,84,128]{3,2,1,0:T(8,128)(2,1)S(1)}, bf16[2,2,84,128]{3,2,1,0:T(8,128)(2,1)S(1)}, u32[]{:S(2)}, u32[]{:S(2)}) collective-permute-start(bf16[2,2,84,128]{3,2,1,0:T(8,128)(2,1)S(1)} %get-tuple-element.17), channel_id=1, source_target_pairs={{0,4},{4,0},{8,12},{12,8},{16,20},{20,16},{24,28},{28,24},{1,5},{5... | collective-permute-start | bytes 258056 | tf_op jit(solution)/shard_map/ppermute | solution.py:301
  15.1 6.9 %collective-permute-start.11 = (bf16[128,256]{1,0:T(8,128)(2,1)S(1)}, bf16[128,256]{1,0:T(8,128)(2,1)S(1)}, u32[]{:S(2)}, u32[]{:S(2)}) collective-permute-start(bf16[128,256]{1,0:T(8,128)(2,1)S(1)} %fusion.17), channel_id=1, source_target_pairs={{0,8},{1,9},{2,10},{3,11},{4,12},{5,13},{6,14},{7,15},{8,0},{9,1},... | collective-permute-start | bytes 196616 | tf_op jit(solution)/shard_map/ppermute | solution.py:318
  19.8 6.8 %collective-permute-start.2 = (bf16[2,2,2,84,128]{4,3,2,1,0:T(8,128)(2,1)S(1)}, bf16[2,2,2,84,128]{4,3,2,1,0:T(8,128)(2,1)S(1)}, u32[]{:S(2)}, u32[]{:S(2)}) collective-permute-start(bf16[2,2,2,84,128]{4,3,2,1,0:T(8,128)(2,1)S(1)} %pad_maximum_fusion.refs_0_), channel_id=1, source_target_pairs={{0,2},{1,3},{2,0},{3,1},{4,6},{5,7},{6,4},{7,5},{8,10},{9,11},{10,... | collective-permute-start | bytes 516104 | tf_op jit(solution)/shard_map/ppermute | solution.py:301
  21.4 5.2 %collective-permute-start.6 = (bf16[2,2,84,128]{3,2,1,0:T(8,128)(2,1)S(1)}, bf16[2,2,84,128]{3,2,1,0:T(8,128)(2,1)S(1)}, u32[]{:S(2)}, u32[]{:S(2)}) collective-permute-start(bf16[2,2,84,128]{3,2,1,0:T(8,128)(2,1)S(1)} %collective-permute-done.4.refs_4_), channel_id=1, source_target_pairs={{0,2},{1,3},{2,0},{3,1},{4,6},{5,7},{6,4},{7,5},{8,10},{9,11},{10,... | collective-permute-start | bytes 258056 | tf_op jit(solution)/shard_map/ppermute | solution.py:301
  22.0 5.2 %collective-permute-start.12 = (bf16[128,256]{1,0:T(8,128)(2,1)S(1)}, bf16[128,256]{1,0:T(8,128)(2,1)S(1)}, u32[]{:S(2)}, u32[]{:S(2)}) collective-permute-start(bf16[128,256]{1,0:T(8,128)(2,1)S(1)} %fusion.20), channel_id=1, source_target_pairs={{0,16},{1,17},{2,18},{3,19},{4,20},{5,21},{6,22},{7,23},{8,24},{9,... | collective-permute-start | bytes 196616 | tf_op jit(solution)/shard_map/ppermute | solution.py:318
  22.6 5.3 %collective-permute-start.1 = (bf16[2,2,2,84,128]{4,3,2,1,0:T(8,128)(2,1)S(1)}, bf16[2,2,2,84,128]{4,3,2,1,0:T(8,128)(2,1)S(1)}, u32[]{:S(2)}, u32[]{:S(2)}) collective-permute-start(bf16[2,2,2,84,128]{4,3,2,1,0:T(8,128)(2,1)S(1)} %pad_maximum_fusion.refs_0_), channel_id=1, source_target_pairs={{0,1},{1,0},{2,3},{3,2},{4,5},{5,4},{6,7},{7,6},{8,9},{9,8},{10,11... | collective-permute-start | bytes 516104 | tf_op jit(solution)/shard_map/ppermute | solution.py:301
  22.6 4.7 %collective-permute-start.5 = (bf16[2,2,84,128]{3,2,1,0:T(8,128)(2,1)S(1)}, bf16[2,2,84,128]{3,2,1,0:T(8,128)(2,1)S(1)}, u32[]{:S(2)}, u32[]{:S(2)}) collective-permute-start(bf16[2,2,84,128]{3,2,1,0:T(8,128)(2,1)S(1)} %collective-permute-done.4.refs_4_), channel_id=1, source_target_pairs={{0,1},{1,0},{2,3},{3,2},{4,5},{5,4},{6,7},{7,6},{8,9},{9,8},{10,11... | collective-permute-start | bytes 258056 | tf_op jit(solution)/shard_map/ppermute | solution.py:301
  26.6 1.3 %collective-permute-start.7 = (bf16[2,2,84,128]{3,2,1,0:T(8,128)(2,1)S(1)}, bf16[2,2,84,128]{3,2,1,0:T(8,128)(2,1)S(1)}, u32[]{:S(2)}, u32[]{:S(2)}) collective-permute-start(bf16[2,2,84,128]{3,2,1,0:T(8,128)(2,1)S(1)} %collective-permute-done.6.refs_6_), channel_id=1, source_target_pairs={{0,1},{1,0},{2,3},{3,2},{4,5},{5,4},{6,7},{7,6},{8,9},{9,8},{10,11... | collective-permute-start | bytes 258056 | tf_op jit(solution)/shard_map/ppermute | solution.py:301
  26.6 1.6 %collective-permute-start.3 = (bf16[2,2,2,84,128]{4,3,2,1,0:T(8,128)(2,1)S(1)}, bf16[2,2,2,84,128]{4,3,2,1,0:T(8,128)(2,1)S(1)}, u32[]{:S(2)}, u32[]{:S(2)}) collective-permute-start(bf16[2,2,2,84,128]{4,3,2,1,0:T(8,128)(2,1)S(1)} %collective-permute-done.2.refs_2_), channel_id=1, source_target_pairs={{0,1},{1,0},{2,3},{3,2},{4,5},{5,4},{6,7},{7,6},{8,9},{9,8},{10,11... | collective-permute-start | bytes 516104 | tf_op jit(solution)/shard_map/ppermute | solution.py:301
  27.2 2.8 %collective-permute-start.13 = (bf16[128,256]{1,0:T(8,128)(2,1)S(1)}, bf16[128,256]{1,0:T(8,128)(2,1)S(1)}, u32[]{:S(2)}, u32[]{:S(2)}) collective-permute-start(bf16[128,256]{1,0:T(8,128)(2,1)S(1)} %get-tuple-element.35), channel_id=1, source_target_pairs={{0,1},{1,0},{2,3},{3,2},{4,5},{5,4},{6,7},{7,6},{8,9},{9,8},{10,11... | collective-permute-start | bytes 196616 | tf_op jit(solution)/shard_map/ppermute | solution.py:301
  30.9 1.3 %collective-permute-start.22 = (bf16[128,256]{1,0:T(8,128)(2,1)S(1)}, bf16[128,256]{1,0:T(8,128)(2,1)S(1)}, u32[]{:S(2)}, u32[]{:S(2)}) collective-permute-start(bf16[128,256]{1,0:T(8,128)(2,1)S(1)} %get-tuple-element.24), channel_id=1, source_target_pairs={{0,1},{1,0},{2,3},{3,2},{4,5},{5,4},{6,7},{7,6},{8,9},{9,8},{10,11... | collective-permute-start | bytes 196616 | tf_op jit(solution)/shard_map/ppermute | solution.py:301
  32.2 4.3 %collective-permute-start.23 = (bf16[128,256]{1,0:T(8,128)(2,1)S(1)}, bf16[128,256]{1,0:T(8,128)(2,1)S(1)}, u32[]{:S(2)}, u32[]{:S(2)}) collective-permute-start(bf16[128,256]{1,0:T(8,128)(2,1)S(1)} %fusion.18), channel_id=1, source_target_pairs={{0,2},{1,5},{2,0},{3,7},{4,6},{5,1},{6,4},{7,3},{8,10},{9,13},{10,... | collective-permute-start | bytes 196616 | tf_op jit(solution)/shard_map/ppermute | solution.py:318
  36.6 4.5 %collective-permute-start.24 = (bf16[128,256]{1,0:T(8,128)(2,1)S(1)}, bf16[128,256]{1,0:T(8,128)(2,1)S(1)}, u32[]{:S(2)}, u32[]{:S(2)}) collective-permute-start(bf16[128,256]{1,0:T(8,128)(2,1)S(1)} %get-tuple-element.33), channel_id=1, source_target_pairs={{0,4},{1,3},{2,6},{3,1},{4,0},{5,7},{6,2},{7,5},{8,12},{9,11},{10,... | collective-permute-start | bytes 196616 | tf_op jit(solution)/shard_map/ppermute | solution.py:318
  36.9 9.6 %collective-permute-start.18 = (bf16[2,2,84,128]{3,2,1,0:T(8,128)(2,1)S(1)}, bf16[2,2,84,128]{3,2,1,0:T(8,128)(2,1)S(1)}, u32[]{:S(2)}, u32[]{:S(2)}) collective-permute-start(bf16[2,2,84,128]{3,2,1,0:T(8,128)(2,1)S(1)} %get-tuple-element.22), channel_id=1, source_target_pairs={{0,28},{4,8},{8,4},{12,16},{16,12},{20,24},{24,20},{28,0},{1,29},{... | collective-permute-start | bytes 258056 | tf_op jit(solution)/shard_map/ppermute | solution.py:309
  41.0 4.5 %collective-permute-start.14 = (bf16[2,2,84,128]{3,2,1,0:T(8,128)(2,1)S(1)}, bf16[2,2,84,128]{3,2,1,0:T(8,128)(2,1)S(1)}, u32[]{:S(2)}, u32[]{:S(2)}) collective-permute-start(bf16[2,2,84,128]{3,2,1,0:T(8,128)(2,1)S(1)} %get-tuple-element.22), channel_id=1, source_target_pairs={{0,4},{4,0},{8,12},{12,8},{16,20},{20,16},{24,28},{28,24},{1,5},{5... | collective-permute-start | bytes 258056 | tf_op jit(solution)/shard_map/ppermute | solution.py:301
  41.1 6.6 %collective-permute-start.25 = (bf16[128,256]{1,0:T(8,128)(2,1)S(1)}, bf16[128,256]{1,0:T(8,128)(2,1)S(1)}, u32[]{:S(2)}, u32[]{:S(2)}) collective-permute-start(bf16[128,256]{1,0:T(8,128)(2,1)S(1)} %fusion.19), channel_id=1, source_target_pairs={{0,8},{1,9},{2,10},{3,11},{4,12},{5,13},{6,14},{7,15},{8,0},{9,1},... | collective-permute-start | bytes 196616 | tf_op jit(solution)/shard_map/ppermute | solution.py:318
  45.6 6.5 %collective-permute-start.16 = (bf16[2,2,2,84,128]{4,3,2,1,0:T(8,128)(2,1)S(1)}, bf16[2,2,2,84,128]{4,3,2,1,0:T(8,128)(2,1)S(1)}, u32[]{:S(2)}, u32[]{:S(2)}) collective-permute-start(bf16[2,2,2,84,128]{4,3,2,1,0:T(8,128)(2,1)S(1)} %pad_maximum_fusion.1.refs_0_), channel_id=1, source_target_pairs={{0,2},{1,3},{2,0},{3,1},{4,6},{5,7},{6,4},{7,5},{8,10},{9,11},{10,... | collective-permute-start | bytes 516104 | tf_op jit(solution)/shard_map/ppermute | solution.py:301
  46.5 5.6 %collective-permute-start.20 = (bf16[2,2,84,128]{3,2,1,0:T(8,128)(2,1)S(1)}, bf16[2,2,84,128]{3,2,1,0:T(8,128)(2,1)S(1)}, u32[]{:S(2)}, u32[]{:S(2)}) collective-permute-start(bf16[2,2,84,128]{3,2,1,0:T(8,128)(2,1)S(1)} %collective-permute-done.18.refs_4_), channel_id=1, source_target_pairs={{0,2},{1,3},{2,0},{3,1},{4,6},{5,7},{6,4},{7,5},{8,10},{9,11},{10,... | collective-permute-start | bytes 258056 | tf_op jit(solution)/shard_map/ppermute | solution.py:301
  47.7 5.7 %collective-permute-start.26 = (bf16[128,256]{1,0:T(8,128)(2,1)S(1)}, bf16[128,256]{1,0:T(8,128)(2,1)S(1)}, u32[]{:S(2)}, u32[]{:S(2)}) collective-permute-start(bf16[128,256]{1,0:T(8,128)(2,1)S(1)} %fusion.21), channel_id=1, source_target_pairs={{0,16},{1,17},{2,18},{3,19},{4,20},{5,21},{6,22},{7,23},{8,24},{9,... | collective-permute-start | bytes 196616 | tf_op jit(solution)/shard_map/ppermute | solution.py:318
  49.0 4.6 %collective-permute-start.15 = (bf16[2,2,2,84,128]{4,3,2,1,0:T(8,128)(2,1)S(1)}, bf16[2,2,2,84,128]{4,3,2,1,0:T(8,128)(2,1)S(1)}, u32[]{:S(2)}, u32[]{:S(2)}) collective-permute-start(bf16[2,2,2,84,128]{4,3,2,1,0:T(8,128)(2,1)S(1)} %pad_maximum_fusion.1.refs_0_), channel_id=1, source_target_pairs={{0,1},{1,0},{2,3},{3,2},{4,5},{5,4},{6,7},{7,6},{8,9},{9,8},{10,11... | collective-permute-start | bytes 516104 | tf_op jit(solution)/shard_map/ppermute | solution.py:301
  49.0 4.5 %collective-permute-start.19 = (bf16[2,2,84,128]{3,2,1,0:T(8,128)(2,1)S(1)}, bf16[2,2,84,128]{3,2,1,0:T(8,128)(2,1)S(1)}, u32[]{:S(2)}, u32[]{:S(2)}) collective-permute-start(bf16[2,2,84,128]{3,2,1,0:T(8,128)(2,1)S(1)} %collective-permute-done.18.refs_4_), channel_id=1, source_target_pairs={{0,1},{1,0},{2,3},{3,2},{4,5},{5,4},{6,7},{7,6},{8,9},{9,8},{10,11... | collective-permute-start | bytes 258056 | tf_op jit(solution)/shard_map/ppermute | solution.py:301
  52.1 1.4 %collective-permute-start.21 = (bf16[2,2,84,128]{3,2,1,0:T(8,128)(2,1)S(1)}, bf16[2,2,84,128]{3,2,1,0:T(8,128)(2,1)S(1)}, u32[]{:S(2)}, u32[]{:S(2)}) collective-permute-start(bf16[2,2,84,128]{3,2,1,0:T(8,128)(2,1)S(1)} %collective-permute-done.20.refs_6_), channel_id=1, source_target_pairs={{0,1},{1,0},{2,3},{3,2},{4,5},{5,4},{6,7},{7,6},{8,9},{9,8},{10,11... | collective-permute-start | bytes 258056 | tf_op jit(solution)/shard_map/ppermute | solution.py:301
  52.1 1.6 %collective-permute-start.17 = (bf16[2,2,2,84,128]{4,3,2,1,0:T(8,128)(2,1)S(1)}, bf16[2,2,2,84,128]{4,3,2,1,0:T(8,128)(2,1)S(1)}, u32[]{:S(2)}, u32[]{:S(2)}) collective-permute-start(bf16[2,2,2,84,128]{4,3,2,1,0:T(8,128)(2,1)S(1)} %collective-permute-done.16.refs_2_), channel_id=1, source_target_pairs={{0,1},{1,0},{2,3},{3,2},{4,5},{5,4},{6,7},{7,6},{8,9},{9,8},{10,11... | collective-permute-start | bytes 516104 | tf_op jit(solution)/shard_map/ppermute | solution.py:301
  53.4 2.1 %collective-permute-start.27 = (bf16[128,256]{1,0:T(8,128)(2,1)S(1)}, bf16[128,256]{1,0:T(8,128)(2,1)S(1)}, u32[]{:S(2)}, u32[]{:S(2)}) collective-permute-start(bf16[128,256]{1,0:T(8,128)(2,1)S(1)} %get-tuple-element.31), channel_id=1, source_target_pairs={{0,1},{1,0},{2,3},{3,2},{4,5},{5,4},{6,7},{7,6},{8,9},{9,8},{10,11... | collective-permute-start | bytes 196616 | tf_op jit(solution)/shard_map/ppermute | solution.py:301
  54.6 0.9 %copy-start.1 = (f32[2,2,84,128]{3,1,2,0:T(2,128)S(1)}, f32[2,2,84,128]{3,1,2,0:T(2,128)}, u32[]{:S(2)}) copy-start(f32[2,2,84,128]{3,1,2,0:T(2,128)} %param.9) | copy-start | bytes 516100
  56.2 1.3 %collective-permute-start.28 = (f32[16,128]{1,0:T(8,128)S(1)}, f32[16,128]{1,0:T(8,128)S(1)}, u32[]{:S(2)}, u32[]{:S(2)}) collective-permute-start(f32[16,128]{1,0:T(8,128)S(1)} %get-tuple-element.26), channel_id=1, source_target_pairs={{0,1},{1,0},{2,3},{3,2},{4,5},{5,4},{6,7},{7,6},{8,9},{9,8},{10,11... | collective-permute-start | bytes 24584 | tf_op jit(solution)/shard_map/ppermute | solution.py:301
  57.4 3.7 %collective-permute-start.29 = (f32[16,128]{1,0:T(8,128)S(1)}, f32[16,128]{1,0:T(8,128)S(1)}, u32[]{:S(2)}, u32[]{:S(2)}) collective-permute-start(f32[16,128]{1,0:T(8,128)S(1)} %add.55), channel_id=1, source_target_pairs={{0,2},{1,3},{2,0},{3,1},{4,6},{5,7},{6,4},{7,5},{8,10},{9,11},{10,... | collective-permute-start | bytes 24584 | tf_op jit(solution)/shard_map/ppermute | solution.py:301
  61.1 3.7 %collective-permute-start.30 = (f32[16,128]{1,0:T(8,128)S(1)}, f32[16,128]{1,0:T(8,128)S(1)}, u32[]{:S(2)}, u32[]{:S(2)}) collective-permute-start(f32[16,128]{1,0:T(8,128)S(1)} %add.56), channel_id=1, source_target_pairs={{0,4},{4,0},{8,12},{12,8},{16,20},{20,16},{24,28},{28,24},{1,5},{5... | collective-permute-start | bytes 24584 | tf_op jit(solution)/shard_map/ppermute | solution.py:301
  64.7 3.7 %collective-permute-start.31 = (f32[16,128]{1,0:T(8,128)S(1)}, f32[16,128]{1,0:T(8,128)S(1)}, u32[]{:S(2)}, u32[]{:S(2)}) collective-permute-start(f32[16,128]{1,0:T(8,128)S(1)} %add.57), channel_id=1, source_target_pairs={{0,8},{4,12},{8,0},{12,4},{16,24},{20,28},{24,16},{28,20},{1,9},{5... | collective-permute-start | bytes 24584 | tf_op jit(solution)/shard_map/ppermute | solution.py:301
  68.4 4.6 %collective-permute-start.32 = (f32[16,128]{1,0:T(8,128)S(1)}, f32[16,128]{1,0:T(8,128)S(1)}, u32[]{:S(2)}, u32[]{:S(2)}) collective-permute-start(f32[16,128]{1,0:T(8,128)S(1)} %add.58), channel_id=1, source_target_pairs={{0,16},{4,20},{8,24},{12,28},{16,0},{20,4},{24,8},{28,12},{1,17},{... | collective-permute-start | bytes 24584 | tf_op jit(solution)/shard_map/ppermute | solution.py:301

commit v4 on v3

--- a/solution.py
+++ b/solution.py
@@ -73,15 +73,10 @@
     copies = [pltpu.make_async_copy(*move, sems.at[i]) for i, move in enumerate(moves)]
     for copy in copies:
         copy.start()
-    for copy in copies:
+    for copy in copies[:-2]:
         copy.wait()
     spheres, _, count, _ = round_ref.shape
     b = lax.axis_index("blk")
-    for a in range(2):
-        part = plane_ref[a, 0:count, :]
-        for p in range(1, plane_ref.shape[1] // count):
-            part = jnp.where(b == p, plane_ref[a, p * count : (p + 1) * count, :], part)
-        part_ref[a] = part
     turns = None
     for d in range(3):
         term = wave_ref[d : d + 1, :].astype(f32) * pos_ref[:, d : d + 1]
@@ -98,6 +93,13 @@
             held[at : at + 1, 0:count] = mie_ref[s, z : z + 1, :]
     columns = held[...].T
     column_ref[...] = columns
+    copies[-2].wait()
+    for a in range(2):
+        part = plane_ref[a, 0:count, :]
+        for p in range(1, plane_ref.shape[1] // count):
+            part = jnp.where(b == p, plane_ref[a, p * count : (p + 1) * count, :], part)
+        part_ref[a] = part
+    copies[-1].wait()
     field = []
     for s in range(spheres):
         field.append([x_ref[s, pl.ds(z, count, stride=2), :].astype(bf16) for z in range(2)])
@@ -144,9 +146,12 @@
             out_ref[i, k] = held[slot * spheres + member_ref[i, k]]
 
 
-def far_field(total, plane_ref, columns, spheres):
-    total_re, total_im = total
-    n = total_re.shape[1]
+def far_half(sums_ref, upper, columns_ref, plane_ref, spheres):
+    half, n = sums_ref.shape[0], sums_ref.shape[1] // 2
+    rows = pl.ds(pl.multiple_of(upper * half, half), half)
+    total_re, total_im = sums_ref[:, :n].astype(f32), sums_ref[:, n:].astype(f32)
+    plane_re, plane_im = plane_ref[0, :, rows], plane_ref[1, :, rows]
+    columns = columns_ref[rows, :]
     fields = []
     for s in range(spheres):
         at = 2 * spheres + s
@@ -154,36 +159,34 @@
         turned = jnp.concatenate(
             [c * total_re - d * total_im, c * total_im + d * total_re], axis=1
         ).astype(bf16)
-        with_re = jnp.dot(plane_ref[0], turned, preferred_element_type=f32)
-        with_im = jnp.dot(plane_ref[1], turned, preferred_element_type=f32)
+        with_re = jnp.dot(plane_re, turned, preferred_element_type=f32)
+        with_im = jnp.dot(plane_im, turned, preferred_element_type=f32)
         fields.append(
             (with_re[:, :n] + with_im[:, n:], with_re[:, n:] - with_im[:, :n])
         )
     return fields
 
 
-def join_halves(mine_ref, other_ref):
-    odd = lax.rem(lax.axis_index("blk"), 2) == 1
-    n = mine_ref.shape[1] // 2
-    out = []
-    for z in range(2):
-        at = slice(z * n, (z + 1) * n)
-        mine, other = mine_ref[:, at], other_ref[:, at].astype(f32)
-        out.append(
-            jnp.concatenate([jnp.where(odd, other, mine), jnp.where(odd, mine, other)], axis=0)
-        )
-    return out
-
-
-def image_fields(near_ref, mine_ref, other_ref, column_ref, plane_ref):
-    spheres, pairs, _, _, count, _ = near_ref.shape
-    far = far_field(join_halves(mine_ref, other_ref), plane_ref, column_ref[...], spheres)
-    out = []
+def field_sum_body(near_ref, mine_ref, column_ref, plane_ref, out_ref):
+    spheres, pairs = near_ref.shape[:2]
+    odd = lax.rem(lax.axis_index("blk"), 2)
+    far = far_half(mine_ref, odd, column_ref, plane_ref, spheres)
     for s in range(spheres):
         sum_re, sum_im = far[s]
         for k in range(pairs):
             sum_re = sum_re + (near_ref[s, k, 0, 0] - near_ref[s, k, 1, 1])
             sum_im = sum_im + (near_ref[s, k, 0, 1] + near_ref[s, k, 1, 0])
+        out_ref[s, 0] = sum_re
+        out_ref[s, 1] = sum_im
+
+
+def image_fields(sum_ref, other_ref, column_ref, plane_ref):
+    spheres, _, count, _ = sum_ref.shape
+    odd = lax.rem(lax.axis_index("blk"), 2)
+    far = far_half(other_ref, 1 - odd, column_ref, plane_ref, spheres)
+    out = []
+    for s in range(spheres):
+        sum_re, sum_im = sum_ref[s, 0] + far[s][0], sum_ref[s, 1] + far[s][1]
         at = 4 * spheres + 2 * s
         m_re = column_ref[0:count, at : at + 1]
         m_im = column_ref[0:count, at + 1 : at + 2]
@@ -192,10 +195,10 @@
 
 
 def first_image_body(
-    near_ref, mine_ref, other_ref, column_ref, plane_ref,
+    sum_ref, other_ref, column_ref, plane_ref,
     image_ref, round_ref, send_ref, keep_ref,
 ):
-    images = image_fields(near_ref, mine_ref, other_ref, column_ref, plane_ref)
+    images = image_fields(sum_ref, other_ref, column_ref, plane_ref)
     field = []
     for s, (re, im) in enumerate(images):
         image_ref[s, 0] = re
@@ -208,9 +211,9 @@
 
 
 def second_image_body(
-    near_ref, mine_ref, other_ref, column_ref, plane_ref, x_ref, g_ref, image_ref, gram_ref,
+    sum_ref, other_ref, column_ref, plane_ref, x_ref, g_ref, image_ref, gram_ref,
 ):
-    images = image_fields(near_ref, mine_ref, other_ref, column_ref, plane_ref)
+    images = image_fields(sum_ref, other_ref, column_ref, plane_ref)
     count = g_ref.shape[2]
     sums = None
     for s, (re, im) in enumerate(images):
@@ -227,9 +230,11 @@
         terms += [h[0] * h[0] + h[1] * h[1]]
         rows = [jnp.sum(term, axis=0, keepdims=True) for term in terms]
         sums = rows if sums is None else [a + r for a, r in zip(sums, rows)]
-    gram_ref[...] = jnp.zeros_like(gram_ref)
-    for i, row in enumerate(sums):
-        gram_ref[i : i + 1, :] = row
+    high = [row.astype(bf16).astype(f32) for row in sums]
+    low = [row - part for row, part in zip(sums, high)]
+    rest = jnp.zeros((gram_ref.shape[1] - 2 * len(sums), gram_ref.shape[2]), f32)
+    both = jnp.concatenate(high + low + [rest], axis=0).astype(bf16)
+    gram_ref[...] = jnp.broadcast_to(both[None], gram_ref.shape)
 
 
 def times(a, b):
@@ -249,8 +254,8 @@
 
 
 def finish_body(entries, gram_ref, x_ref, g_ref, h_ref, basis_ref, residual_ref, hess_ref):
-    gram = gram_ref[...] / entries
-    row = [gram[i : i + 1, :] for i in range(9)]
+    gram = jnp.sum(gram_ref[...].astype(f32), axis=0) / entries
+    row = [gram[i : i + 1, :] + gram[9 + i : 10 + i, :] for i in range(9)]
     xx, gg, hh = row[0], row[3], row[8]
     xg, xh, gh = (row[1], row[2]), (row[4], row[5]), (row[6], row[7])
     square = xx + epsilon
@@ -309,15 +314,6 @@
     return lax.ppermute(value, "slab", pairs)
 
 
-def trade_mixed(value, even, odd):
-    blocks = lax.axis_size("blk")
-    pairs = []
-    for i in range(blocks * lax.axis_size("slab")):
-        axis, bit = odd if i % 2 else even
-        pairs.append((i, i ^ (bit if axis == "blk" else bit * blocks)))
-    return lax.ppermute(value, ("slab", "blk"), pairs)
-
-
 def bits(axis, start=1):
     out, bit = [], start
     while bit < lax.axis_size(axis):
@@ -343,17 +339,10 @@
 def total_sums(send, keep):
     keep = keep + trade(send, "blk", 1).astype(f32)
     steps = [("blk", bit) for bit in bits("blk", 2)] + [("slab", bit) for bit in bits("slab")]
-    crossed = steps[1::-1] + steps[2:] if len(steps) > 1 else steps
-    for even, odd in zip(steps, crossed):
-        keep = keep + trade_mixed(keep.astype(bf16), even, odd).astype(f32)
+    steps[1:3] = steps[2:0:-1]
+    for axis, bit in steps:
+        keep = keep + trade(keep.astype(bf16), axis, bit).astype(f32)
     return keep, trade(keep.astype(bf16), "blk", 1)
-
-
-def total_gram(gram):
-    for axis in ("blk", "slab"):
-        for bit in bits(axis):
-            gram = gram + trade(gram, axis, bit)
-    return gram
 
 
 def per_device(
@@ -392,23 +381,28 @@
             "ikarc,ikzcn->ikazrn", translation, gathered, preferred_element_type=f32
         )
 
+    def both_fields(own, send, keep, columns, plane):
+        mine, other = total_sums(send, keep)
+        near = near_products(own)
+        field_sums = call(field_sum_body, field, [VM] * 4)(near, mine, columns, plane)
+        return field_sums, other
+
     operands = (x, plane, wave_index.T, positions, ewald_weight.reshape(1, waves), mie_coef)
     buffers = [pltpu.VMEM(v.shape, v.dtype) for v in operands]
     buffers += [pltpu.VMEM((held_rows, waves), f32), pltpu.SemaphoreType.DMA((len(operands),))]
     rounded, send, keep, columns, plane = call(
         first_sums_body, (field_half, sums_half, sums, column, part), [HB] * len(operands), buffers
     )(*in_hbm(operands))
-    mine, other = total_sums(send, keep)
-    near = near_products(rounded)
+    field_sums, other = both_fields(rounded, send, keep, columns, plane)
     image, image_rounded, send, keep = call(
-        first_image_body, (field, field_half, sums_half, sums), [VM] * 5
-    )(near, mine, other, columns, plane)
-    mine, other = total_sums(send, keep)
-    near = near_products(image_rounded)
-    image_two, gram = call(second_image_body, (field, shape((16, n))), [VM] * 7)(
-        near, mine, other, columns, plane, x, image
-    )
-    gram = total_gram(gram)
+        first_image_body, (field, field_half, sums_half, sums), [VM] * 4
+    )(field_sums, other, columns, plane)
+    field_sums, other = both_fields(image_rounded, send, keep, columns, plane)
+    devices = blocks * lax.axis_size("slab")
+    image_two, gram = call(
+        second_image_body, (field, shape((devices, 24, n), bf16)), [VM] * 6
+    )(field_sums, other, columns, plane, x, image)
+    gram = lax.all_to_all(gram, ("slab", "blk"), 0, 0, tiled=True)
     flat = shape((spheres, 2 * count, n))
     basis, residual, hessenberg = call(
         lambda *refs: finish_body(float(entries), *refs), (flat, flat, shape((9, n))), [VM] * 4

time: 74 us -> 70.2 us (0.949)
  blocking collectives: 0 us -> 12.4 us
  waiting for transfers between devices: 33.6 us -> 24.5 us
  starting transfers between devices: 31.4 us -> 23.5 us
    all_to_all x0 -> x1, blocking collectives: none -> 12.4 us  [per_device(): gram = lax.all_to_all(gram, ('slab', 'blk'), 0, 0, tiled=True)]
    ppermute x8 -> x0, starting transfers between devices: 12.3 us -> none  [trade_mixed(): return lax.ppermute(value, ('slab', 'blk'), pairs)]
    ppermute x8 -> x0, waiting for transfers between devices: 6.37 us -> none  [trade_mixed(): return lax.ppermute(value, ('slab', 'blk'), pairs)]
    ppermute x23 -> x26, starting transfers between devices: 11.4 us -> 17.5 us  [trade(): lax.ppermute(value, axis, [(i, i ^ bit) for i in range(lax.axis_size(axis...]
    ppermute x23 -> x26, waiting for transfers between devices: 27.2 us -> 24.5 us  [trade(): lax.ppermute(value, axis, [(i, i ^ bit) for i in range(lax.axis_size(axis...]
    ppermute x2, starting transfers between devices: 7.69 us -> 6.03 us  [trade_odd(): return lax.ppermute(value, 'slab', pairs)]
    pallas_call x2 -> x4, Pallas kernels: 1.36 us -> 1.84 us  [the longest x2 0.86 us: both_fields(): call(field_sum_body, field, [VM] * 4)(near, mine, columns, plane)]
  transfers between devices with their start and end apart: 33 -> 28, of which waited for: 18 -> 15; matrix products, arithmetic and copies ran while one was open for 3% -> 3% of each run, Pallas kernels for 2% -> 4%
where the time goes in v4:
time: 70.2 us; the launch traced here: 70 us
  waiting for transfers between devices  24.5 us (35%)
  starting transfers between devices  23.5 us (33%)
  blocking collectives  12.4 us (18%)
  Pallas kernels  6.22 us (9%)
  matrix products  1.83 us (3%)
  between operations  0.86 us (1%)
    ppermute x26, waiting for transfers between devices, trade(): lax.ppermute(value, axis, [(i, i ^ bit) for i in range(lax.axis_size(axis...  24.5 us
    ppermute x26, starting transfers between devices, trade(): lax.ppermute(value, axis, [(i, i ^ bit) for i in range(lax.axis_size(axis...  17.5 us
    all_to_all x1, blocking collectives, per_device(): gram = lax.all_to_all(gram, ('slab', 'blk'), 0, 0, tiled=True)  12.4 us
    ppermute x2, starting transfers between devices, trade_odd(): return lax.ppermute(value, 'slab', pairs)  6.03 us
    dot_general x2, matrix products, near_work(): jnp.einsum('ikarc,ikzcn->ikazrn', translation, gathered, preferred_elemen...  1.83 us
    pallas_call x2, Pallas kernels, near_work(): call(gather_body, sources, [HB, HB] + [VM] * (2 * blocks), buffers)  1.82 us
    pallas_call x1, Pallas kernels, per_device(): call(first_sums_body, (field_half, sums_half, sums, column, part), [HB] *...  1.66 us
  transfers between devices with their start and end apart: 28, of which 15 were waited for; matrix products, arithmetic and copies ran while one was open for 3% of the time, Pallas kernels for 4%

profile of v4, /device:TPU:0, one launch (start us, length us, event | category | flops | bytes accessed | tf_op | source)
XLA Modules:
  0.0 70.0 jit_solution(18223433477298178283)
XLA Ops:
  0.6 0.0 copy-start
  0.6 1.7 %shard_map.112 = (bf16[2,2,84,128]{3,2,1,0:T(8,128)(2,1)S(1)}, bf16[128,256]{1,0:T(8,128)(2,1)S(1)}, f32[128,256]{1,0:T(8,128)S(1)}, f32[256,16]{1,0:T(8,128)S(1)}, bf16[2,84,256]{2,1,0:T(8,128)(2,1)S(1)}) custom-call(f32[2,168,128]{2,1,0:T(8,128)} %bitcast.38, bf16[2,336,256]{2,1,0:T(8,128)(2,1)} %bitcast.43, s32[3,256]{1,0:T(4,128)} %bitcast.46, ...), custom_call_target="tpu_custom_call" | custom-call | tf_op jit(solution)/shard_map/pallas_call | solution.py:393
  2.3 0.6 collective-permute-start.8
  2.9 0.9 %collective-permute-done.8 = bf16[128,256]{1,0:T(8,128)(2,1)S(1)} collective-permute-done((bf16[128,256]{1,0:T(8,128)(2,1)S(1)}, bf16[128,256]{1,0:T(8,128)(2,1)S(1)}, u32[]{:S(2)}, u32[]{:S(2)}) %collective-permute-start.8) | collective-permute-done | bytes 65568 | tf_op jit(solution)/shard_map/ppermute | solution.py:306
  3.8 2.9 %collective-permute-start.9 = (bf16[128,256]{1,0:T(8,128)(2,1)S(1)}, bf16[128,256]{1,0:T(8,128)(2,1)S(1)}, u32[]{:S(2)}, u32[]{:S(2)}) collective-permute-start(bf16[128,256]{1,0:T(8,128)(2,1)S(1)} %fusion.16), channel_id=1, source_target_pairs={{0,2},{1,3},{2,0},{3,1},{4,6},{5,7},{6,4},{7,5},{8,10},{9,11},{10,... | collective-permute-start | bytes 196616 | tf_op jit(solution)/shard_map/ppermute | solution.py:306
  6.7 2.4 %collective-permute-done.9 = bf16[128,256]{1,0:T(8,128)(2,1)S(1)} collective-permute-done((bf16[128,256]{1,0:T(8,128)(2,1)S(1)}, bf16[128,256]{1,0:T(8,128)(2,1)S(1)}, u32[]{:S(2)}, u32[]{:S(2)}) %collective-permute-start.9) | collective-permute-done | bytes 65568 | tf_op jit(solution)/shard_map/ppermute | solution.py:306
  9.2 2.0 %collective-permute-start.10 = (bf16[128,256]{1,0:T(8,128)(2,1)S(1)}, bf16[128,256]{1,0:T(8,128)(2,1)S(1)}, u32[]{:S(2)}, u32[]{:S(2)}) collective-permute-start(bf16[128,256]{1,0:T(8,128)(2,1)S(1)} %get-tuple-element.37), channel_id=1, source_target_pairs={{0,8},{4,12},{8,0},{12,4},{16,24},{20,28},{24,16},{28,20},{1,9},{5... | collective-permute-start | bytes 196616 | tf_op jit(solution)/shard_map/ppermute | solution.py:306
  11.1 3.4 %collective-permute-start.4 = (bf16[2,2,84,128]{3,2,1,0:T(8,128)(2,1)S(1)}, bf16[2,2,84,128]{3,2,1,0:T(8,128)(2,1)S(1)}, u32[]{:S(2)}, u32[]{:S(2)}) collective-permute-start(bf16[2,2,84,128]{3,2,1,0:T(8,128)(2,1)S(1)} %get-tuple-element.17), channel_id=1, source_target_pairs={{0,28},{4,8},{8,4},{12,16},{16,12},{20,24},{24,20},{28,0},{1,29},{... | collective-permute-start | bytes 258056 | tf_op jit(solution)/shard_map/ppermute | solution.py:314
  14.5 0.0 collective-permute-start
  14.5 0.0 collective-permute-done.10
  14.6 2.1 %collective-permute-start.11 = (bf16[128,256]{1,0:T(8,128)(2,1)S(1)}, bf16[128,256]{1,0:T(8,128)(2,1)S(1)}, u32[]{:S(2)}, u32[]{:S(2)}) collective-permute-start(bf16[128,256]{1,0:T(8,128)(2,1)S(1)} %fusion.17), channel_id=1, source_target_pairs={{0,4},{4,0},{8,12},{12,8},{16,20},{20,16},{24,28},{28,24},{1,5},{5... | collective-permute-start | bytes 196616 | tf_op jit(solution)/shard_map/ppermute | solution.py:306
  16.7 3.1 %collective-permute-done = bf16[2,2,84,128]{3,2,1,0:T(8,128)(2,1)S(1)} collective-permute-done((bf16[2,2,84,128]{3,2,1,0:T(8,128)(2,1)S(1)}, bf16[2,2,84,128]{3,2,1,0:T(8,128)(2,1)S(1)}, u32[]{:S(2)}, u32[]{:S(2)}) %collective-permute-start) | collective-permute-done | bytes 86048 | tf_op jit(solution)/shard_map/ppermute | solution.py:306
  19.7 1.6 %collective-permute-start.2 = (bf16[2,2,2,84,128]{4,3,2,1,0:T(8,128)(2,1)S(1)}, bf16[2,2,2,84,128]{4,3,2,1,0:T(8,128)(2,1)S(1)}, u32[]{:S(2)}, u32[]{:S(2)}) collective-permute-start(bf16[2,2,2,84,128]{4,3,2,1,0:T(8,128)(2,1)S(1)} %pad_maximum_fusion.refs_0_), channel_id=1, source_target_pairs={{0,2},{1,3},{2,0},{3,1},{4,6},{5,7},{6,4},{7,5},{8,10},{9,11},{10,... | collective-permute-start | bytes 516104 | tf_op jit(solution)/shard_map/ppermute | solution.py:306
  21.3 0.0 collective-permute-done.4.refs_4_
  21.3 0.5 collective-permute-start.6
  21.8 0.0 collective-permute-done.11
  21.9 0.1 collective-permute-start.12
  22.0 0.1 collective-permute-start.1
  22.0 0.5 collective-permute-start.5
  22.5 3.7 %collective-permute-done.6.refs_6_ = bf16[2,2,84,128]{3,2,1,0:T(8,128)(2,1)S(1)} collective-permute-done((bf16[2,2,84,128]{3,2,1,0:T(8,128)(2,1)S(1)}, bf16[2,2,84,128]{3,2,1,0:T(8,128)(2,1)S(1)}, u32[]{:S(2)}, u32[]{:S(2)}) %collective-permute-start.6) | collective-permute-done | bytes 86048 | tf_op jit(solution)/shard_map/ppermute | solution.py:306
  26.3 0.0 collective-permute-start.7
  26.3 0.0 collective-permute-done.2.refs_2_
  26.3 0.5 collective-permute-start.3
  26.8 0.3 collective-permute-done.12
  27.1 0.1 collective-permute-start.13
  27.2 0.0 collective-permute-done.5.refs_5_
  27.2 0.3 collective-permute-done.7.refs_7_
  27.6 0.0 collective-permute-done.1.refs_1_
  27.6 0.3 collective-permute-done.3.refs_3_
  27.8 0.9 %shard_map.113 = bf16[2,8,2,336,128]{4,3,2,1,0:T(8,128)(2,1)S(1)} custom-call(s32[2,8]{1,0:T(2,128)} %shift_hbm.3, s32[2,8]{1,0:T(2,128)} %member_hbm.3, bf16[2,2,2,84,128]{4,3,2,1,0:T(8,128)(2,1)S(1)} %pad_maximum_fusion.refs_0_, bf16[2,2,2,84,128]{4,3,2,1,0:T(8,128)(2,1)S(1)} %collective-permute-done.1.refs_1_, ...), custom_call_target="tpu_custom_call" | custom-call | tf_op jit(solution)/shard_map/pallas_call | solution.py:377
  28.8 0.9 %fusion.6.near_ref = f32[2,8,2,2,84,128]{5,4,3,2,1,0:T(8,128)S(1)} fusion(bf16[2,8,2,84,336,1]{4,2,3,1,0,5:T(2,128)(2,1)S(1)} %bitcast.36, bf16[2,8,2,336,128]{4,3,2,1,0:T(8,128)(2,1)S(1)} %shard_map.113), kind=kOutput, calls=%fused_computation.6 | convolution fusion | flops 462422016 | bytes 7311360 | tf_op jit(solution)/shard_map/ikarc,ikzcn->ikazrn/dot_general | solution.py:380
  29.7 0.4 shard_map.114.sum_ref
  30.1 0.0 collective-permute-done.13.other_ref
  30.1 0.6 shard_map.115
  30.7 0.4 collective-permute-start.22
  31.2 0.9 %collective-permute-done.22 = bf16[128,256]{1,0:T(8,128)(2,1)S(1)} collective-permute-done((bf16[128,256]{1,0:T(8,128)(2,1)S(1)}, bf16[128,256]{1,0:T(8,128)(2,1)S(1)}, u32[]{:S(2)}, u32[]{:S(2)}) %collective-permute-start.22) | collective-permute-done | bytes 65568 | tf_op jit(solution)/shard_map/ppermute | solution.py:306
  32.1 1.6 %collective-permute-start.23 = (bf16[128,256]{1,0:T(8,128)(2,1)S(1)}, bf16[128,256]{1,0:T(8,128)(2,1)S(1)}, u32[]{:S(2)}, u32[]{:S(2)}) collective-permute-start(bf16[128,256]{1,0:T(8,128)(2,1)S(1)} %fusion.18), channel_id=1, source_target_pairs={{0,2},{1,3},{2,0},{3,1},{4,6},{5,7},{6,4},{7,5},{8,10},{9,11},{10,... | collective-permute-start | bytes 196616 | tf_op jit(solution)/shard_map/ppermute | solution.py:306
  33.7 2.8 %collective-permute-done.23 = bf16[128,256]{1,0:T(8,128)(2,1)S(1)} collective-permute-done((bf16[128,256]{1,0:T(8,128)(2,1)S(1)}, bf16[128,256]{1,0:T(8,128)(2,1)S(1)}, u32[]{:S(2)}, u32[]{:S(2)}) %collective-permute-start.23) | collective-permute-done | bytes 65568 | tf_op jit(solution)/shard_map/ppermute | solution.py:306
  36.5 0.1 collective-permute-start.24
  36.6 2.6 %collective-permute-start.18 = (bf16[2,2,84,128]{3,2,1,0:T(8,128)(2,1)S(1)}, bf16[2,2,84,128]{3,2,1,0:T(8,128)(2,1)S(1)}, u32[]{:S(2)}, u32[]{:S(2)}) collective-permute-start(bf16[2,2,84,128]{3,2,1,0:T(8,128)(2,1)S(1)} %get-tuple-element.22), channel_id=1, source_target_pairs={{0,28},{4,8},{8,4},{12,16},{16,12},{20,24},{24,20},{28,0},{1,29},{... | collective-permute-start | bytes 258056 | tf_op jit(solution)/shard_map/ppermute | solution.py:314
  39.2 0.8 %collective-permute-start.14 = (bf16[2,2,84,128]{3,2,1,0:T(8,128)(2,1)S(1)}, bf16[2,2,84,128]{3,2,1,0:T(8,128)(2,1)S(1)}, u32[]{:S(2)}, u32[]{:S(2)}) collective-permute-start(bf16[2,2,84,128]{3,2,1,0:T(8,128)(2,1)S(1)} %get-tuple-element.22), channel_id=1, source_target_pairs={{0,4},{4,0},{8,12},{12,8},{16,20},{20,16},{24,28},{28,24},{1,5},{5... | collective-permute-start | bytes 258056 | tf_op jit(solution)/shard_map/ppermute | solution.py:306
  40.1 1.0 %collective-permute-done.24 = bf16[128,256]{1,0:T(8,128)(2,1)S(1)} collective-permute-done((bf16[128,256]{1,0:T(8,128)(2,1)S(1)}, bf16[128,256]{1,0:T(8,128)(2,1)S(1)}, u32[]{:S(2)}, u32[]{:S(2)}) %collective-permute-start.24) | collective-permute-done | bytes 65568 | tf_op jit(solution)/shard_map/ppermute | solution.py:306
  41.1 0.3 collective-permute-start.25
  41.3 4.1 %collective-permute-done.14 = bf16[2,2,84,128]{3,2,1,0:T(8,128)(2,1)S(1)} collective-permute-done((bf16[2,2,84,128]{3,2,1,0:T(8,128)(2,1)S(1)}, bf16[2,2,84,128]{3,2,1,0:T(8,128)(2,1)S(1)}, u32[]{:S(2)}, u32[]{:S(2)}) %collective-permute-start.14) | collective-permute-done | bytes 86048 | tf_op jit(solution)/shard_map/ppermute | solution.py:306
  45.5 1.6 %collective-permute-start.16 = (bf16[2,2,2,84,128]{4,3,2,1,0:T(8,128)(2,1)S(1)}, bf16[2,2,2,84,128]{4,3,2,1,0:T(8,128)(2,1)S(1)}, u32[]{:S(2)}, u32[]{:S(2)}) collective-permute-start(bf16[2,2,2,84,128]{4,3,2,1,0:T(8,128)(2,1)S(1)} %pad_maximum_fusion.1.refs_0_), channel_id=1, source_target_pairs={{0,2},{1,3},{2,0},{3,1},{4,6},{5,7},{6,4},{7,5},{8,10},{9,11},{10,... | collective-permute-start | bytes 516104 | tf_op jit(solution)/shard_map/ppermute | solution.py:306
  47.1 0.0 collective-permute-done.18.refs_4_
  47.1 0.5 collective-permute-start.20
  47.6 0.0 collective-permute-done.25
  47.6 0.2 collective-permute-start.26
  47.9 0.5 collective-permute-start.19
  48.4 3.6 %collective-permute-done.20.refs_6_ = bf16[2,2,84,128]{3,2,1,0:T(8,128)(2,1)S(1)} collective-permute-done((bf16[2,2,84,128]{3,2,1,0:T(8,128)(2,1)S(1)}, bf16[2,2,84,128]{3,2,1,0:T(8,128)(2,1)S(1)}, u32[]{:S(2)}, u32[]{:S(2)}) %collective-permute-start.20) | collective-permute-done | bytes 86048 | tf_op jit(solution)/shard_map/ppermute | solution.py:306
  52.0 0.5 collective-permute-start.17
  52.5 0.3 collective-permute-done.26
  52.9 0.1 collective-permute-start.27
  53.0 0.3 collective-permute-done.21.refs_7_
  53.3 0.3 collective-permute-done.17.refs_3_
  53.6 0.9 %shard_map.116 = bf16[2,8,2,336,128]{4,3,2,1,0:T(8,128)(2,1)S(1)} custom-call(s32[2,8]{1,0:T(2,128)} %shift_hbm.3, s32[2,8]{1,0:T(2,128)} %member_hbm.3, bf16[2,2,2,84,128]{4,3,2,1,0:T(8,128)(2,1)S(1)} %pad_maximum_fusion.1.refs_0_, bf16[2,2,2,84,128]{4,3,2,1,0:T(8,128)(2,1)S(1)} %collective-permute-done.15.refs_1_, ...), custom_call_target="tpu_custom_call" | custom-call | tf_op jit(solution)/shard_map/pallas_call | solution.py:377
  54.5 0.9 %fusion.11.near_ref = f32[2,8,2,2,84,128]{5,4,3,2,1,0:T(8,128)S(1)} fusion(bf16[2,8,2,84,336,1]{4,2,3,1,0,5:T(2,128)(2,1)S(1)} %bitcast.37, bf16[2,8,2,336,128]{4,3,2,1,0:T(8,128)(2,1)S(1)} %shard_map.116), kind=kOutput, calls=%fused_computation.7 | convolution fusion | flops 462422016 | bytes 7311360 | tf_op jit(solution)/shard_map/ikarc,ikzcn->ikazrn/dot_general | solution.py:380
  55.4 0.0 copy-start.1
  55.4 0.4 shard_map.117.sum_ref
  55.9 0.5 copy-done.1
  56.3 0.4 shard_map.118
  56.8 12.4 %all_to_all.5.refs_0_ = bf16[32,24,128]{2,1,0:T(8,128)(2,1)S(1)} all-to-all(bf16[32,24,128]{2,1,0:T(8,128)(2,1)S(1)} %get-tuple-element.26), channel_id=1, replica_groups=mesh['slab'=8,'blk'=4] {'slab','blk'}, dimensions={0} | all-to-all | bytes 393216 | tf_op jit(solution)/shard_map/all_to_all | solution.py:405
  69.1 0.9 %shard_map.119 = (f32[2,168,128]{2,1,0:T(8,128)}, f32[2,168,128]{2,1,0:T(8,128)}, f32[9,128]{1,0:T(8,128)}) custom-call(bf16[32,24,128]{2,1,0:T(8,128)(2,1)S(1)} %all_to_all.5.refs_0_, f32[2,168,128]{2,1,0:T(8,128)S(1)} %bitcast.40, f32[2,2,84,128]{3,2,1,0:T(8,128)S(1)} %get-tuple-element.25.g_ref.refs_2_, f32[2,2,84,128]{3,2,1,0:T(8,128)S(1)} %get-tuple-element.27.refs_3_), custom_call_target="tpu_custom_call" | custom-call | tf_op jit(solution)/shard_map/pallas_call | solution.py:407
  (19 shorter events, 0.3 us)
Async XLA Ops:
  0.6 28.1 %copy-start = (bf16[2,8,2,84,336]{4,2,3,1,0:T(2,128)(2,1)S(1)}, bf16[2,8,2,84,336]{4,2,3,1,0:T(2,128)(2,1)}, u32[]{:S(2)}) copy-start(bf16[2,8,2,84,336]{4,2,3,1,0:T(2,128)(2,1)} %param.11) | copy-start | bytes 5419012
  2.3 1.5 %collective-permute-start.8 = (bf16[128,256]{1,0:T(8,128)(2,1)S(1)}, bf16[128,256]{1,0:T(8,128)(2,1)S(1)}, u32[]{:S(2)}, u32[]{:S(2)}) collective-permute-start(bf16[128,256]{1,0:T(8,128)(2,1)S(1)} %get-tuple-element.19), channel_id=1, source_target_pairs={{0,1},{1,0},{2,3},{3,2},{4,5},{5,4},{6,7},{7,6},{8,9},{9,8},{10,11... | collective-permute-start | bytes 196616 | tf_op jit(solution)/shard_map/ppermute | solution.py:306
  3.8 5.3 %collective-permute-start.9 = (bf16[128,256]{1,0:T(8,128)(2,1)S(1)}, bf16[128,256]{1,0:T(8,128)(2,1)S(1)}, u32[]{:S(2)}, u32[]{:S(2)}) collective-permute-start(bf16[128,256]{1,0:T(8,128)(2,1)S(1)} %fusion.16), channel_id=1, source_target_pairs={{0,2},{1,3},{2,0},{3,1},{4,6},{5,7},{6,4},{7,5},{8,10},{9,11},{10,... | collective-permute-start | bytes 196616 | tf_op jit(solution)/shard_map/ppermute | solution.py:306
  9.2 5.4 %collective-permute-start.10 = (bf16[128,256]{1,0:T(8,128)(2,1)S(1)}, bf16[128,256]{1,0:T(8,128)(2,1)S(1)}, u32[]{:S(2)}, u32[]{:S(2)}) collective-permute-start(bf16[128,256]{1,0:T(8,128)(2,1)S(1)} %get-tuple-element.37), channel_id=1, source_target_pairs={{0,8},{4,12},{8,0},{12,4},{16,24},{20,28},{24,16},{28,20},{1,9},{5... | collective-permute-start | bytes 196616 | tf_op jit(solution)/shard_map/ppermute | solution.py:306
  11.1 10.2 %collective-permute-start.4 = (bf16[2,2,84,128]{3,2,1,0:T(8,128)(2,1)S(1)}, bf16[2,2,84,128]{3,2,1,0:T(8,128)(2,1)S(1)}, u32[]{:S(2)}, u32[]{:S(2)}) collective-permute-start(bf16[2,2,84,128]{3,2,1,0:T(8,128)(2,1)S(1)} %get-tuple-element.17), channel_id=1, source_target_pairs={{0,28},{4,8},{8,4},{12,16},{16,12},{20,24},{24,20},{28,0},{1,29},{... | collective-permute-start | bytes 258056 | tf_op jit(solution)/shard_map/ppermute | solution.py:314
  14.5 5.2 %collective-permute-start = (bf16[2,2,84,128]{3,2,1,0:T(8,128)(2,1)S(1)}, bf16[2,2,84,128]{3,2,1,0:T(8,128)(2,1)S(1)}, u32[]{:S(2)}, u32[]{:S(2)}) collective-permute-start(bf16[2,2,84,128]{3,2,1,0:T(8,128)(2,1)S(1)} %get-tuple-element.17), channel_id=1, source_target_pairs={{0,4},{4,0},{8,12},{12,8},{16,20},{20,16},{24,28},{28,24},{1,5},{5... | collective-permute-start | bytes 258056 | tf_op jit(solution)/shard_map/ppermute | solution.py:306
  14.6 7.3 %collective-permute-start.11 = (bf16[128,256]{1,0:T(8,128)(2,1)S(1)}, bf16[128,256]{1,0:T(8,128)(2,1)S(1)}, u32[]{:S(2)}, u32[]{:S(2)}) collective-permute-start(bf16[128,256]{1,0:T(8,128)(2,1)S(1)} %fusion.17), channel_id=1, source_target_pairs={{0,4},{4,0},{8,12},{12,8},{16,20},{20,16},{24,28},{28,24},{1,5},{5... | collective-permute-start | bytes 196616 | tf_op jit(solution)/shard_map/ppermute | solution.py:306
  19.7 6.5 %collective-permute-start.2 = (bf16[2,2,2,84,128]{4,3,2,1,0:T(8,128)(2,1)S(1)}, bf16[2,2,2,84,128]{4,3,2,1,0:T(8,128)(2,1)S(1)}, u32[]{:S(2)}, u32[]{:S(2)}) collective-permute-start(bf16[2,2,2,84,128]{4,3,2,1,0:T(8,128)(2,1)S(1)} %pad_maximum_fusion.refs_0_), channel_id=1, source_target_pairs={{0,2},{1,3},{2,0},{3,1},{4,6},{5,7},{6,4},{7,5},{8,10},{9,11},{10,... | collective-permute-start | bytes 516104 | tf_op jit(solution)/shard_map/ppermute | solution.py:306
  21.3 4.9 %collective-permute-start.6 = (bf16[2,2,84,128]{3,2,1,0:T(8,128)(2,1)S(1)}, bf16[2,2,84,128]{3,2,1,0:T(8,128)(2,1)S(1)}, u32[]{:S(2)}, u32[]{:S(2)}) collective-permute-start(bf16[2,2,84,128]{3,2,1,0:T(8,128)(2,1)S(1)} %collective-permute-done.4.refs_4_), channel_id=1, source_target_pairs={{0,2},{1,3},{2,0},{3,1},{4,6},{5,7},{6,4},{7,5},{8,10},{9,11},{10,... | collective-permute-start | bytes 258056 | tf_op jit(solution)/shard_map/ppermute | solution.py:306
  21.9 5.2 %collective-permute-start.12 = (bf16[128,256]{1,0:T(8,128)(2,1)S(1)}, bf16[128,256]{1,0:T(8,128)(2,1)S(1)}, u32[]{:S(2)}, u32[]{:S(2)}) collective-permute-start(bf16[128,256]{1,0:T(8,128)(2,1)S(1)} %fusion.20), channel_id=1, source_target_pairs={{0,16},{4,20},{8,24},{12,28},{16,0},{20,4},{24,8},{28,12},{1,17},{... | collective-permute-start | bytes 196616 | tf_op jit(solution)/shard_map/ppermute | solution.py:306
  22.0 5.6 %collective-permute-start.1 = (bf16[2,2,2,84,128]{4,3,2,1,0:T(8,128)(2,1)S(1)}, bf16[2,2,2,84,128]{4,3,2,1,0:T(8,128)(2,1)S(1)}, u32[]{:S(2)}, u32[]{:S(2)}) collective-permute-start(bf16[2,2,2,84,128]{4,3,2,1,0:T(8,128)(2,1)S(1)} %pad_maximum_fusion.refs_0_), channel_id=1, source_target_pairs={{0,1},{1,0},{2,3},{3,2},{4,5},{5,4},{6,7},{7,6},{8,9},{9,8},{10,11... | collective-permute-start | bytes 516104 | tf_op jit(solution)/shard_map/ppermute | solution.py:306
  22.0 5.2 %collective-permute-start.5 = (bf16[2,2,84,128]{3,2,1,0:T(8,128)(2,1)S(1)}, bf16[2,2,84,128]{3,2,1,0:T(8,128)(2,1)S(1)}, u32[]{:S(2)}, u32[]{:S(2)}) collective-permute-start(bf16[2,2,84,128]{3,2,1,0:T(8,128)(2,1)S(1)} %collective-permute-done.4.refs_4_), channel_id=1, source_target_pairs={{0,1},{1,0},{2,3},{3,2},{4,5},{5,4},{6,7},{7,6},{8,9},{9,8},{10,11... | collective-permute-start | bytes 258056 | tf_op jit(solution)/shard_map/ppermute | solution.py:306
  26.3 1.3 %collective-permute-start.7 = (bf16[2,2,84,128]{3,2,1,0:T(8,128)(2,1)S(1)}, bf16[2,2,84,128]{3,2,1,0:T(8,128)(2,1)S(1)}, u32[]{:S(2)}, u32[]{:S(2)}) collective-permute-start(bf16[2,2,84,128]{3,2,1,0:T(8,128)(2,1)S(1)} %collective-permute-done.6.refs_6_), channel_id=1, source_target_pairs={{0,1},{1,0},{2,3},{3,2},{4,5},{5,4},{6,7},{7,6},{8,9},{9,8},{10,11... | collective-permute-start | bytes 258056 | tf_op jit(solution)/shard_map/ppermute | solution.py:306
  26.3 1.6 %collective-permute-start.3 = (bf16[2,2,2,84,128]{4,3,2,1,0:T(8,128)(2,1)S(1)}, bf16[2,2,2,84,128]{4,3,2,1,0:T(8,128)(2,1)S(1)}, u32[]{:S(2)}, u32[]{:S(2)}) collective-permute-start(bf16[2,2,2,84,128]{4,3,2,1,0:T(8,128)(2,1)S(1)} %collective-permute-done.2.refs_2_), channel_id=1, source_target_pairs={{0,1},{1,0},{2,3},{3,2},{4,5},{5,4},{6,7},{7,6},{8,9},{9,8},{10,11... | collective-permute-start | bytes 516104 | tf_op jit(solution)/shard_map/ppermute | solution.py:306
  27.1 3.0 %collective-permute-start.13 = (bf16[128,256]{1,0:T(8,128)(2,1)S(1)}, bf16[128,256]{1,0:T(8,128)(2,1)S(1)}, u32[]{:S(2)}, u32[]{:S(2)}) collective-permute-start(bf16[128,256]{1,0:T(8,128)(2,1)S(1)} %get-tuple-element.35), channel_id=1, source_target_pairs={{0,1},{1,0},{2,3},{3,2},{4,5},{5,4},{6,7},{7,6},{8,9},{9,8},{10,11... | collective-permute-start | bytes 196616 | tf_op jit(solution)/shard_map/ppermute | solution.py:306
  30.7 1.3 %collective-permute-start.22 = (bf16[128,256]{1,0:T(8,128)(2,1)S(1)}, bf16[128,256]{1,0:T(8,128)(2,1)S(1)}, u32[]{:S(2)}, u32[]{:S(2)}) collective-permute-start(bf16[128,256]{1,0:T(8,128)(2,1)S(1)} %get-tuple-element.24), channel_id=1, source_target_pairs={{0,1},{1,0},{2,3},{3,2},{4,5},{5,4},{6,7},{7,6},{8,9},{9,8},{10,11... | collective-permute-start | bytes 196616 | tf_op jit(solution)/shard_map/ppermute | solution.py:306
  32.1 4.4 %collective-permute-start.23 = (bf16[128,256]{1,0:T(8,128)(2,1)S(1)}, bf16[128,256]{1,0:T(8,128)(2,1)S(1)}, u32[]{:S(2)}, u32[]{:S(2)}) collective-permute-start(bf16[128,256]{1,0:T(8,128)(2,1)S(1)} %fusion.18), channel_id=1, source_target_pairs={{0,2},{1,3},{2,0},{3,1},{4,6},{5,7},{6,4},{7,5},{8,10},{9,11},{10,... | collective-permute-start | bytes 196616 | tf_op jit(solution)/shard_map/ppermute | solution.py:306
  36.5 4.5 %collective-permute-start.24 = (bf16[128,256]{1,0:T(8,128)(2,1)S(1)}, bf16[128,256]{1,0:T(8,128)(2,1)S(1)}, u32[]{:S(2)}, u32[]{:S(2)}) collective-permute-start(bf16[128,256]{1,0:T(8,128)(2,1)S(1)} %get-tuple-element.33), channel_id=1, source_target_pairs={{0,8},{4,12},{8,0},{12,4},{16,24},{20,28},{24,16},{28,20},{1,9},{5... | collective-permute-start | bytes 196616 | tf_op jit(solution)/shard_map/ppermute | solution.py:306
  36.6 10.5 %collective-permute-start.18 = (bf16[2,2,84,128]{3,2,1,0:T(8,128)(2,1)S(1)}, bf16[2,2,84,128]{3,2,1,0:T(8,128)(2,1)S(1)}, u32[]{:S(2)}, u32[]{:S(2)}) collective-permute-start(bf16[2,2,84,128]{3,2,1,0:T(8,128)(2,1)S(1)} %get-tuple-element.22), channel_id=1, source_target_pairs={{0,28},{4,8},{8,4},{12,16},{16,12},{20,24},{24,20},{28,0},{1,29},{... | collective-permute-start | bytes 258056 | tf_op jit(solution)/shard_map/ppermute | solution.py:314
  39.2 6.2 %collective-permute-start.14 = (bf16[2,2,84,128]{3,2,1,0:T(8,128)(2,1)S(1)}, bf16[2,2,84,128]{3,2,1,0:T(8,128)(2,1)S(1)}, u32[]{:S(2)}, u32[]{:S(2)}) collective-permute-start(bf16[2,2,84,128]{3,2,1,0:T(8,128)(2,1)S(1)} %get-tuple-element.22), channel_id=1, source_target_pairs={{0,4},{4,0},{8,12},{12,8},{16,20},{20,16},{24,28},{28,24},{1,5},{5... | collective-permute-start | bytes 258056 | tf_op jit(solution)/shard_map/ppermute | solution.py:306
  41.1 6.5 %collective-permute-start.25 = (bf16[128,256]{1,0:T(8,128)(2,1)S(1)}, bf16[128,256]{1,0:T(8,128)(2,1)S(1)}, u32[]{:S(2)}, u32[]{:S(2)}) collective-permute-start(bf16[128,256]{1,0:T(8,128)(2,1)S(1)} %fusion.19), channel_id=1, source_target_pairs={{0,4},{4,0},{8,12},{12,8},{16,20},{20,16},{24,28},{28,24},{1,5},{5... | collective-permute-start | bytes 196616 | tf_op jit(solution)/shard_map/ppermute | solution.py:306
  45.5 6.5 %collective-permute-start.16 = (bf16[2,2,2,84,128]{4,3,2,1,0:T(8,128)(2,1)S(1)}, bf16[2,2,2,84,128]{4,3,2,1,0:T(8,128)(2,1)S(1)}, u32[]{:S(2)}, u32[]{:S(2)}) collective-permute-start(bf16[2,2,2,84,128]{4,3,2,1,0:T(8,128)(2,1)S(1)} %pad_maximum_fusion.1.refs_0_), channel_id=1, source_target_pairs={{0,2},{1,3},{2,0},{3,1},{4,6},{5,7},{6,4},{7,5},{8,10},{9,11},{10,... | collective-permute-start | bytes 516104 | tf_op jit(solution)/shard_map/ppermute | solution.py:306
  47.1 5.0 %collective-permute-start.20 = (bf16[2,2,84,128]{3,2,1,0:T(8,128)(2,1)S(1)}, bf16[2,2,84,128]{3,2,1,0:T(8,128)(2,1)S(1)}, u32[]{:S(2)}, u32[]{:S(2)}) collective-permute-start(bf16[2,2,84,128]{3,2,1,0:T(8,128)(2,1)S(1)} %collective-permute-done.18.refs_4_), channel_id=1, source_target_pairs={{0,2},{1,3},{2,0},{3,1},{4,6},{5,7},{6,4},{7,5},{8,10},{9,11},{10,... | collective-permute-start | bytes 258056 | tf_op jit(solution)/shard_map/ppermute | solution.py:306
  47.6 5.2 %collective-permute-start.26 = (bf16[128,256]{1,0:T(8,128)(2,1)S(1)}, bf16[128,256]{1,0:T(8,128)(2,1)S(1)}, u32[]{:S(2)}, u32[]{:S(2)}) collective-permute-start(bf16[128,256]{1,0:T(8,128)(2,1)S(1)} %fusion.21), channel_id=1, source_target_pairs={{0,16},{4,20},{8,24},{12,28},{16,0},{20,4},{24,8},{28,12},{1,17},{... | collective-permute-start | bytes 196616 | tf_op jit(solution)/shard_map/ppermute | solution.py:306
  47.9 5.4 %collective-permute-start.15 = (bf16[2,2,2,84,128]{4,3,2,1,0:T(8,128)(2,1)S(1)}, bf16[2,2,2,84,128]{4,3,2,1,0:T(8,128)(2,1)S(1)}, u32[]{:S(2)}, u32[]{:S(2)}) collective-permute-start(bf16[2,2,2,84,128]{4,3,2,1,0:T(8,128)(2,1)S(1)} %pad_maximum_fusion.1.refs_0_), channel_id=1, source_target_pairs={{0,1},{1,0},{2,3},{3,2},{4,5},{5,4},{6,7},{7,6},{8,9},{9,8},{10,11... | collective-permute-start | bytes 516104 | tf_op jit(solution)/shard_map/ppermute | solution.py:306
  47.9 5.1 %collective-permute-start.19 = (bf16[2,2,84,128]{3,2,1,0:T(8,128)(2,1)S(1)}, bf16[2,2,84,128]{3,2,1,0:T(8,128)(2,1)S(1)}, u32[]{:S(2)}, u32[]{:S(2)}) collective-permute-start(bf16[2,2,84,128]{3,2,1,0:T(8,128)(2,1)S(1)} %collective-permute-done.18.refs_4_), channel_id=1, source_target_pairs={{0,1},{1,0},{2,3},{3,2},{4,5},{5,4},{6,7},{7,6},{8,9},{9,8},{10,11... | collective-permute-start | bytes 258056 | tf_op jit(solution)/shard_map/ppermute | solution.py:306
  52.0 1.3 %collective-permute-start.21 = (bf16[2,2,84,128]{3,2,1,0:T(8,128)(2,1)S(1)}, bf16[2,2,84,128]{3,2,1,0:T(8,128)(2,1)S(1)}, u32[]{:S(2)}, u32[]{:S(2)}) collective-permute-start(bf16[2,2,84,128]{3,2,1,0:T(8,128)(2,1)S(1)} %collective-permute-done.20.refs_6_), channel_id=1, source_target_pairs={{0,1},{1,0},{2,3},{3,2},{4,5},{5,4},{6,7},{7,6},{8,9},{9,8},{10,11... | collective-permute-start | bytes 258056 | tf_op jit(solution)/shard_map/ppermute | solution.py:306
  52.0 1.6 %collective-permute-start.17 = (bf16[2,2,2,84,128]{4,3,2,1,0:T(8,128)(2,1)S(1)}, bf16[2,2,2,84,128]{4,3,2,1,0:T(8,128)(2,1)S(1)}, u32[]{:S(2)}, u32[]{:S(2)}) collective-permute-start(bf16[2,2,2,84,128]{4,3,2,1,0:T(8,128)(2,1)S(1)} %collective-permute-done.16.refs_2_), channel_id=1, source_target_pairs={{0,1},{1,0},{2,3},{3,2},{4,5},{5,4},{6,7},{7,6},{8,9},{9,8},{10,11... | collective-permute-start | bytes 516104 | tf_op jit(solution)/shard_map/ppermute | solution.py:306
  52.9 3.0 %collective-permute-start.27 = (bf16[128,256]{1,0:T(8,128)(2,1)S(1)}, bf16[128,256]{1,0:T(8,128)(2,1)S(1)}, u32[]{:S(2)}, u32[]{:S(2)}) collective-permute-start(bf16[128,256]{1,0:T(8,128)(2,1)S(1)} %get-tuple-element.31), channel_id=1, source_target_pairs={{0,1},{1,0},{2,3},{3,2},{4,5},{5,4},{6,7},{7,6},{8,9},{9,8},{10,11... | collective-permute-start | bytes 196616 | tf_op jit(solution)/shard_map/ppermute | solution.py:306
  55.4 0.9 %copy-start.1 = (f32[2,2,84,128]{3,1,2,0:T(2,128)S(1)}, f32[2,2,84,128]{3,1,2,0:T(2,128)}, u32[]{:S(2)}) copy-start(f32[2,2,84,128]{3,1,2,0:T(2,128)} %param.9) | copy-start | bytes 516100

commit v5 on v4

v5 whole, which is shorter than its diff:
```python
import jax
import jax.numpy as jnp
from jax import lax
from jax.experimental import pallas as pl
from jax.experimental.layout import Layout, with_layout_constraint
from jax.experimental.pallas import tpu as pltpu
from jax.sharding import PartitionSpec as P

two_pi = 6.283185307179586
epsilon = 1e-06
f32 = jnp.float32
bf16 = jnp.bfloat16

VM = pl.BlockSpec(memory_space=pltpu.VMEM)
SM = pl.BlockSpec(memory_space=pltpu.SMEM)
HB = pl.BlockSpec(memory_space=pltpu.HBM)


def call(body, outs, specs, scratch=()):
    return pl.pallas_call(
        body,
        out_shape=outs,
        in_specs=specs,
        out_specs=jax.tree.map(lambda _: VM, outs),
        scratch_shapes=scratch,
        compiler_params=pltpu.CompilerParams(vmem_limit_bytes=16 << 20),
    )


def in_hbm(arrays):
    return [pltpu.with_memory_space_constraint(v, pltpu.HBM) for v in arrays]


def shape(dims, dtype=f32):
    return jax.ShapeDtypeStruct(dims, dtype)


def turn(value):
    half = value.shape[1] // 2
    lane = lax.broadcasted_iota(jnp.int32, (1, 2 * half), 1)
    return pltpu.roll(value, half, 1) * jnp.where(lane < half, -1.0, 1.0)


def second():
    return lax.rem(lax.axis_index("blk"), 2) == 1


def split_body(x_hbm, send_ref, keep_ref, x_ref, sem):
    copy = pltpu.make_async_copy(x_hbm, x_ref, sem)
    copy.start()
    copy.wait()
    spheres, count, n = keep_ref.shape
    half = n // 2
    for s in range(spheres):
        re, im = (x_ref[s, pl.ds(z, count, stride=2), :] for z in range(2))
        low = jnp.concatenate([re[:, :half], im[:, :half]], axis=1)
        high = jnp.concatenate([re[:, half:], im[:, half:]], axis=1)
        send_ref[s] = jnp.where(second(), low, high)
        keep_ref[s] = jnp.where(second(), high, low)


def tables_body(
    mie_other_ref, plane_hbm, wave_hbm, pos_hbm, weight_hbm, mie_hbm,
    column_ref, part_ref, plane_ref, wave_ref, pos_ref, weight_ref, mie_ref, held, sems,
):
    moves = ((wave_hbm, wave_ref), (pos_hbm, pos_ref), (weight_hbm, weight_ref), (mie_hbm, mie_ref))
    moves += ((plane_hbm, plane_ref),)
    copies = [pltpu.make_async_copy(*move, sems.at[i]) for i, move in enumerate(moves)]
    for copy in copies:
        copy.start()
    for copy in copies[:-1]:
        copy.wait()
    spheres, _, count = mie_ref.shape
    b = lax.axis_index("blk")
    turns = None
    for d in range(3):
        term = wave_ref[d : d + 1, :].astype(f32) * pos_ref[:, d : d + 1]
        turns = term if turns is None else turns + term
    angles = two_pi * (turns - jnp.floor(turns + 0.5))
    cos, sin = jnp.cos(angles), jnp.sin(angles)
    weight = weight_ref[...]
    held[...] = jnp.zeros_like(held)
    for i, value in enumerate((cos, sin, weight * cos, weight * sin)):
        held[i * spheres : (i + 1) * spheres, :] = value
    for o, ref in enumerate((mie_ref, mie_other_ref)):
        for s in range(spheres):
            for z in range(2):
                at = 4 * spheres + 2 * (o * spheres + s) + z
                held[at : at + 1, 0:count] = ref[s, z : z + 1, :]
    column_ref[...] = held[...].T
    copies[-1].wait()
    mate = b + 1 - 2 * lax.rem(b, 2)
    for o, block in enumerate((b, mate)):
        for a in range(2):
            part = plane_ref[a, 0:count, :]
            for p in range(1, plane_ref.shape[1] // count):
                part = jnp.where(block == p, plane_ref[a, p * count : (p + 1) * count, :], part)
            part_ref[o, a] = part


def project(field, part_ref, columns, spheres):
    total = None
    lead = (((0,), (0,)), ((), ()))
    with_re = with_im = None
    for o in range(2):
        side = jnp.concatenate([field[s][o] for s in range(spheres)], axis=1)
        one = lax.dot_general(part_ref[o, 0], side, lead, preferred_element_type=f32)
        two = lax.dot_general(part_ref[o, 1], side, lead, preferred_element_type=f32)
        with_re = one if with_re is None else with_re + one
        with_im = two if with_im is None else with_im + two
    n = with_re.shape[1] // spheres
    for s in range(spheres):
        at = slice(s * n, (s + 1) * n)
        part = with_re[:, at] + turn(with_im[:, at])
        c, d = columns[:, s : s + 1], columns[:, spheres + s : spheres + s + 1]
        value = c * part - d * turn(part)
        total = value if total is None else total + value
    return total


def put_rounded(round_ref, s, mine, other):
    first = jnp.where(second(), other, mine)
    last = jnp.where(second(), mine, other)
    round_ref[s] = jnp.concatenate([first, last], axis=0).astype(bf16)


def first_sums_body(mine_ref, other_ref, column_ref, part_ref, round_ref, send_ref, keep_ref):
    spheres = mine_ref.shape[0]
    field = []
    for s in range(spheres):
        put_rounded(round_ref, s, mine_ref[s], other_ref[s])
        field.append([mine_ref[s].astype(bf16), other_ref[s].astype(bf16)])
    total = project(field, part_ref, column_ref[...], spheres)
    keep_ref[...] = total
    send_ref[...] = total.astype(bf16)


def gather_body(shift_hbm, member_hbm, *refs):
    *piece_refs, out_ref, held, shift_ref, member_ref, sems = refs
    copies = [
        pltpu.make_async_copy(shift_hbm, shift_ref, sems.at[0]),
        pltpu.make_async_copy(member_hbm, member_ref, sems.at[1]),
    ]
    for copy in copies:
        copy.start()
    groups = len(piece_refs) // 2
    near_refs, odd_refs = piece_refs[:groups], piece_refs[groups:]
    spheres = odd_refs[0].shape[0]
    place = lax.div(lax.axis_index("blk"), 2)
    parity = lax.rem(lax.axis_index("slab"), 2)
    for slot in range(3):
        for s in range(spheres):
            parts = [ref[slot, s] for ref in near_refs] if slot < 2 else [ref[s] for ref in odd_refs]
            bit = 1
            while bit < groups:
                swap = lax.rem(lax.div(place, bit), 2) == 1
                parts = [jnp.where(swap, parts[i ^ bit], parts[i]) for i in range(groups)]
                bit *= 2
            held[slot * spheres + s] = jnp.concatenate(parts, axis=0)
    for copy in copies:
        copy.wait()
    for i in range(out_ref.shape[0]):
        for k in range(out_ref.shape[1]):
            shift = shift_ref[i, k]
            forward = (shift == 1) == (parity == 0)
            slot = jnp.where(shift == 0, 0, jnp.where(forward, 1, 2))
            out_ref[i, k] = held[slot * spheres + member_ref[i, k]]


def near_sum_body(mine_ref, other_ref, out_ref):
    spheres, pairs = mine_ref.shape[:2]
    for o, ref in enumerate((mine_ref, other_ref)):
        for s in range(spheres):
            with_re, with_im = ref[s, 0, 0], ref[s, 0, 1]
            for k in range(1, pairs):
                with_re = with_re + ref[s, k, 0]
                with_im = with_im + ref[s, k, 1]
            out_ref[o, s] = with_re + turn(with_im)


def image_fields(near_ref, total_ref, column_ref, part_ref):
    _, spheres, count, _ = near_ref.shape
    columns, total = column_ref[...], total_ref[...]
    turned_total = turn(total)
    sides = []
    for s in range(spheres):
        at = 2 * spheres + s
        c, d = columns[:, at : at + 1], columns[:, at + spheres : at + spheres + 1]
        sides.append((c * total + d * turned_total).astype(bf16))
    turned = jnp.concatenate(sides, axis=1)
    n = total.shape[1]
    out = [[] for _ in range(spheres)]
    for o in range(2):
        with_re = jnp.dot(part_ref[o, 0], turned, preferred_element_type=f32)
        with_im = jnp.dot(part_ref[o, 1], turned, preferred_element_type=f32)
        for s in range(spheres):
            at = slice(s * n, (s + 1) * n)
            value = near_ref[o, s] + with_re[:, at] - turn(with_im[:, at])
            at = 4 * spheres + 2 * (o * spheres + s)
            m_re, m_im = column_ref[0:count, at : at + 1], column_ref[0:count, at + 1 : at + 2]
            out[s].append(m_re * value + m_im * turn(value))
    return out


def first_image_body(
    near_ref, total_ref, column_ref, part_ref, mine_ref, other_ref, round_ref, send_ref, keep_ref
):
    images = image_fields(near_ref, total_ref, column_ref, part_ref)
    field = []
    for s, (mine, other) in enumerate(images):
        mine_ref[s] = mine
        other_ref[s] = other
        put_rounded(round_ref, s, mine, other)
        field.append([mine.astype(bf16), other.astype(bf16)])
    total = project(field, part_ref, column_ref[...], len(images))
    keep_ref[...] = total
    send_ref[...] = total.astype(bf16)


def second_image_body(
    near_ref, total_ref, column_ref, part_ref, x_ref, x_other_ref, g_ref, g_other_ref,
    mine_ref, other_ref, gram_ref,
):
    images = image_fields(near_ref, total_ref, column_ref, part_ref)
    half = total_ref.shape[1] // 2
    sums = None
    for s, rows in enumerate(images):
        mine_ref[s] = rows[0]
        other_ref[s] = rows[1]
        for x, g, h in ((x_ref[s], g_ref[s], rows[0]), (x_other_ref[s], g_other_ref[s], rows[1])):
            tx, tg = turn(x), turn(g)
            terms = (x * x, x * g, tx * g, g * g, x * h, tx * h, g * h, tg * h, h * h)
            found = [jnp.sum(term, axis=0, keepdims=True) for term in terms]
            sums = found if sums is None else [a + r for a, r in zip(sums, found)]
    sums = [row[:, :half] + row[:, half:] for row in sums] + [jnp.zeros((1, half), f32)]
    rows = [jnp.concatenate(sums[i : i + 2], axis=1) for i in range(0, len(sums), 2)]
    rest = jnp.zeros((gram_ref.shape[1] - len(rows), 2 * half), f32)
    gram_ref[...] = jnp.broadcast_to(jnp.concatenate(rows + [rest], axis=0)[None], gram_ref.shape)


def times(a, b):
    return (a[0] * b[0] - a[1] * b[1], a[0] * b[1] + a[1] * b[0])


def conj_times(a, b):
    return (a[0] * b[0] + a[1] * b[1], a[0] * b[1] - a[1] * b[0])


def plus(*terms):
    return (sum(t[0] for t in terms), sum(t[1] for t in terms))


def scaled(a, r):
    return (a[0] * r, a[1] * r)


def finish_body(
    entries, gram_ref, x_ref, g_ref, g_other_ref, h_ref, h_other_ref, basis_ref, residual_ref, hess_ref
):
    devices = gram_ref.shape[0]
    parts = [gram_ref[i] for i in range(2)]
    for i in range(2, devices):
        parts[i % 2] = parts[i % 2] + gram_ref[i]
    low, high = (part / entries for part in parts)
    half = low.shape[1] // 2
    row = []
    for i in range(9):
        at = (slice(i // 2, i // 2 + 1), slice(i % 2 * half, (i % 2 + 1) * half))
        row.append(jnp.concatenate([low[at], high[at]], axis=1))
    xx, gg, hh = row[0], row[3], row[8]
    xg, xh, gh = (row[1], row[2]), (row[4], row[5]), (row[6], row[7])
    square = xx + epsilon
    beta = jnp.sqrt(square)
    inv = 1.0 / beta
    h11 = ((xx - xg[0]) / square, -xg[1] / square)
    alpha = ((epsilon + xg[0]) / square * inv, xg[1] / square * inv)
    delta = -inv
    cross = alpha[0] * xg[0] + alpha[1] * xg[1]
    norm = (alpha[0] * alpha[0] + alpha[1] * alpha[1]) * xx + delta * delta * gg + 2.0 * delta * cross
    h21 = jnp.sqrt(jnp.maximum(norm, 0.0) + epsilon)
    a = (alpha[0] / h21, alpha[1] / h21)
    d = delta / h21
    b = (d - a[0], -a[1])
    h12 = scaled(plus(scaled(a, xx), times(b, xg), scaled(xh, -d)), inv)
    e = (a[0] - h12[0] * inv, a[1] - h12[1] * inv)
    with_x = plus(scaled(e, xx), times(b, xg), scaled(xh, -d))
    with_g = plus(times(e, (xg[0], -xg[1])), scaled(b, gg), scaled(gh, -d))
    h22 = plus(conj_times(a, with_x), scaled(with_g, d))
    c0 = plus(e, scaled(times(h22, a), -1.0))
    c1 = plus(b, scaled(h22, -d))
    c2 = -d
    last = (
        (c0[0] * c0[0] + c0[1] * c0[1]) * xx
        + (c1[0] * c1[0] + c1[1] * c1[1]) * gg
        + c2 * c2 * hh
        + 2.0 * times(conj_times(c0, c1), xg)[0]
        + 2.0 * c2 * conj_times(c0, xh)[0]
        + 2.0 * c2 * conj_times(c1, gh)[0]
    )
    h32 = jnp.sqrt(jnp.maximum(last, 0.0) + epsilon)
    for i, value in enumerate((beta, h11[0], h11[1], h21, h12[0], h12[1], h22[0], h22[1], h32)):
        hess_ref[i : i + 1, :] = value
    count = g_ref.shape[1]

    def whole(mine, other):
        low, high = jnp.where(second(), other, mine), jnp.where(second(), mine, other)
        return tuple(
            jnp.concatenate([low[:, at : at + half], high[:, at : at + half]], axis=1) for at in (0, half)
        )

    for s in range(g_ref.shape[0]):
        rows = [pl.ds(z, count, stride=2) for z in range(2)]
        x = (x_ref[s, rows[0], :], x_ref[s, rows[1], :])
        g = whole(g_ref[s], g_other_ref[s])
        h = whole(h_ref[s], h_other_ref[s])
        basis = plus(times(a, x), scaled(g, d))
        residual = plus(times(c0, x), times(c1, g), scaled(h, c2))
        for z in range(2):
            basis_ref[s, rows[z], :] = basis[z]
            residual_ref[s, rows[z], :] = residual[z]


def trade(value, axis, bit):
    return lax.ppermute(value, axis, [(i, i ^ bit) for i in range(lax.axis_size(axis))])


def trade_odd(value):
    count = lax.axis_size("slab")
    pairs = []
    for i in range(count):
        pairs.append((i, (i + 1) % count if i % 2 else (i - 1) % count))
    return lax.ppermute(value, "slab", pairs)


def bits(axis, start=1):
    out, bit = [], start
    while bit < lax.axis_size(axis):
        out.append(bit)
        bit *= 2
    return out


def fetch_pieces(own):
    out = []
    even = trade(own, "slab", 1)
    groups = [jnp.stack([own, even]), trade_odd(own)]
    for group in groups:
        pieces = {0: group}
        for bit in bits("blk", 2):
            pieces.update({r | bit // 2: trade(value, "blk", bit) for r, value in list(pieces.items())})
        out += [pieces[r] for r in range(len(pieces))]
    return out


def total_sums(send, keep):
    steps = [("blk", bit) for bit in bits("blk", 2)] + [("slab", bit) for bit in bits("slab")]
    steps[1:3] = steps[2:0:-1]
    for axis, bit in steps:
        keep = keep + trade(send, axis, bit).astype(f32)
        send = keep.astype(bf16)
    return keep


def per_device(
    incident, mie_coef, translation, pair_shift, pair_member, positions, wave_index, plane_coef,
    ewald_weight,
):
    spheres, _, count, n = incident.shape
    pairs = translation.shape[1]
    blocks = lax.axis_size("blk")
    devices = blocks * lax.axis_size("slab")
    waves = plane_coef.shape[0]
    entries = spheres * lax.axis_size("slab") * count * blocks
    x = incident.transpose(0, 2, 1, 3).reshape(spheres, 2 * count, n)

    field = shape((spheres, count, n))
    both = shape((2, spheres, count, n))
    pair_half = shape((spheres, 2 * count, n), bf16)
    sums = shape((waves, n))
    sums_half = shape((waves, n), bf16)
    sources = shape((spheres, pairs, count * blocks, n), bf16)
    held_rows = -(-8 * spheres // 8) * 8
    column = shape((waves, held_rows))
    part = shape((2, 2, count, waves), bf16)

    def both_fields(own, send, keep):
        total = total_sums(send, keep)
        pieces = fetch_pieces(own)
        table = pltpu.SMEM((spheres, pairs), jnp.int32)
        buffers = [pltpu.VMEM((3 * spheres, count * blocks, n), bf16), table, table]
        buffers.append(pltpu.SemaphoreType.DMA((2,)))
        gathered = call(gather_body, sources, [HB, HB] + [VM] * blocks, buffers)(
            *in_hbm((pair_shift, pair_member)), *pieces
        )
        products = [
            jnp.einsum("ikarc,ikcn->ikarn", rows, gathered, preferred_element_type=f32)
            for rows in (rows_mine, rows_other)
        ]
        near = call(near_sum_body, both, [VM] * 2)(*products)
        return near, total

    mie_other = trade(mie_coef, "blk", 1)
    buffers = [pltpu.VMEM(x.shape, f32), pltpu.SemaphoreType.DMA]
    send, x_mine = call(split_body, (field, field), [HB], buffers)(*in_hbm([x]))
    x_other = trade(send, "blk", 1)
    stored = Layout(major_to_minor=(0, 1, 3, 2, 4))
    rows_mine = with_layout_constraint(translation, stored)
    operands = (
        plane_coef.transpose(1, 2, 0), wave_index.T, positions, ewald_weight.reshape(1, waves), mie_coef
    )
    buffers = [pltpu.VMEM(v.shape, v.dtype) for v in operands]
    buffers += [pltpu.VMEM((held_rows, waves), f32), pltpu.SemaphoreType.DMA((len(operands),))]
    columns, plane = call(
        tables_body, (column, part), [VM] + [HB] * len(operands), buffers
    )(mie_other, *in_hbm(operands))
    rounded, send, keep = call(first_sums_body, (pair_half, sums_half, sums), [VM] * 4)(x_mine, x_other, columns, plane)
    rows_other = with_layout_constraint(trade(rows_mine, "blk", 1), stored)
    near, total = both_fields(rounded, send, keep)
    g_mine, g_other, rounded, send, keep = call(
        first_image_body, (field, field, pair_half, sums_half, sums), [VM] * 4
    )(near, total, columns, plane)
    g_back = trade(g_other, "blk", 1)
    near, total = both_fields(rounded, send, keep)
    h_mine, h_other, gram = call(
        second_image_body, (field, field, shape((devices, 8, n))), [VM] * 8
    )(near, total, columns, plane, x_mine, x_other, g_mine, g_other)
    h_back = trade(h_other, "blk", 1)
    gram = lax.all_to_all(gram, ("slab", "blk"), 0, 0, tiled=True)
    flat = shape((spheres, 2 * count, n))
    basis, residual, hessenberg = call(
        lambda *refs: finish_body(float(entries), *refs), (flat, flat, shape((9, n))), [VM] * 6
    )(gram, x, g_mine, g_back, h_mine, h_back)

    def unflatten(value):
        return value.reshape(spheres, count, 2, n).transpose(0, 2, 1, 3)

    return unflatten(basis), unflatten(residual), hessenberg


def solution(mesh):
    placed = (
        P("slab", None, "blk", None),
        P("slab", None, "blk"),
        P("slab", None, None, "blk", None),
        P("slab", None),
        P("slab", None),
        P("slab", None),
        P(),
        P(),
        P(),
    )
    return jax.shard_map(
        per_device,
        mesh=mesh,
        in_specs=placed,
        out_specs=(P("slab", None, "blk", None), P("slab", None, "blk", None), P()),
        check_vma=False,
    )
```

time: 70.2 us -> 68.1 us (0.970)
  blocking collectives: 12.4 us -> 0 us
  waiting for transfers between devices: 24.5 us -> 30.5 us
  Pallas kernels: 6.22 us -> 8.26 us
  starting transfers between devices: 23.5 us -> 24.8 us
  matrix products: 1.83 us -> 3.12 us
    all_to_all x1 -> x0, blocking collectives: 12.4 us -> none  [per_device(): gram = lax.all_to_all(gram, ('slab', 'blk'), 0, 0, tiled=True)]
    all_to_all x0 -> x1, waiting for transfers between devices: none -> 6.6 us  [per_device(): gram = lax.all_to_all(gram, ('slab', 'blk'), 0, 0, tiled=True)]
    all_to_all x0 -> x1, starting transfers between devices: none -> 2.67 us  [per_device(): gram = lax.all_to_all(gram, ('slab', 'blk'), 0, 0, tiled=True)]
    pallas_call x7 -> x9, Pallas kernels: 5.33 us -> 7.31 us  [the longest x2 1.65 us: both_fields(): call(gather_body, sources, [HB, HB] + [VM] * blocks, buffers)]
    ppermute x26 -> x19, starting transfers between devices: 17.5 us -> 16 us  [trade(): lax.ppermute(value, axis, [(i, i ^ bit) for i in range(lax.axis_size(axis...]
    dot_general x2 -> x4, matrix products: 1.83 us -> 3.12 us  [both_fields(): jnp.einsum('ikarc,ikcn->ikarn', rows, gathered, preferred_element_type=f32)]
    ppermute x26 -> x19, waiting for transfers between devices: 24.5 us -> 23.9 us  [trade(): lax.ppermute(value, axis, [(i, i ^ bit) for i in range(lax.axis_size(axis...]
  transfers between devices with their start and end apart: 28 -> 22, of which waited for: 15 -> 11; matrix products, arithmetic and copies ran while one was open for 3% -> 4% of each run, Pallas kernels for 4% -> 7%
where the time goes in v5:
time: 68.1 us; the launch traced here: 67.9 us
  waiting for transfers between devices  30.5 us (45%)
  starting transfers between devices  24.8 us (36%)
  Pallas kernels  8.26 us (12%)
  matrix products  3.12 us (5%)
  between operations  0.86 us (1%)
    ppermute x19, waiting for transfers between devices, trade(): lax.ppermute(value, axis, [(i, i ^ bit) for i in range(lax.axis_size(axis...  23.9 us
    ppermute x19, starting transfers between devices, trade(): lax.ppermute(value, axis, [(i, i ^ bit) for i in range(lax.axis_size(axis...  16 us
    all_to_all x1, waiting for transfers between devices, per_device(): gram = lax.all_to_all(gram, ('slab', 'blk'), 0, 0, tiled=True)  6.6 us
    ppermute x2, starting transfers between devices, trade_odd(): return lax.ppermute(value, 'slab', pairs)  6.11 us
    dot_general x4, matrix products, both_fields(): jnp.einsum('ikarc,ikcn->ikarn', rows, gathered, preferred_element_type=f32)  3.12 us
    all_to_all x1, starting transfers between devices, per_device(): gram = lax.all_to_all(gram, ('slab', 'blk'), 0, 0, tiled=True)  2.67 us
    pallas_call x2, Pallas kernels, both_fields(): call(gather_body, sources, [HB, HB] + [VM] * blocks, buffers)  1.65 us
    pallas_call x1, Pallas kernels, per_device(): call(second_image_body, (field, field, shape((devices, 8, n))), [VM] * 8)  1.56 us
  transfers between devices with their start and end apart: 22, of which 11 were waited for; matrix products, arithmetic and copies ran while one was open for 4% of the time, Pallas kernels for 7%

profile of v5, /device:TPU:0, one launch (start us, length us, event | category | flops | bytes accessed | tf_op | source)
XLA Modules:
  0.0 67.9 jit_solution(2160217436743477679)
XLA Ops:
  0.6 0.6 collective-permute-start.6
  1.2 1.0 %shard_map.112 = (f32[2,84,128]{2,1,0:T(8,128)S(1)}, f32[2,84,128]{2,1,0:T(8,128)S(1)}) custom-call(f32[2,168,128]{2,1,0:T(8,128)} %bitcast.38), custom_call_target="tpu_custom_call" | custom-call | tf_op jit(solution)/shard_map/pallas_call | solution.py:404
  2.2 0.1 collective-permute-start
  2.3 0.5 collective-permute-start.1
  2.8 2.5 %collective-permute-done.1.mie_other_ref = f32[2,2,84]{2,1,0:T(2,128)S(1)} collective-permute-done((f32[2,2,84]{2,1,0:T(2,128)}, f32[2,2,84]{2,1,0:T(2,128)S(1)}, u32[]{:S(2)}, u32[]{:S(2)}) %collective-permute-start.1) | collective-permute-done | bytes 1376 | tf_op jit(solution)/shard_map/ppermute | solution.py:324
  5.3 1.2 %shard_map.113 = (f32[256,16]{1,0:T(8,128)S(1)}, bf16[2,2,84,256]{3,2,1,0:T(8,128)(2,1)S(1)}) custom-call(f32[2,2,84]{2,1,0:T(2,128)S(1)} %collective-permute-done.1.mie_other_ref, bf16[2,336,256]{2,1,0:T(8,128)(2,1)} %bitcast.42, s32[3,256]{1,0:T(4,128)} %bitcast.45, f32[2,3]{1,0:T(2,128)} %pos_hbm.1, f32[1,256]{1,0:T(1,128)} %bitcast.46, f32[2,2,84]{2,1,0:T(2,128)} %mie_hbm.1), custom_call_target="tpu_custom_call" | custom-call | tf_op jit(solution)/shard_map/pallas_call | solution.py:413
  6.5 0.0 collective-permute-done.other_ref.x_other_ref
  6.5 0.5 shard_map.114
  7.0 2.9 %collective-permute-start.7 = (bf16[256,128]{1,0:T(8,128)(2,1)S(1)}, bf16[256,128]{1,0:T(8,128)(2,1)S(1)}, u32[]{:S(2)}, u32[]{:S(2)}) collective-permute-start(bf16[256,128]{1,0:T(8,128)(2,1)S(1)} %get-tuple-element.27), channel_id=1, source_target_pairs={{0,2},{1,3},{2,0},{3,1},{4,6},{5,7},{6,4},{7,5},{8,10},{9,11},{10,... | collective-permute-start | bytes 196616 | tf_op jit(solution)/shard_map/ppermute | solution.py:324
  9.9 2.4 %collective-permute-done.7 = bf16[256,128]{1,0:T(8,128)(2,1)S(1)} collective-permute-done((bf16[256,128]{1,0:T(8,128)(2,1)S(1)}, bf16[256,128]{1,0:T(8,128)(2,1)S(1)}, u32[]{:S(2)}, u32[]{:S(2)}) %collective-permute-start.7) | collective-permute-done | bytes 65568 | tf_op jit(solution)/shard_map/ppermute | solution.py:324
  12.3 2.0 %collective-permute-start.8 = (bf16[256,128]{1,0:T(8,128)(2,1)S(1)}, bf16[256,128]{1,0:T(8,128)(2,1)S(1)}, u32[]{:S(2)}, u32[]{:S(2)}) collective-permute-start(bf16[256,128]{1,0:T(8,128)(2,1)S(1)} %fusion.24), channel_id=1, source_target_pairs={{0,8},{4,12},{8,0},{12,4},{16,24},{20,28},{24,16},{28,20},{1,9},{5... | collective-permute-start | bytes 196616 | tf_op jit(solution)/shard_map/ppermute | solution.py:324
  14.3 0.0 copy-start.1
  14.3 3.4 %collective-permute-start.4 = (bf16[2,168,128]{2,1,0:T(8,128)(2,1)S(1)}, bf16[2,168,128]{2,1,0:T(8,128)(2,1)S(1)}, u32[]{:S(2)}, u32[]{:S(2)}) collective-permute-start(bf16[2,168,128]{2,1,0:T(8,128)(2,1)S(1)} %get-tuple-element.25), channel_id=1, source_target_pairs={{0,28},{4,8},{8,4},{12,16},{16,12},{20,24},{24,20},{28,0},{1,29},{... | collective-permute-start | bytes 258056 | tf_op jit(solution)/shard_map/ppermute | solution.py:332
  17.7 0.0 collective-permute-start.2
  17.7 0.0 collective-permute-done.8
  17.8 2.1 %collective-permute-start.9 = (bf16[256,128]{1,0:T(8,128)(2,1)S(1)}, bf16[256,128]{1,0:T(8,128)(2,1)S(1)}, u32[]{:S(2)}, u32[]{:S(2)}) collective-permute-start(bf16[256,128]{1,0:T(8,128)(2,1)S(1)} %fusion.28), channel_id=1, source_target_pairs={{0,4},{4,0},{8,12},{12,8},{16,20},{20,16},{24,28},{28,24},{1,5},{5... | collective-permute-start | bytes 196616 | tf_op jit(solution)/shard_map/ppermute | solution.py:324
  19.9 2.9 %collective-permute-done.2 = bf16[2,168,128]{2,1,0:T(8,128)(2,1)S(1)} collective-permute-done((bf16[2,168,128]{2,1,0:T(8,128)(2,1)S(1)}, bf16[2,168,128]{2,1,0:T(8,128)(2,1)S(1)}, u32[]{:S(2)}, u32[]{:S(2)}) %collective-permute-start.2) | collective-permute-done | bytes 86048 | tf_op jit(solution)/shard_map/ppermute | solution.py:324
  22.7 1.6 %collective-permute-start.3 = (bf16[2,2,168,128]{3,2,1,0:T(8,128)(2,1)S(1)}, bf16[2,2,168,128]{3,2,1,0:T(8,128)(2,1)S(1)}, u32[]{:S(2)}, u32[]{:S(2)}) collective-permute-start(bf16[2,2,168,128]{3,2,1,0:T(8,128)(2,1)S(1)} %pad_maximum_fusion.refs_0_), channel_id=1, source_target_pairs={{0,2},{1,3},{2,0},{3,1},{4,6},{5,7},{6,4},{7,5},{8,10},{9,11},{10,... | collective-permute-start | bytes 516104 | tf_op jit(solution)/shard_map/ppermute | solution.py:324
  24.3 0.0 collective-permute-done.4.refs_2_
  24.3 0.5 collective-permute-start.5
  24.8 0.0 collective-permute-done.9
  24.9 0.1 collective-permute-start.10
  25.0 4.2 %collective-permute-done.5.refs_3_ = bf16[2,168,128]{2,1,0:T(8,128)(2,1)S(1)} collective-permute-done((bf16[2,168,128]{2,1,0:T(8,128)(2,1)S(1)}, bf16[2,168,128]{2,1,0:T(8,128)(2,1)S(1)}, u32[]{:S(2)}, u32[]{:S(2)}) %collective-permute-start.5) | collective-permute-done | bytes 86048 | tf_op jit(solution)/shard_map/ppermute | solution.py:324
  29.1 0.0 collective-permute-done.3.refs_1_
  29.1 0.8 %shard_map.115 = bf16[2,8,336,128]{3,2,1,0:T(8,128)(2,1)S(1)} custom-call(s32[2,8]{1,0:T(2,128)} %shift_hbm.3, s32[2,8]{1,0:T(2,128)} %member_hbm.3, bf16[2,2,168,128]{3,2,1,0:T(8,128)(2,1)S(1)} %pad_maximum_fusion.refs_0_, bf16[2,2,168,128]{3,2,1,0:T(8,128)(2,1)S(1)} %collective-permute-done.3.refs_1_, ...), custom_call_target="tpu_custom_call" | custom-call | tf_op jit(solution)/shard_map/pallas_call | solution.py:392
  30.0 0.0 copy-done.1
  30.0 0.8 %fusion.8.mine_ref = f32[2,8,2,84,128]{4,3,2,1,0:T(8,128)S(1)} fusion(bf16[2,8,2,84,336]{4,2,3,1,0:T(2,128)(2,1)S(1)} %copy-done.1, bf16[2,8,336,128]{3,2,1,0:T(8,128)(2,1)S(1)} %shard_map.115), kind=kOutput, calls=%fused_computation.8 | convolution fusion | flops 231211008 | bytes 4558848 | tf_op jit(solution)/shard_map/ikarc,ikcn->ikarn/dot_general | solution.py:396
  30.8 0.0 collective-permute-done.10
  30.8 0.0 collective-permute-done.6
  30.8 0.8 %fusion.14.other_ref = f32[2,8,2,84,128]{4,3,2,1,0:T(8,128)S(1)} fusion(bf16[2,8,2,84,336]{4,2,3,1,0:T(2,128)(2,1)S(1)} %collective-permute-done.6, bf16[2,8,336,128]{3,2,1,0:T(8,128)(2,1)S(1)} %shard_map.115), kind=kOutput, calls=%fused_computation.10 | convolution fusion | flops 231211008 | bytes 4558848 | tf_op jit(solution)/shard_map/ikarc,ikcn->ikarn/dot_general | solution.py:396
  31.6 0.1 shard_map.116.near_ref
  31.8 1.1 %shard_map.117 = (f32[2,84,128]{2,1,0:T(8,128)S(1)}, f32[2,84,128]{2,1,0:T(8,128)S(1)}, bf16[2,168,128]{2,1,0:T(8,128)(2,1)S(1)}, bf16[256,128]{1,0:T(8,128)(2,1)S(1)}, f32[256,128]{1,0:T(8,128)S(1)}) custom-call(f32[2,2,84,128]{3,2,1,0:T(8,128)S(1)} %shard_map.116.near_ref, f32[256,128]{1,0:T(8,128)S(1)} %convert_add_fusion.4.total_ref, ...), custom_call_target="tpu_custom_call" | custom-call | tf_op jit(solution)/shard_map/pallas_call | solution.py:419
  32.9 1.6 %collective-permute-start.15 = (bf16[256,128]{1,0:T(8,128)(2,1)S(1)}, bf16[256,128]{1,0:T(8,128)(2,1)S(1)}, u32[]{:S(2)}, u32[]{:S(2)}) collective-permute-start(bf16[256,128]{1,0:T(8,128)(2,1)S(1)} %get-tuple-element.30), channel_id=1, source_target_pairs={{0,2},{1,3},{2,0},{3,1},{4,6},{5,7},{6,4},{7,5},{8,10},{9,11},{10,... | collective-permute-start | bytes 196616 | tf_op jit(solution)/shard_map/ppermute | solution.py:324
  34.5 2.7 %collective-permute-done.15 = bf16[256,128]{1,0:T(8,128)(2,1)S(1)} collective-permute-done((bf16[256,128]{1,0:T(8,128)(2,1)S(1)}, bf16[256,128]{1,0:T(8,128)(2,1)S(1)}, u32[]{:S(2)}, u32[]{:S(2)}) %collective-permute-start.15) | collective-permute-done | bytes 65568 | tf_op jit(solution)/shard_map/ppermute | solution.py:324
  37.2 0.1 collective-permute-start.16
  37.3 2.7 %collective-permute-start.13 = (bf16[2,168,128]{2,1,0:T(8,128)(2,1)S(1)}, bf16[2,168,128]{2,1,0:T(8,128)(2,1)S(1)}, u32[]{:S(2)}, u32[]{:S(2)}) collective-permute-start(bf16[2,168,128]{2,1,0:T(8,128)(2,1)S(1)} %get-tuple-element.28), channel_id=1, source_target_pairs={{0,28},{4,8},{8,4},{12,16},{16,12},{20,24},{24,20},{28,0},{1,29},{... | collective-permute-start | bytes 258056 | tf_op jit(solution)/shard_map/ppermute | solution.py:332
  40.0 0.8 %collective-permute-start.11 = (bf16[2,168,128]{2,1,0:T(8,128)(2,1)S(1)}, bf16[2,168,128]{2,1,0:T(8,128)(2,1)S(1)}, u32[]{:S(2)}, u32[]{:S(2)}) collective-permute-start(bf16[2,168,128]{2,1,0:T(8,128)(2,1)S(1)} %get-tuple-element.28), channel_id=1, source_target_pairs={{0,4},{4,0},{8,12},{12,8},{16,20},{20,16},{24,28},{28,24},{1,5},{5... | collective-permute-start | bytes 258056 | tf_op jit(solution)/shard_map/ppermute | solution.py:324
  40.8 0.8 %collective-permute-done.16 = bf16[256,128]{1,0:T(8,128)(2,1)S(1)} collective-permute-done((bf16[256,128]{1,0:T(8,128)(2,1)S(1)}, bf16[256,128]{1,0:T(8,128)(2,1)S(1)}, u32[]{:S(2)}, u32[]{:S(2)}) %collective-permute-start.16) | collective-permute-done | bytes 65568 | tf_op jit(solution)/shard_map/ppermute | solution.py:324
  41.6 0.6 collective-permute-start.17
  42.1 3.3 %collective-permute-done.11 = bf16[2,168,128]{2,1,0:T(8,128)(2,1)S(1)} collective-permute-done((bf16[2,168,128]{2,1,0:T(8,128)(2,1)S(1)}, bf16[2,168,128]{2,1,0:T(8,128)(2,1)S(1)}, u32[]{:S(2)}, u32[]{:S(2)}) %collective-permute-start.11) | collective-permute-done | bytes 86048 | tf_op jit(solution)/shard_map/ppermute | solution.py:324
  45.4 1.6 %collective-permute-start.12 = (bf16[2,2,168,128]{3,2,1,0:T(8,128)(2,1)S(1)}, bf16[2,2,168,128]{3,2,1,0:T(8,128)(2,1)S(1)}, u32[]{:S(2)}, u32[]{:S(2)}) collective-permute-start(bf16[2,2,168,128]{3,2,1,0:T(8,128)(2,1)S(1)} %pad_maximum_fusion.1.refs_0_), channel_id=1, source_target_pairs={{0,2},{1,3},{2,0},{3,1},{4,6},{5,7},{6,4},{7,5},{8,10},{9,11},{10,... | collective-permute-start | bytes 516104 | tf_op jit(solution)/shard_map/ppermute | solution.py:324
  47.0 0.0 collective-permute-done.13.refs_2_
  47.0 0.5 collective-permute-start.14
  47.5 0.0 collective-permute-done.17
  47.6 0.1 collective-permute-start.18
  47.7 4.2 %collective-permute-done.14.refs_3_ = bf16[2,168,128]{2,1,0:T(8,128)(2,1)S(1)} collective-permute-done((bf16[2,168,128]{2,1,0:T(8,128)(2,1)S(1)}, bf16[2,168,128]{2,1,0:T(8,128)(2,1)S(1)}, u32[]{:S(2)}, u32[]{:S(2)}) %collective-permute-start.14) | collective-permute-done | bytes 86048 | tf_op jit(solution)/shard_map/ppermute | solution.py:324
  51.8 0.0 collective-permute-done.12.refs_1_
  51.8 0.8 %shard_map.118 = bf16[2,8,336,128]{3,2,1,0:T(8,128)(2,1)S(1)} custom-call(s32[2,8]{1,0:T(2,128)} %shift_hbm.3, s32[2,8]{1,0:T(2,128)} %member_hbm.3, bf16[2,2,168,128]{3,2,1,0:T(8,128)(2,1)S(1)} %pad_maximum_fusion.1.refs_0_, bf16[2,2,168,128]{3,2,1,0:T(8,128)(2,1)S(1)} %collective-permute-done.12.refs_1_, ...), custom_call_target="tpu_custom_call" | custom-call | tf_op jit(solution)/shard_map/pallas_call | solution.py:392
  52.7 0.8 %fusion.11.mine_ref = f32[2,8,2,84,128]{4,3,2,1,0:T(8,128)S(1)} fusion(bf16[2,8,2,84,336]{4,2,3,1,0:T(2,128)(2,1)S(1)} %copy-done.1, bf16[2,8,336,128]{3,2,1,0:T(8,128)(2,1)S(1)} %shard_map.118), kind=kOutput, calls=%fused_computation.9 | convolution fusion | flops 231211008 | bytes 4558848 | tf_op jit(solution)/shard_map/ikarc,ikcn->ikarn/dot_general | solution.py:396
  53.5 0.8 %fusion.17.other_ref = f32[2,8,2,84,128]{4,3,2,1,0:T(8,128)S(1)} fusion(bf16[2,8,2,84,336]{4,2,3,1,0:T(2,128)(2,1)S(1)} %collective-permute-done.6, bf16[2,8,336,128]{3,2,1,0:T(8,128)(2,1)S(1)} %shard_map.118), kind=kOutput, calls=%fused_computation.11 | convolution fusion | flops 231211008 | bytes 4558848 | tf_op jit(solution)/shard_map/ikarc,ikcn->ikarn/dot_general | solution.py:396
  54.2 0.1 shard_map.119.near_ref
  54.4 0.0 copy-start
  54.4 0.0 collective-permute-done.18
  54.5 1.6 %shard_map.120 = (f32[2,84,128]{2,1,0:T(8,128)S(1)}, f32[2,84,128]{2,1,0:T(8,128)S(1)}, f32[32,8,128]{2,1,0:T(8,128)}) custom-call(f32[2,2,84,128]{3,2,1,0:T(8,128)S(1)} %shard_map.119.near_ref, f32[256,128]{1,0:T(8,128)S(1)} %convert_add_fusion.total_ref, f32[256,16]{1,0:T(8,128)S(1)} %get-tuple-element.23.column_ref, ...), custom_call_target="tpu_custom_call" | custom-call | tf_op jit(solution)/shard_map/pallas_call | solution.py:424
  56.0 2.7 %all-to-all-start = ((f32[32,8,128]{2,1,0:T(8,128)}), f32[32,8,128]{2,1,0:T(8,128)S(1)}, u32[]{:S(2)}, u32[]{:S(2)}) async-start(f32[32,8,128]{2,1,0:T(8,128)} %get-tuple-element.33), calls=%async_computation | async-start | bytes 262144 | tf_op jit(solution)/shard_map/all_to_all | solution.py:428
  58.7 0.3 collective-permute-start.19
  59.0 0.3 collective-permute-start.20
  59.3 0.8 %collective-permute-done.19.refs_3_ = f32[2,84,128]{2,1,0:T(8,128)S(1)} collective-permute-done((f32[2,84,128]{2,1,0:T(8,128)S(1)}, f32[2,84,128]{2,1,0:T(8,128)S(1)}, u32[]{:S(2)}, u32[]{:S(2)}) %collective-permute-start.19) | collective-permute-done | bytes 86048 | tf_op jit(solution)/shard_map/ppermute | solution.py:324
  60.0 0.3 collective-permute-done.20.refs_5_
  60.3 6.6 %all-to-all-done.refs_0_ = f32[32,8,128]{2,1,0:T(8,128)S(1)} async-done(((f32[32,8,128]{2,1,0:T(8,128)}), f32[32,8,128]{2,1,0:T(8,128)S(1)}, u32[]{:S(2)}, u32[]{:S(2)}) %all-to-all-start) | async-done | bytes 131104 | tf_op jit(solution)/shard_map/all_to_all | solution.py:428
  66.9 0.0 copy-done
  66.9 1.0 %shard_map.121 = (f32[2,168,128]{2,1,0:T(8,128)}, f32[2,168,128]{2,1,0:T(8,128)}, f32[9,128]{1,0:T(8,128)}) custom-call(f32[32,8,128]{2,1,0:T(8,128)S(1)} %all-to-all-done.refs_0_, f32[2,168,128]{2,1,0:T(8,128)S(1)} %bitcast.39, f32[2,84,128]{2,1,0:T(8,128)S(1)} %get-tuple-element.31.g_ref.refs_2_, f32[2,84,128]{2,1,0:T(8,128)S(1)} %collective-permute-done.19.refs_3_, ...), custom_call_target="tpu_custom_call" | custom-call | tf_op jit(solution)/shard_map/pallas_call | solution.py:430
  (10 shorter events, 0.3 us)
Async XLA Ops:
  0.6 30.2 %collective-permute-start.6 = (bf16[2,8,2,84,336]{4,2,3,1,0:T(2,128)(2,1)}, bf16[2,8,2,84,336]{4,2,3,1,0:T(2,128)(2,1)S(1)}, u32[]{:S(2)}, u32[]{:S(2)}) collective-permute-start(bf16[2,8,2,84,336]{4,2,3,1,0:T(2,128)(2,1)} %param.11), channel_id=1, source_target_pairs={{0,1},{1,0},{2,3},{3,2},{4,5},{5,4},{6,7},{7,6},{8,9},{9,8},{10,11... | collective-permute-start | bytes 5419016 | tf_op jit(solution)/shard_map/ppermute | solution.py:324
  2.2 4.2 %collective-permute-start = (f32[2,84,128]{2,1,0:T(8,128)S(1)}, f32[2,84,128]{2,1,0:T(8,128)S(1)}, u32[]{:S(2)}, u32[]{:S(2)}) collective-permute-start(f32[2,84,128]{2,1,0:T(8,128)S(1)} %get-tuple-element.22), channel_id=1, source_target_pairs={{0,1},{1,0},{2,3},{3,2},{4,5},{5,4},{6,7},{7,6},{8,9},{9,8},{10,11... | collective-permute-start | bytes 258056 | tf_op jit(solution)/shard_map/ppermute | solution.py:324
  2.3 2.9 %collective-permute-start.1 = (f32[2,2,84]{2,1,0:T(2,128)}, f32[2,2,84]{2,1,0:T(2,128)S(1)}, u32[]{:S(2)}, u32[]{:S(2)}) collective-permute-start(f32[2,2,84]{2,1,0:T(2,128)} %mie_hbm.1), channel_id=1, source_target_pairs={{0,1},{1,0},{2,3},{3,2},{4,5},{5,4},{6,7},{7,6},{8,9},{9,8},{10,11... | collective-permute-start | bytes 4040 | tf_op jit(solution)/shard_map/ppermute | solution.py:324
  7.0 5.3 %collective-permute-start.7 = (bf16[256,128]{1,0:T(8,128)(2,1)S(1)}, bf16[256,128]{1,0:T(8,128)(2,1)S(1)}, u32[]{:S(2)}, u32[]{:S(2)}) collective-permute-start(bf16[256,128]{1,0:T(8,128)(2,1)S(1)} %get-tuple-element.27), channel_id=1, source_target_pairs={{0,2},{1,3},{2,0},{3,1},{4,6},{5,7},{6,4},{7,5},{8,10},{9,11},{10,... | collective-permute-start | bytes 196616 | tf_op jit(solution)/shard_map/ppermute | solution.py:324
  12.3 5.4 %collective-permute-start.8 = (bf16[256,128]{1,0:T(8,128)(2,1)S(1)}, bf16[256,128]{1,0:T(8,128)(2,1)S(1)}, u32[]{:S(2)}, u32[]{:S(2)}) collective-permute-start(bf16[256,128]{1,0:T(8,128)(2,1)S(1)} %fusion.24), channel_id=1, source_target_pairs={{0,8},{4,12},{8,0},{12,4},{16,24},{20,28},{24,16},{28,20},{1,9},{5... | collective-permute-start | bytes 196616 | tf_op jit(solution)/shard_map/ppermute | solution.py:324
  14.3 15.6 %copy-start.1 = (bf16[2,8,2,84,336]{4,2,3,1,0:T(2,128)(2,1)S(1)}, bf16[2,8,2,84,336]{4,2,3,1,0:T(2,128)(2,1)}, u32[]{:S(2)}) copy-start(bf16[2,8,2,84,336]{4,2,3,1,0:T(2,128)(2,1)} %param.11) | copy-start | bytes 5419012
  14.3 10.0 %collective-permute-start.4 = (bf16[2,168,128]{2,1,0:T(8,128)(2,1)S(1)}, bf16[2,168,128]{2,1,0:T(8,128)(2,1)S(1)}, u32[]{:S(2)}, u32[]{:S(2)}) collective-permute-start(bf16[2,168,128]{2,1,0:T(8,128)(2,1)S(1)} %get-tuple-element.25), channel_id=1, source_target_pairs={{0,28},{4,8},{8,4},{12,16},{16,12},{20,24},{24,20},{28,0},{1,29},{... | collective-permute-start | bytes 258056 | tf_op jit(solution)/shard_map/ppermute | solution.py:332
  17.7 5.0 %collective-permute-start.2 = (bf16[2,168,128]{2,1,0:T(8,128)(2,1)S(1)}, bf16[2,168,128]{2,1,0:T(8,128)(2,1)S(1)}, u32[]{:S(2)}, u32[]{:S(2)}) collective-permute-start(bf16[2,168,128]{2,1,0:T(8,128)(2,1)S(1)} %get-tuple-element.25), channel_id=1, source_target_pairs={{0,4},{4,0},{8,12},{12,8},{16,20},{20,16},{24,28},{28,24},{1,5},{5... | collective-permute-start | bytes 258056 | tf_op jit(solution)/shard_map/ppermute | solution.py:324
  17.8 7.1 %collective-permute-start.9 = (bf16[256,128]{1,0:T(8,128)(2,1)S(1)}, bf16[256,128]{1,0:T(8,128)(2,1)S(1)}, u32[]{:S(2)}, u32[]{:S(2)}) collective-permute-start(bf16[256,128]{1,0:T(8,128)(2,1)S(1)} %fusion.28), channel_id=1, source_target_pairs={{0,4},{4,0},{8,12},{12,8},{16,20},{20,16},{24,28},{28,24},{1,5},{5... | collective-permute-start | bytes 196616 | tf_op jit(solution)/shard_map/ppermute | solution.py:324
  22.7 6.4 %collective-permute-start.3 = (bf16[2,2,168,128]{3,2,1,0:T(8,128)(2,1)S(1)}, bf16[2,2,168,128]{3,2,1,0:T(8,128)(2,1)S(1)}, u32[]{:S(2)}, u32[]{:S(2)}) collective-permute-start(bf16[2,2,168,128]{3,2,1,0:T(8,128)(2,1)S(1)} %pad_maximum_fusion.refs_0_), channel_id=1, source_target_pairs={{0,2},{1,3},{2,0},{3,1},{4,6},{5,7},{6,4},{7,5},{8,10},{9,11},{10,... | collective-permute-start | bytes 516104 | tf_op jit(solution)/shard_map/ppermute | solution.py:324
  24.3 4.8 %collective-permute-start.5 = (bf16[2,168,128]{2,1,0:T(8,128)(2,1)S(1)}, bf16[2,168,128]{2,1,0:T(8,128)(2,1)S(1)}, u32[]{:S(2)}, u32[]{:S(2)}) collective-permute-start(bf16[2,168,128]{2,1,0:T(8,128)(2,1)S(1)} %collective-permute-done.4.refs_2_), channel_id=1, source_target_pairs={{0,2},{1,3},{2,0},{3,1},{4,6},{5,7},{6,4},{7,5},{8,10},{9,11},{10,... | collective-permute-start | bytes 258056 | tf_op jit(solution)/shard_map/ppermute | solution.py:324
  24.9 5.9 %collective-permute-start.10 = (bf16[256,128]{1,0:T(8,128)(2,1)S(1)}, bf16[256,128]{1,0:T(8,128)(2,1)S(1)}, u32[]{:S(2)}, u32[]{:S(2)}) collective-permute-start(bf16[256,128]{1,0:T(8,128)(2,1)S(1)} %fusion.25), channel_id=1, source_target_pairs={{0,16},{4,20},{8,24},{12,28},{16,0},{20,4},{24,8},{28,12},{1,17},{... | collective-permute-start | bytes 196616 | tf_op jit(solution)/shard_map/ppermute | solution.py:324
  32.9 4.3 %collective-permute-start.15 = (bf16[256,128]{1,0:T(8,128)(2,1)S(1)}, bf16[256,128]{1,0:T(8,128)(2,1)S(1)}, u32[]{:S(2)}, u32[]{:S(2)}) collective-permute-start(bf16[256,128]{1,0:T(8,128)(2,1)S(1)} %get-tuple-element.30), channel_id=1, source_target_pairs={{0,2},{1,3},{2,0},{3,1},{4,6},{5,7},{6,4},{7,5},{8,10},{9,11},{10,... | collective-permute-start | bytes 196616 | tf_op jit(solution)/shard_map/ppermute | solution.py:324
  37.2 4.3 %collective-permute-start.16 = (bf16[256,128]{1,0:T(8,128)(2,1)S(1)}, bf16[256,128]{1,0:T(8,128)(2,1)S(1)}, u32[]{:S(2)}, u32[]{:S(2)}) collective-permute-start(bf16[256,128]{1,0:T(8,128)(2,1)S(1)} %fusion.26), channel_id=1, source_target_pairs={{0,8},{4,12},{8,0},{12,4},{16,24},{20,28},{24,16},{28,20},{1,9},{5... | collective-permute-start | bytes 196616 | tf_op jit(solution)/shard_map/ppermute | solution.py:324
  37.3 9.7 %collective-permute-start.13 = (bf16[2,168,128]{2,1,0:T(8,128)(2,1)S(1)}, bf16[2,168,128]{2,1,0:T(8,128)(2,1)S(1)}, u32[]{:S(2)}, u32[]{:S(2)}) collective-permute-start(bf16[2,168,128]{2,1,0:T(8,128)(2,1)S(1)} %get-tuple-element.28), channel_id=1, source_target_pairs={{0,28},{4,8},{8,4},{12,16},{16,12},{20,24},{24,20},{28,0},{1,29},{... | collective-permute-start | bytes 258056 | tf_op jit(solution)/shard_map/ppermute | solution.py:332
  40.0 5.4 %collective-permute-start.11 = (bf16[2,168,128]{2,1,0:T(8,128)(2,1)S(1)}, bf16[2,168,128]{2,1,0:T(8,128)(2,1)S(1)}, u32[]{:S(2)}, u32[]{:S(2)}) collective-permute-start(bf16[2,168,128]{2,1,0:T(8,128)(2,1)S(1)} %get-tuple-element.28), channel_id=1, source_target_pairs={{0,4},{4,0},{8,12},{12,8},{16,20},{20,16},{24,28},{28,24},{1,5},{5... | collective-permute-start | bytes 258056 | tf_op jit(solution)/shard_map/ppermute | solution.py:324
  41.6 6.0 %collective-permute-start.17 = (bf16[256,128]{1,0:T(8,128)(2,1)S(1)}, bf16[256,128]{1,0:T(8,128)(2,1)S(1)}, u32[]{:S(2)}, u32[]{:S(2)}) collective-permute-start(bf16[256,128]{1,0:T(8,128)(2,1)S(1)} %fusion.29), channel_id=1, source_target_pairs={{0,4},{4,0},{8,12},{12,8},{16,20},{20,16},{24,28},{28,24},{1,5},{5... | collective-permute-start | bytes 196616 | tf_op jit(solution)/shard_map/ppermute | solution.py:324
  45.4 6.4 %collective-permute-start.12 = (bf16[2,2,168,128]{3,2,1,0:T(8,128)(2,1)S(1)}, bf16[2,2,168,128]{3,2,1,0:T(8,128)(2,1)S(1)}, u32[]{:S(2)}, u32[]{:S(2)}) collective-permute-start(bf16[2,2,168,128]{3,2,1,0:T(8,128)(2,1)S(1)} %pad_maximum_fusion.1.refs_0_), channel_id=1, source_target_pairs={{0,2},{1,3},{2,0},{3,1},{4,6},{5,7},{6,4},{7,5},{8,10},{9,11},{10,... | collective-permute-start | bytes 516104 | tf_op jit(solution)/shard_map/ppermute | solution.py:324
  47.0 4.8 %collective-permute-start.14 = (bf16[2,168,128]{2,1,0:T(8,128)(2,1)S(1)}, bf16[2,168,128]{2,1,0:T(8,128)(2,1)S(1)}, u32[]{:S(2)}, u32[]{:S(2)}) collective-permute-start(bf16[2,168,128]{2,1,0:T(8,128)(2,1)S(1)} %collective-permute-done.13.refs_2_), channel_id=1, source_target_pairs={{0,2},{1,3},{2,0},{3,1},{4,6},{5,7},{6,4},{7,5},{8,10},{9,11},{10,... | collective-permute-start | bytes 258056 | tf_op jit(solution)/shard_map/ppermute | solution.py:324
  47.6 6.8 %collective-permute-start.18 = (bf16[256,128]{1,0:T(8,128)(2,1)S(1)}, bf16[256,128]{1,0:T(8,128)(2,1)S(1)}, u32[]{:S(2)}, u32[]{:S(2)}) collective-permute-start(bf16[256,128]{1,0:T(8,128)(2,1)S(1)} %fusion.27), channel_id=1, source_target_pairs={{0,16},{4,20},{8,24},{12,28},{16,0},{20,4},{24,8},{28,12},{1,17},{... | collective-permute-start | bytes 196616 | tf_op jit(solution)/shard_map/ppermute | solution.py:324
  54.4 12.5 %copy-start = (f32[2,2,84,128]{3,1,2,0:T(2,128)S(1)}, f32[2,2,84,128]{3,1,2,0:T(2,128)}, u32[]{:S(2)}) copy-start(f32[2,2,84,128]{3,1,2,0:T(2,128)} %param.9) | copy-start | bytes 516100
  56.0 10.9 %all-to-all-start = ((f32[32,8,128]{2,1,0:T(8,128)}), f32[32,8,128]{2,1,0:T(8,128)S(1)}, u32[]{:S(2)}, u32[]{:S(2)}) async-start(f32[32,8,128]{2,1,0:T(8,128)} %get-tuple-element.33), calls=%async_computation | async-start | bytes 262144 | tf_op jit(solution)/shard_map/all_to_all | solution.py:428
  58.7 1.4 %collective-permute-start.19 = (f32[2,84,128]{2,1,0:T(8,128)S(1)}, f32[2,84,128]{2,1,0:T(8,128)S(1)}, u32[]{:S(2)}, u32[]{:S(2)}) collective-permute-start(f32[2,84,128]{2,1,0:T(8,128)S(1)} %get-tuple-element.32.g_other_ref), channel_id=1, source_target_pairs={{0,1},{1,0},{2,3},{3,2},{4,5},{5,4},{6,7},{7,6},{8,9},{9,8},{10,11... | collective-permute-start | bytes 258056 | tf_op jit(solution)/shard_map/ppermute | solution.py:324
  59.0 1.3 %collective-permute-start.20 = (f32[2,84,128]{2,1,0:T(8,128)S(1)}, f32[2,84,128]{2,1,0:T(8,128)S(1)}, u32[]{:S(2)}, u32[]{:S(2)}) collective-permute-start(f32[2,84,128]{2,1,0:T(8,128)S(1)} %get-tuple-element.35), channel_id=1, source_target_pairs={{0,1},{1,0},{2,3},{3,2},{4,5},{5,4},{6,7},{7,6},{8,9},{9,8},{10,11... | collective-permute-start | bytes 258056 | tf_op jit(solution)/shard_map/ppermute | solution.py:324

commit v6 on v5

--- a/solution.py
+++ b/solution.py
@@ -98,7 +98,16 @@
             part_ref[o, a] = part
 
 
-def project(field, part_ref, columns, spheres):
+def spread_body(column_ref, wide_ref, wide_mie_ref):
+    for i in range(wide_ref.shape[0]):
+        wide_ref[i] = jnp.broadcast_to(column_ref[:, i : i + 1], wide_ref.shape[1:])
+    count = wide_mie_ref.shape[1]
+    for i in range(wide_mie_ref.shape[0]):
+        at = wide_ref.shape[0] + i
+        wide_mie_ref[i] = jnp.broadcast_to(column_ref[0:count, at : at + 1], wide_mie_ref.shape[1:])
+
+
+def project(field, part_ref, column, spheres):
     total = None
     lead = (((0,), (0,)), ((), ()))
     with_re = with_im = None
@@ -112,7 +121,7 @@
     for s in range(spheres):
         at = slice(s * n, (s + 1) * n)
         part = with_re[:, at] + turn(with_im[:, at])
-        c, d = columns[:, s : s + 1], columns[:, spheres + s : spheres + s + 1]
+        c, d = column(s), column(spheres + s)
         value = c * part - d * turn(part)
         total = value if total is None else total + value
     return total
@@ -130,7 +139,7 @@
     for s in range(spheres):
         put_rounded(round_ref, s, mine_ref[s], other_ref[s])
         field.append([mine_ref[s].astype(bf16), other_ref[s].astype(bf16)])
-    total = project(field, part_ref, column_ref[...], spheres)
+    total = project(field, part_ref, lambda i: column_ref[:, i : i + 1], spheres)
     keep_ref[...] = total
     send_ref[...] = total.astype(bf16)
 
@@ -178,15 +187,14 @@
             out_ref[o, s] = with_re + turn(with_im)
 
 
-def image_fields(near_ref, total_ref, column_ref, part_ref):
-    _, spheres, count, _ = near_ref.shape
-    columns, total = column_ref[...], total_ref[...]
+def image_fields(near_ref, total_ref, wide_ref, wide_mie_ref, part_ref):
+    spheres = near_ref.shape[1]
+    total = total_ref[...]
     turned_total = turn(total)
     sides = []
     for s in range(spheres):
         at = 2 * spheres + s
-        c, d = columns[:, at : at + 1], columns[:, at + spheres : at + spheres + 1]
-        sides.append((c * total + d * turned_total).astype(bf16))
+        sides.append((wide_ref[at] * total + wide_ref[at + spheres] * turned_total).astype(bf16))
     turned = jnp.concatenate(sides, axis=1)
     n = total.shape[1]
     out = [[] for _ in range(spheres)]
@@ -196,32 +204,32 @@
         for s in range(spheres):
             at = slice(s * n, (s + 1) * n)
             value = near_ref[o, s] + with_re[:, at] - turn(with_im[:, at])
-            at = 4 * spheres + 2 * (o * spheres + s)
-            m_re, m_im = column_ref[0:count, at : at + 1], column_ref[0:count, at + 1 : at + 2]
+            at = 2 * (o * spheres + s)
+            m_re, m_im = wide_mie_ref[at], wide_mie_ref[at + 1]
             out[s].append(m_re * value + m_im * turn(value))
     return out
 
 
 def first_image_body(
-    near_ref, total_ref, column_ref, part_ref, mine_ref, other_ref, round_ref, send_ref, keep_ref
+    near_ref, total_ref, wide_ref, wide_mie_ref, part_ref, mine_ref, other_ref, round_ref, send_ref, keep_ref
 ):
-    images = image_fields(near_ref, total_ref, column_ref, part_ref)
+    images = image_fields(near_ref, total_ref, wide_ref, wide_mie_ref, part_ref)
     field = []
     for s, (mine, other) in enumerate(images):
         mine_ref[s] = mine
         other_ref[s] = other
         put_rounded(round_ref, s, mine, other)
         field.append([mine.astype(bf16), other.astype(bf16)])
-    total = project(field, part_ref, column_ref[...], len(images))
+    total = project(field, part_ref, lambda i: wide_ref[i], len(images))
     keep_ref[...] = total
     send_ref[...] = total.astype(bf16)
 
 
 def second_image_body(
-    near_ref, total_ref, column_ref, part_ref, x_ref, x_other_ref, g_ref, g_other_ref,
+    near_ref, total_ref, wide_ref, wide_mie_ref, part_ref, x_ref, x_other_ref, g_ref, g_other_ref,
     mine_ref, other_ref, gram_ref,
 ):
-    images = image_fields(near_ref, total_ref, column_ref, part_ref)
+    images = image_fields(near_ref, total_ref, wide_ref, wide_mie_ref, part_ref)
     half = total_ref.shape[1] // 2
     sums = None
     for s, rows in enumerate(images):
@@ -416,14 +424,16 @@
     rounded, send, keep = call(first_sums_body, (pair_half, sums_half, sums), [VM] * 4)(x_mine, x_other, columns, plane)
     rows_other = with_layout_constraint(trade(rows_mine, "blk", 1), stored)
     near, total = both_fields(rounded, send, keep)
+    tables = (shape((4 * spheres, waves, n)), shape((4 * spheres, count, n)))
+    wide = call(spread_body, tables, [VM])(columns)
     g_mine, g_other, rounded, send, keep = call(
-        first_image_body, (field, field, pair_half, sums_half, sums), [VM] * 4
-    )(near, total, columns, plane)
+        first_image_body, (field, field, pair_half, sums_half, sums), [VM] * 5
+    )(near, total, *wide, plane)
     g_back = trade(g_other, "blk", 1)
     near, total = both_fields(rounded, send, keep)
     h_mine, h_other, gram = call(
-        second_image_body, (field, field, shape((devices, 8, n))), [VM] * 8
-    )(near, total, columns, plane, x_mine, x_other, g_mine, g_other)
+        second_image_body, (field, field, shape((devices, 8, n))), [VM] * 9
+    )(near, total, *wide, plane, x_mine, x_other, g_mine, g_other)
     h_back = trade(h_other, "blk", 1)
     gram = lax.all_to_all(gram, ("slab", "blk"), 0, 0, tiled=True)
     flat = shape((spheres, 2 * count, n))

time: 68.1 us -> 66.4 us (0.975)
  waiting for transfers between devices: 30.5 us -> 27.6 us
  starting transfers between devices: 24.8 us -> 26 us
    ppermute x19, waiting for transfers between devices: 23.9 us -> 15.8 us  [trade(): lax.ppermute(value, axis, [(i, i ^ bit) for i in range(lax.axis_size(axis...]
    ppermute x2, waiting for transfers between devices: 0.01 us -> 5.24 us  [trade_odd(): return lax.ppermute(value, 'slab', pairs)]
    ppermute x19, starting transfers between devices: 16 us -> 17.3 us  [trade(): lax.ppermute(value, axis, [(i, i ^ bit) for i in range(lax.axis_size(axis...]
    pallas_call x2 -> x3, Pallas kernels: 2.64 us -> 2.63 us  [the longest x1 1.3 us: per_device(): call(second_image_body, (field, field, shape((devices, 8, n))), [VM] * 9)]
  transfers between devices with their start and end apart: 22 -> 22, of which waited for: 11 -> 14; matrix products, arithmetic and copies ran while one was open for 4% -> 4% of each run, Pallas kernels for 7% -> 8%
where the time goes in v6:
time: 66.4 us; the launch traced here: 66.1 us
  waiting for transfers between devices  27.6 us (42%)
  starting transfers between devices  26 us (39%)
  Pallas kernels  8.24 us (12%)
  matrix products  3.12 us (5%)
  between operations  0.84 us (1%)
    ppermute x19, starting transfers between devices, trade(): lax.ppermute(value, axis, [(i, i ^ bit) for i in range(lax.axis_size(axis...  17.3 us
    ppermute x19, waiting for transfers between devices, trade(): lax.ppermute(value, axis, [(i, i ^ bit) for i in range(lax.axis_size(axis...  15.8 us
    all_to_all x1, waiting for transfers between devices, per_device(): gram = lax.all_to_all(gram, ('slab', 'blk'), 0, 0, tiled=True)  6.6 us
    ppermute x2, starting transfers between devices, trade_odd(): return lax.ppermute(value, 'slab', pairs)  5.51 us
    ppermute x2, waiting for transfers between devices, trade_odd(): return lax.ppermute(value, 'slab', pairs)  5.24 us
    all_to_all x1, starting transfers between devices, per_device(): gram = lax.all_to_all(gram, ('slab', 'blk'), 0, 0, tiled=True)  3.17 us
    dot_general x4, matrix products, both_fields(): jnp.einsum('ikarc,ikcn->ikarn', rows, gathered, preferred_element_type=f32)  3.12 us
    pallas_call x2, Pallas kernels, both_fields(): call(gather_body, sources, [HB, HB] + [VM] * blocks, buffers)  1.65 us
  transfers between devices with their start and end apart: 22, of which 14 were waited for; matrix products, arithmetic and copies ran while one was open for 4% of the time, Pallas kernels for 8%

profile of v6, /device:TPU:0, one launch (start us, length us, event | category | flops | bytes accessed | tf_op | source)
XLA Modules:
  0.0 66.1 jit_solution(5912845245661569507)
XLA Ops:
  0.6 0.6 collective-permute-start.6
  1.2 1.0 %shard_map.112 = (f32[2,84,128]{2,1,0:T(8,128)S(1)}, f32[2,84,128]{2,1,0:T(8,128)S(1)}) custom-call(f32[2,168,128]{2,1,0:T(8,128)} %bitcast.38), custom_call_target="tpu_custom_call" | custom-call | tf_op jit(solution)/shard_map/pallas_call | solution.py:412
  2.2 0.1 collective-permute-start
  2.3 0.5 collective-permute-start.1
  2.8 2.5 %collective-permute-done.1.mie_other_ref = f32[2,2,84]{2,1,0:T(2,128)S(1)} collective-permute-done((f32[2,2,84]{2,1,0:T(2,128)}, f32[2,2,84]{2,1,0:T(2,128)S(1)}, u32[]{:S(2)}, u32[]{:S(2)}) %collective-permute-start.1) | collective-permute-done | bytes 1376 | tf_op jit(solution)/shard_map/ppermute | solution.py:332
  5.3 1.2 %shard_map.113 = (f32[256,16]{1,0:T(8,128)S(1)}, bf16[2,2,84,256]{3,2,1,0:T(8,128)(2,1)S(1)}) custom-call(f32[2,2,84]{2,1,0:T(2,128)S(1)} %collective-permute-done.1.mie_other_ref, bf16[2,336,256]{2,1,0:T(8,128)(2,1)} %bitcast.42, s32[3,256]{1,0:T(4,128)} %bitcast.45, f32[2,3]{1,0:T(2,128)} %pos_hbm.1, f32[1,256]{1,0:T(1,128)} %bitcast.46, f32[2,2,84]{2,1,0:T(2,128)} %mie_hbm.1), custom_call_target="tpu_custom_call" | custom-call | tf_op jit(solution)/shard_map/pallas_call | solution.py:421
  6.5 0.0 collective-permute-done.other_ref.x_other_ref
  6.5 0.5 shard_map.114
  7.0 2.9 %collective-permute-start.7 = (bf16[256,128]{1,0:T(8,128)(2,1)S(1)}, bf16[256,128]{1,0:T(8,128)(2,1)S(1)}, u32[]{:S(2)}, u32[]{:S(2)}) collective-permute-start(bf16[256,128]{1,0:T(8,128)(2,1)S(1)} %get-tuple-element.29), channel_id=1, source_target_pairs={{0,2},{1,3},{2,0},{3,1},{4,6},{5,7},{6,4},{7,5},{8,10},{9,11},{10,... | collective-permute-start | bytes 196616 | tf_op jit(solution)/shard_map/ppermute | solution.py:332
  9.9 2.4 %collective-permute-done.7 = bf16[256,128]{1,0:T(8,128)(2,1)S(1)} collective-permute-done((bf16[256,128]{1,0:T(8,128)(2,1)S(1)}, bf16[256,128]{1,0:T(8,128)(2,1)S(1)}, u32[]{:S(2)}, u32[]{:S(2)}) %collective-permute-start.7) | collective-permute-done | bytes 65568 | tf_op jit(solution)/shard_map/ppermute | solution.py:332
  12.3 2.0 %collective-permute-start.8 = (bf16[256,128]{1,0:T(8,128)(2,1)S(1)}, bf16[256,128]{1,0:T(8,128)(2,1)S(1)}, u32[]{:S(2)}, u32[]{:S(2)}) collective-permute-start(bf16[256,128]{1,0:T(8,128)(2,1)S(1)} %fusion.24), channel_id=1, source_target_pairs={{0,8},{4,12},{8,0},{12,4},{16,24},{20,28},{24,16},{28,20},{1,9},{5... | collective-permute-start | bytes 196616 | tf_op jit(solution)/shard_map/ppermute | solution.py:332
  14.3 0.4 shard_map.117
  14.8 0.0 copy-start.1
  14.8 1.6 %collective-permute-start.2 = (bf16[2,168,128]{2,1,0:T(8,128)(2,1)S(1)}, bf16[2,168,128]{2,1,0:T(8,128)(2,1)S(1)}, u32[]{:S(2)}, u32[]{:S(2)}) collective-permute-start(bf16[2,168,128]{2,1,0:T(8,128)(2,1)S(1)} %get-tuple-element.27), channel_id=1, source_target_pairs={{0,4},{4,0},{8,12},{12,8},{16,20},{20,16},{24,28},{28,24},{1,5},{5... | collective-permute-start | bytes 258056 | tf_op jit(solution)/shard_map/ppermute | solution.py:332
  16.4 2.5 %collective-permute-start.4 = (bf16[2,168,128]{2,1,0:T(8,128)(2,1)S(1)}, bf16[2,168,128]{2,1,0:T(8,128)(2,1)S(1)}, u32[]{:S(2)}, u32[]{:S(2)}) collective-permute-start(bf16[2,168,128]{2,1,0:T(8,128)(2,1)S(1)} %get-tuple-element.27), channel_id=1, source_target_pairs={{0,28},{4,8},{8,4},{12,16},{16,12},{20,24},{24,20},{28,0},{1,29},{... | collective-permute-start | bytes 258056 | tf_op jit(solution)/shard_map/ppermute | solution.py:340
  18.8 0.0 collective-permute-done.8
  18.8 0.1 collective-permute-start.9
  18.9 0.4 collective-permute-done.2
  19.4 1.6 %collective-permute-start.3 = (bf16[2,2,168,128]{3,2,1,0:T(8,128)(2,1)S(1)}, bf16[2,2,168,128]{3,2,1,0:T(8,128)(2,1)S(1)}, u32[]{:S(2)}, u32[]{:S(2)}) collective-permute-start(bf16[2,2,168,128]{3,2,1,0:T(8,128)(2,1)S(1)} %pad_maximum_fusion.refs_0_), channel_id=1, source_target_pairs={{0,2},{1,3},{2,0},{3,1},{4,6},{5,7},{6,4},{7,5},{8,10},{9,11},{10,... | collective-permute-start | bytes 516104 | tf_op jit(solution)/shard_map/ppermute | solution.py:332
  21.0 2.7 %collective-permute-done.4.refs_2_ = bf16[2,168,128]{2,1,0:T(8,128)(2,1)S(1)} collective-permute-done((bf16[2,168,128]{2,1,0:T(8,128)(2,1)S(1)}, bf16[2,168,128]{2,1,0:T(8,128)(2,1)S(1)}, u32[]{:S(2)}, u32[]{:S(2)}) %collective-permute-start.4) | collective-permute-done | bytes 86048 | tf_op jit(solution)/shard_map/ppermute | solution.py:340
  23.6 1.5 %collective-permute-start.5 = (bf16[2,168,128]{2,1,0:T(8,128)(2,1)S(1)}, bf16[2,168,128]{2,1,0:T(8,128)(2,1)S(1)}, u32[]{:S(2)}, u32[]{:S(2)}) collective-permute-start(bf16[2,168,128]{2,1,0:T(8,128)(2,1)S(1)} %collective-permute-done.4.refs_2_), channel_id=1, source_target_pairs={{0,2},{1,3},{2,0},{3,1},{4,6},{5,7},{6,4},{7,5},{8,10},{9,11},{10,... | collective-permute-start | bytes 258056 | tf_op jit(solution)/shard_map/ppermute | solution.py:332
  25.2 0.0 collective-permute-done.9
  25.2 0.9 %collective-permute-start.10 = (bf16[256,128]{1,0:T(8,128)(2,1)S(1)}, bf16[256,128]{1,0:T(8,128)(2,1)S(1)}, u32[]{:S(2)}, u32[]{:S(2)}) collective-permute-start(bf16[256,128]{1,0:T(8,128)(2,1)S(1)} %fusion.25), channel_id=1, source_target_pairs={{0,16},{4,20},{8,24},{12,28},{16,0},{20,4},{24,8},{28,12},{1,17},{... | collective-permute-start | bytes 196616 | tf_op jit(solution)/shard_map/ppermute | solution.py:332
  26.1 2.1 %collective-permute-done.5.refs_3_ = bf16[2,168,128]{2,1,0:T(8,128)(2,1)S(1)} collective-permute-done((bf16[2,168,128]{2,1,0:T(8,128)(2,1)S(1)}, bf16[2,168,128]{2,1,0:T(8,128)(2,1)S(1)}, u32[]{:S(2)}, u32[]{:S(2)}) %collective-permute-start.5) | collective-permute-done | bytes 86048 | tf_op jit(solution)/shard_map/ppermute | solution.py:332
  28.1 0.0 collective-permute-done.3.refs_1_
  28.1 0.8 %shard_map.115 = bf16[2,8,336,128]{3,2,1,0:T(8,128)(2,1)S(1)} custom-call(s32[2,8]{1,0:T(2,128)} %shift_hbm.3, s32[2,8]{1,0:T(2,128)} %member_hbm.3, bf16[2,2,168,128]{3,2,1,0:T(8,128)(2,1)S(1)} %pad_maximum_fusion.refs_0_, bf16[2,2,168,128]{3,2,1,0:T(8,128)(2,1)S(1)} %collective-permute-done.3.refs_1_, ...), custom_call_target="tpu_custom_call" | custom-call | tf_op jit(solution)/shard_map/pallas_call | solution.py:400
  29.0 0.0 copy-done.1
  29.0 0.8 %fusion.8.mine_ref = f32[2,8,2,84,128]{4,3,2,1,0:T(8,128)S(1)} fusion(bf16[2,8,2,84,336]{4,2,3,1,0:T(2,128)(2,1)S(1)} %copy-done.1, bf16[2,8,336,128]{3,2,1,0:T(8,128)(2,1)S(1)} %shard_map.115), kind=kOutput, calls=%fused_computation.8 | convolution fusion | flops 231211008 | bytes 4558848 | tf_op jit(solution)/shard_map/ikarc,ikcn->ikarn/dot_general | solution.py:404
  29.8 0.7 %collective-permute-done.10 = bf16[256,128]{1,0:T(8,128)(2,1)S(1)} collective-permute-done((bf16[256,128]{1,0:T(8,128)(2,1)S(1)}, bf16[256,128]{1,0:T(8,128)(2,1)S(1)}, u32[]{:S(2)}, u32[]{:S(2)}) %collective-permute-start.10) | collective-permute-done | bytes 65568 | tf_op jit(solution)/shard_map/ppermute | solution.py:332
  30.5 0.0 collective-permute-done.6
  30.5 0.8 %fusion.14.other_ref = f32[2,8,2,84,128]{4,3,2,1,0:T(8,128)S(1)} fusion(bf16[2,8,2,84,336]{4,2,3,1,0:T(2,128)(2,1)S(1)} %collective-permute-done.6, bf16[2,8,336,128]{3,2,1,0:T(8,128)(2,1)S(1)} %shard_map.115), kind=kOutput, calls=%fused_computation.10 | convolution fusion | flops 231211008 | bytes 4558848 | tf_op jit(solution)/shard_map/ikarc,ikcn->ikarn/dot_general | solution.py:404
  31.3 0.1 shard_map.116.near_ref
  31.4 0.9 %shard_map.118 = (f32[2,84,128]{2,1,0:T(8,128)S(1)}, f32[2,84,128]{2,1,0:T(8,128)S(1)}, bf16[2,168,128]{2,1,0:T(8,128)(2,1)S(1)}, bf16[256,128]{1,0:T(8,128)(2,1)S(1)}, f32[256,128]{1,0:T(8,128)S(1)}) custom-call(f32[2,2,84,128]{3,2,1,0:T(8,128)S(1)} %shard_map.116.near_ref, f32[256,128]{1,0:T(8,128)S(1)} %convert_add_fusion.4.total_ref, ...), custom_call_target="tpu_custom_call" | custom-call | tf_op jit(solution)/shard_map/pallas_call | solution.py:429
  32.3 0.9 %collective-permute-start.15 = (bf16[256,128]{1,0:T(8,128)(2,1)S(1)}, bf16[256,128]{1,0:T(8,128)(2,1)S(1)}, u32[]{:S(2)}, u32[]{:S(2)}) collective-permute-start(bf16[256,128]{1,0:T(8,128)(2,1)S(1)} %get-tuple-element.34), channel_id=1, source_target_pairs={{0,2},{1,3},{2,0},{3,1},{4,6},{5,7},{6,4},{7,5},{8,10},{9,11},{10,... | collective-permute-start | bytes 196616 | tf_op jit(solution)/shard_map/ppermute | solution.py:332
  33.2 3.4 %collective-permute-done.15 = bf16[256,128]{1,0:T(8,128)(2,1)S(1)} collective-permute-done((bf16[256,128]{1,0:T(8,128)(2,1)S(1)}, bf16[256,128]{1,0:T(8,128)(2,1)S(1)}, u32[]{:S(2)}, u32[]{:S(2)}) %collective-permute-start.15) | collective-permute-done | bytes 65568 | tf_op jit(solution)/shard_map/ppermute | solution.py:332
  36.7 0.1 collective-permute-start.16
  36.7 0.7 collective-permute-start.11
  37.4 3.1 %collective-permute-start.13 = (bf16[2,168,128]{2,1,0:T(8,128)(2,1)S(1)}, bf16[2,168,128]{2,1,0:T(8,128)(2,1)S(1)}, u32[]{:S(2)}, u32[]{:S(2)}) collective-permute-start(bf16[2,168,128]{2,1,0:T(8,128)(2,1)S(1)} %get-tuple-element.32), channel_id=1, source_target_pairs={{0,28},{4,8},{8,4},{12,16},{16,12},{20,24},{24,20},{28,0},{1,29},{... | collective-permute-start | bytes 258056 | tf_op jit(solution)/shard_map/ppermute | solution.py:340
  40.4 0.5 collective-permute-done.16
  41.0 0.2 collective-permute-start.17
  41.2 0.1 collective-permute-done.11
  41.3 1.5 %collective-permute-start.12 = (bf16[2,2,168,128]{3,2,1,0:T(8,128)(2,1)S(1)}, bf16[2,2,168,128]{3,2,1,0:T(8,128)(2,1)S(1)}, u32[]{:S(2)}, u32[]{:S(2)}) collective-permute-start(bf16[2,2,168,128]{3,2,1,0:T(8,128)(2,1)S(1)} %pad_maximum_fusion.1.refs_0_), channel_id=1, source_target_pairs={{0,2},{1,3},{2,0},{3,1},{4,6},{5,7},{6,4},{7,5},{8,10},{9,11},{10,... | collective-permute-start | bytes 516104 | tf_op jit(solution)/shard_map/ppermute | solution.py:332
  42.8 2.6 %collective-permute-done.13.refs_2_ = bf16[2,168,128]{2,1,0:T(8,128)(2,1)S(1)} collective-permute-done((bf16[2,168,128]{2,1,0:T(8,128)(2,1)S(1)}, bf16[2,168,128]{2,1,0:T(8,128)(2,1)S(1)}, u32[]{:S(2)}, u32[]{:S(2)}) %collective-permute-start.13) | collective-permute-done | bytes 86048 | tf_op jit(solution)/shard_map/ppermute | solution.py:340
  45.4 1.1 %collective-permute-start.14 = (bf16[2,168,128]{2,1,0:T(8,128)(2,1)S(1)}, bf16[2,168,128]{2,1,0:T(8,128)(2,1)S(1)}, u32[]{:S(2)}, u32[]{:S(2)}) collective-permute-start(bf16[2,168,128]{2,1,0:T(8,128)(2,1)S(1)} %collective-permute-done.13.refs_2_), channel_id=1, source_target_pairs={{0,2},{1,3},{2,0},{3,1},{4,6},{5,7},{6,4},{7,5},{8,10},{9,11},{10,... | collective-permute-start | bytes 258056 | tf_op jit(solution)/shard_map/ppermute | solution.py:332
  46.4 0.0 collective-permute-done.17
  46.5 0.7 %collective-permute-start.18 = (bf16[256,128]{1,0:T(8,128)(2,1)S(1)}, bf16[256,128]{1,0:T(8,128)(2,1)S(1)}, u32[]{:S(2)}, u32[]{:S(2)}) collective-permute-start(bf16[256,128]{1,0:T(8,128)(2,1)S(1)} %fusion.27), channel_id=1, source_target_pairs={{0,16},{4,20},{8,24},{12,28},{16,0},{20,4},{24,8},{28,12},{1,17},{... | collective-permute-start | bytes 196616 | tf_op jit(solution)/shard_map/ppermute | solution.py:332
  47.1 2.7 %collective-permute-done.14.refs_3_ = bf16[2,168,128]{2,1,0:T(8,128)(2,1)S(1)} collective-permute-done((bf16[2,168,128]{2,1,0:T(8,128)(2,1)S(1)}, bf16[2,168,128]{2,1,0:T(8,128)(2,1)S(1)}, u32[]{:S(2)}, u32[]{:S(2)}) %collective-permute-start.14) | collective-permute-done | bytes 86048 | tf_op jit(solution)/shard_map/ppermute | solution.py:332
  49.9 0.0 collective-permute-done.12.refs_1_
  49.9 0.8 %shard_map.119 = bf16[2,8,336,128]{3,2,1,0:T(8,128)(2,1)S(1)} custom-call(s32[2,8]{1,0:T(2,128)} %shift_hbm.3, s32[2,8]{1,0:T(2,128)} %member_hbm.3, bf16[2,2,168,128]{3,2,1,0:T(8,128)(2,1)S(1)} %pad_maximum_fusion.1.refs_0_, bf16[2,2,168,128]{3,2,1,0:T(8,128)(2,1)S(1)} %collective-permute-done.12.refs_1_, ...), custom_call_target="tpu_custom_call" | custom-call | tf_op jit(solution)/shard_map/pallas_call | solution.py:400
  50.7 0.8 %fusion.11.mine_ref = f32[2,8,2,84,128]{4,3,2,1,0:T(8,128)S(1)} fusion(bf16[2,8,2,84,336]{4,2,3,1,0:T(2,128)(2,1)S(1)} %copy-done.1, bf16[2,8,336,128]{3,2,1,0:T(8,128)(2,1)S(1)} %shard_map.119), kind=kOutput, calls=%fused_computation.9 | convolution fusion | flops 231211008 | bytes 4558848 | tf_op jit(solution)/shard_map/ikarc,ikcn->ikarn/dot_general | solution.py:404
  51.5 0.8 %fusion.17.other_ref = f32[2,8,2,84,128]{4,3,2,1,0:T(8,128)S(1)} fusion(bf16[2,8,2,84,336]{4,2,3,1,0:T(2,128)(2,1)S(1)} %collective-permute-done.6, bf16[2,8,336,128]{3,2,1,0:T(8,128)(2,1)S(1)} %shard_map.119), kind=kOutput, calls=%fused_computation.11 | convolution fusion | flops 231211008 | bytes 4558848 | tf_op jit(solution)/shard_map/ikarc,ikcn->ikarn/dot_general | solution.py:404
  52.3 0.1 shard_map.120.near_ref
  52.4 0.0 copy-start
  52.4 0.0 collective-permute-done.18
  52.5 1.3 %shard_map.121 = (f32[2,84,128]{2,1,0:T(8,128)S(1)}, f32[2,84,128]{2,1,0:T(8,128)S(1)}, f32[32,8,128]{2,1,0:T(8,128)}) custom-call(f32[2,2,84,128]{3,2,1,0:T(8,128)S(1)} %shard_map.120.near_ref, f32[256,128]{1,0:T(8,128)S(1)} %convert_add_fusion.total_ref, f32[8,256,128]{2,1,0:T(8,128)S(1)} %get-tuple-element.30.wide_ref, ...), custom_call_target="tpu_custom_call" | custom-call | tf_op jit(solution)/shard_map/pallas_call | solution.py:434
  53.8 3.2 %all-to-all-start = ((f32[32,8,128]{2,1,0:T(8,128)}), f32[32,8,128]{2,1,0:T(8,128)S(1)}, u32[]{:S(2)}, u32[]{:S(2)}) async-start(f32[32,8,128]{2,1,0:T(8,128)} %get-tuple-element.37), calls=%async_computation | async-start | bytes 262144 | tf_op jit(solution)/shard_map/all_to_all | solution.py:438
  57.0 0.3 collective-permute-start.19
  57.3 0.3 collective-permute-start.20
  57.5 0.8 %collective-permute-done.19.refs_3_ = f32[2,84,128]{2,1,0:T(8,128)S(1)} collective-permute-done((f32[2,84,128]{2,1,0:T(8,128)S(1)}, f32[2,84,128]{2,1,0:T(8,128)S(1)}, u32[]{:S(2)}, u32[]{:S(2)}) %collective-permute-start.19) | collective-permute-done | bytes 86048 | tf_op jit(solution)/shard_map/ppermute | solution.py:332
  58.3 0.3 collective-permute-done.20.refs_5_
  58.6 6.6 %all-to-all-done.refs_0_ = f32[32,8,128]{2,1,0:T(8,128)S(1)} async-done(((f32[32,8,128]{2,1,0:T(8,128)}), f32[32,8,128]{2,1,0:T(8,128)S(1)}, u32[]{:S(2)}, u32[]{:S(2)}) %all-to-all-start) | async-done | bytes 131104 | tf_op jit(solution)/shard_map/all_to_all | solution.py:438
  65.2 0.0 copy-done
  65.2 1.0 %shard_map.122 = (f32[2,168,128]{2,1,0:T(8,128)}, f32[2,168,128]{2,1,0:T(8,128)}, f32[9,128]{1,0:T(8,128)}) custom-call(f32[32,8,128]{2,1,0:T(8,128)S(1)} %all-to-all-done.refs_0_, f32[2,168,128]{2,1,0:T(8,128)S(1)} %bitcast.39, f32[2,84,128]{2,1,0:T(8,128)S(1)} %get-tuple-element.35.g_ref.refs_2_, f32[2,84,128]{2,1,0:T(8,128)S(1)} %collective-permute-done.19.refs_3_, ...), custom_call_target="tpu_custom_call" | custom-call | tf_op jit(solution)/shard_map/pallas_call | solution.py:440
  (10 shorter events, 0.3 us)
Async XLA Ops:
  0.6 29.9 %collective-permute-start.6 = (bf16[2,8,2,84,336]{4,2,3,1,0:T(2,128)(2,1)}, bf16[2,8,2,84,336]{4,2,3,1,0:T(2,128)(2,1)S(1)}, u32[]{:S(2)}, u32[]{:S(2)}) collective-permute-start(bf16[2,8,2,84,336]{4,2,3,1,0:T(2,128)(2,1)} %param.11), channel_id=1, source_target_pairs={{0,1},{1,0},{2,3},{3,2},{4,5},{5,4},{6,7},{7,6},{8,9},{9,8},{10,11... | collective-permute-start | bytes 5419016 | tf_op jit(solution)/shard_map/ppermute | solution.py:332
  2.2 4.2 %collective-permute-start = (f32[2,84,128]{2,1,0:T(8,128)S(1)}, f32[2,84,128]{2,1,0:T(8,128)S(1)}, u32[]{:S(2)}, u32[]{:S(2)}) collective-permute-start(f32[2,84,128]{2,1,0:T(8,128)S(1)} %get-tuple-element.24), channel_id=1, source_target_pairs={{0,1},{1,0},{2,3},{3,2},{4,5},{5,4},{6,7},{7,6},{8,9},{9,8},{10,11... | collective-permute-start | bytes 258056 | tf_op jit(solution)/shard_map/ppermute | solution.py:332
  2.3 2.9 %collective-permute-start.1 = (f32[2,2,84]{2,1,0:T(2,128)}, f32[2,2,84]{2,1,0:T(2,128)S(1)}, u32[]{:S(2)}, u32[]{:S(2)}) collective-permute-start(f32[2,2,84]{2,1,0:T(2,128)} %mie_hbm.1), channel_id=1, source_target_pairs={{0,1},{1,0},{2,3},{3,2},{4,5},{5,4},{6,7},{7,6},{8,9},{9,8},{10,11... | collective-permute-start | bytes 4040 | tf_op jit(solution)/shard_map/ppermute | solution.py:332
  7.0 5.3 %collective-permute-start.7 = (bf16[256,128]{1,0:T(8,128)(2,1)S(1)}, bf16[256,128]{1,0:T(8,128)(2,1)S(1)}, u32[]{:S(2)}, u32[]{:S(2)}) collective-permute-start(bf16[256,128]{1,0:T(8,128)(2,1)S(1)} %get-tuple-element.29), channel_id=1, source_target_pairs={{0,2},{1,3},{2,0},{3,1},{4,6},{5,7},{6,4},{7,5},{8,10},{9,11},{10,... | collective-permute-start | bytes 196616 | tf_op jit(solution)/shard_map/ppermute | solution.py:332
  12.3 6.5 %collective-permute-start.8 = (bf16[256,128]{1,0:T(8,128)(2,1)S(1)}, bf16[256,128]{1,0:T(8,128)(2,1)S(1)}, u32[]{:S(2)}, u32[]{:S(2)}) collective-permute-start(bf16[256,128]{1,0:T(8,128)(2,1)S(1)} %fusion.24), channel_id=1, source_target_pairs={{0,8},{4,12},{8,0},{12,4},{16,24},{20,28},{24,16},{28,20},{1,9},{5... | collective-permute-start | bytes 196616 | tf_op jit(solution)/shard_map/ppermute | solution.py:332
  14.8 14.2 %copy-start.1 = (bf16[2,8,2,84,336]{4,2,3,1,0:T(2,128)(2,1)S(1)}, bf16[2,8,2,84,336]{4,2,3,1,0:T(2,128)(2,1)}, u32[]{:S(2)}) copy-start(bf16[2,8,2,84,336]{4,2,3,1,0:T(2,128)(2,1)} %param.11) | copy-start | bytes 5419012
  14.8 4.6 %collective-permute-start.2 = (bf16[2,168,128]{2,1,0:T(8,128)(2,1)S(1)}, bf16[2,168,128]{2,1,0:T(8,128)(2,1)S(1)}, u32[]{:S(2)}, u32[]{:S(2)}) collective-permute-start(bf16[2,168,128]{2,1,0:T(8,128)(2,1)S(1)} %get-tuple-element.27), channel_id=1, source_target_pairs={{0,4},{4,0},{8,12},{12,8},{16,20},{20,16},{24,28},{28,24},{1,5},{5... | collective-permute-start | bytes 258056 | tf_op jit(solution)/shard_map/ppermute | solution.py:332
  16.4 7.3 %collective-permute-start.4 = (bf16[2,168,128]{2,1,0:T(8,128)(2,1)S(1)}, bf16[2,168,128]{2,1,0:T(8,128)(2,1)S(1)}, u32[]{:S(2)}, u32[]{:S(2)}) collective-permute-start(bf16[2,168,128]{2,1,0:T(8,128)(2,1)S(1)} %get-tuple-element.27), channel_id=1, source_target_pairs={{0,28},{4,8},{8,4},{12,16},{16,12},{20,24},{24,20},{28,0},{1,29},{... | collective-permute-start | bytes 258056 | tf_op jit(solution)/shard_map/ppermute | solution.py:340
  18.8 6.3 %collective-permute-start.9 = (bf16[256,128]{1,0:T(8,128)(2,1)S(1)}, bf16[256,128]{1,0:T(8,128)(2,1)S(1)}, u32[]{:S(2)}, u32[]{:S(2)}) collective-permute-start(bf16[256,128]{1,0:T(8,128)(2,1)S(1)} %fusion.28), channel_id=1, source_target_pairs={{0,4},{4,0},{8,12},{12,8},{16,20},{20,16},{24,28},{28,24},{1,5},{5... | collective-permute-start | bytes 196616 | tf_op jit(solution)/shard_map/ppermute | solution.py:332
  19.4 8.8 %collective-permute-start.3 = (bf16[2,2,168,128]{3,2,1,0:T(8,128)(2,1)S(1)}, bf16[2,2,168,128]{3,2,1,0:T(8,128)(2,1)S(1)}, u32[]{:S(2)}, u32[]{:S(2)}) collective-permute-start(bf16[2,2,168,128]{3,2,1,0:T(8,128)(2,1)S(1)} %pad_maximum_fusion.refs_0_), channel_id=1, source_target_pairs={{0,2},{1,3},{2,0},{3,1},{4,6},{5,7},{6,4},{7,5},{8,10},{9,11},{10,... | collective-permute-start | bytes 516104 | tf_op jit(solution)/shard_map/ppermute | solution.py:332
  23.6 4.5 %collective-permute-start.5 = (bf16[2,168,128]{2,1,0:T(8,128)(2,1)S(1)}, bf16[2,168,128]{2,1,0:T(8,128)(2,1)S(1)}, u32[]{:S(2)}, u32[]{:S(2)}) collective-permute-start(bf16[2,168,128]{2,1,0:T(8,128)(2,1)S(1)} %collective-permute-done.4.refs_2_), channel_id=1, source_target_pairs={{0,2},{1,3},{2,0},{3,1},{4,6},{5,7},{6,4},{7,5},{8,10},{9,11},{10,... | collective-permute-start | bytes 258056 | tf_op jit(solution)/shard_map/ppermute | solution.py:332
  25.2 5.2 %collective-permute-start.10 = (bf16[256,128]{1,0:T(8,128)(2,1)S(1)}, bf16[256,128]{1,0:T(8,128)(2,1)S(1)}, u32[]{:S(2)}, u32[]{:S(2)}) collective-permute-start(bf16[256,128]{1,0:T(8,128)(2,1)S(1)} %fusion.25), channel_id=1, source_target_pairs={{0,16},{4,20},{8,24},{12,28},{16,0},{20,4},{24,8},{28,12},{1,17},{... | collective-permute-start | bytes 196616 | tf_op jit(solution)/shard_map/ppermute | solution.py:332
  32.3 4.3 %collective-permute-start.15 = (bf16[256,128]{1,0:T(8,128)(2,1)S(1)}, bf16[256,128]{1,0:T(8,128)(2,1)S(1)}, u32[]{:S(2)}, u32[]{:S(2)}) collective-permute-start(bf16[256,128]{1,0:T(8,128)(2,1)S(1)} %get-tuple-element.34), channel_id=1, source_target_pairs={{0,2},{1,3},{2,0},{3,1},{4,6},{5,7},{6,4},{7,5},{8,10},{9,11},{10,... | collective-permute-start | bytes 196616 | tf_op jit(solution)/shard_map/ppermute | solution.py:332
  36.7 4.3 %collective-permute-start.16 = (bf16[256,128]{1,0:T(8,128)(2,1)S(1)}, bf16[256,128]{1,0:T(8,128)(2,1)S(1)}, u32[]{:S(2)}, u32[]{:S(2)}) collective-permute-start(bf16[256,128]{1,0:T(8,128)(2,1)S(1)} %fusion.26), channel_id=1, source_target_pairs={{0,8},{4,12},{8,0},{12,4},{16,24},{20,28},{24,16},{28,20},{1,9},{5... | collective-permute-start | bytes 196616 | tf_op jit(solution)/shard_map/ppermute | solution.py:332
  36.7 4.6 %collective-permute-start.11 = (bf16[2,168,128]{2,1,0:T(8,128)(2,1)S(1)}, bf16[2,168,128]{2,1,0:T(8,128)(2,1)S(1)}, u32[]{:S(2)}, u32[]{:S(2)}) collective-permute-start(bf16[2,168,128]{2,1,0:T(8,128)(2,1)S(1)} %get-tuple-element.32), channel_id=1, source_target_pairs={{0,4},{4,0},{8,12},{12,8},{16,20},{20,16},{24,28},{28,24},{1,5},{5... | collective-permute-start | bytes 258056 | tf_op jit(solution)/shard_map/ppermute | solution.py:332
  37.4 8.0 %collective-permute-start.13 = (bf16[2,168,128]{2,1,0:T(8,128)(2,1)S(1)}, bf16[2,168,128]{2,1,0:T(8,128)(2,1)S(1)}, u32[]{:S(2)}, u32[]{:S(2)}) collective-permute-start(bf16[2,168,128]{2,1,0:T(8,128)(2,1)S(1)} %get-tuple-element.32), channel_id=1, source_target_pairs={{0,28},{4,8},{8,4},{12,16},{16,12},{20,24},{24,20},{28,0},{1,29},{... | collective-permute-start | bytes 258056 | tf_op jit(solution)/shard_map/ppermute | solution.py:340
  41.0 5.4 %collective-permute-start.17 = (bf16[256,128]{1,0:T(8,128)(2,1)S(1)}, bf16[256,128]{1,0:T(8,128)(2,1)S(1)}, u32[]{:S(2)}, u32[]{:S(2)}) collective-permute-start(bf16[256,128]{1,0:T(8,128)(2,1)S(1)} %fusion.29), channel_id=1, source_target_pairs={{0,4},{4,0},{8,12},{12,8},{16,20},{20,16},{24,28},{28,24},{1,5},{5... | collective-permute-start | bytes 196616 | tf_op jit(solution)/shard_map/ppermute | solution.py:332
  41.3 8.6 %collective-permute-start.12 = (bf16[2,2,168,128]{3,2,1,0:T(8,128)(2,1)S(1)}, bf16[2,2,168,128]{3,2,1,0:T(8,128)(2,1)S(1)}, u32[]{:S(2)}, u32[]{:S(2)}) collective-permute-start(bf16[2,2,168,128]{3,2,1,0:T(8,128)(2,1)S(1)} %pad_maximum_fusion.1.refs_0_), channel_id=1, source_target_pairs={{0,2},{1,3},{2,0},{3,1},{4,6},{5,7},{6,4},{7,5},{8,10},{9,11},{10,... | collective-permute-start | bytes 516104 | tf_op jit(solution)/shard_map/ppermute | solution.py:332
  45.4 4.5 %collective-permute-start.14 = (bf16[2,168,128]{2,1,0:T(8,128)(2,1)S(1)}, bf16[2,168,128]{2,1,0:T(8,128)(2,1)S(1)}, u32[]{:S(2)}, u32[]{:S(2)}) collective-permute-start(bf16[2,168,128]{2,1,0:T(8,128)(2,1)S(1)} %collective-permute-done.13.refs_2_), channel_id=1, source_target_pairs={{0,2},{1,3},{2,0},{3,1},{4,6},{5,7},{6,4},{7,5},{8,10},{9,11},{10,... | collective-permute-start | bytes 258056 | tf_op jit(solution)/shard_map/ppermute | solution.py:332
  46.5 6.0 %collective-permute-start.18 = (bf16[256,128]{1,0:T(8,128)(2,1)S(1)}, bf16[256,128]{1,0:T(8,128)(2,1)S(1)}, u32[]{:S(2)}, u32[]{:S(2)}) collective-permute-start(bf16[256,128]{1,0:T(8,128)(2,1)S(1)} %fusion.27), channel_id=1, source_target_pairs={{0,16},{4,20},{8,24},{12,28},{16,0},{20,4},{24,8},{28,12},{1,17},{... | collective-permute-start | bytes 196616 | tf_op jit(solution)/shard_map/ppermute | solution.py:332
  52.4 12.8 %copy-start = (f32[2,2,84,128]{3,1,2,0:T(2,128)S(1)}, f32[2,2,84,128]{3,1,2,0:T(2,128)}, u32[]{:S(2)}) copy-start(f32[2,2,84,128]{3,1,2,0:T(2,128)} %param.9) | copy-start | bytes 516100
  53.8 11.4 %all-to-all-start = ((f32[32,8,128]{2,1,0:T(8,128)}), f32[32,8,128]{2,1,0:T(8,128)S(1)}, u32[]{:S(2)}, u32[]{:S(2)}) async-start(f32[32,8,128]{2,1,0:T(8,128)} %get-tuple-element.37), calls=%async_computation | async-start | bytes 262144 | tf_op jit(solution)/shard_map/all_to_all | solution.py:438
  57.0 1.4 %collective-permute-start.19 = (f32[2,84,128]{2,1,0:T(8,128)S(1)}, f32[2,84,128]{2,1,0:T(8,128)S(1)}, u32[]{:S(2)}, u32[]{:S(2)}) collective-permute-start(f32[2,84,128]{2,1,0:T(8,128)S(1)} %get-tuple-element.36.g_other_ref), channel_id=1, source_target_pairs={{0,1},{1,0},{2,3},{3,2},{4,5},{5,4},{6,7},{7,6},{8,9},{9,8},{10,11... | collective-permute-start | bytes 258056 | tf_op jit(solution)/shard_map/ppermute | solution.py:332
  57.3 1.3 %collective-permute-start.20 = (f32[2,84,128]{2,1,0:T(8,128)S(1)}, f32[2,84,128]{2,1,0:T(8,128)S(1)}, u32[]{:S(2)}, u32[]{:S(2)}) collective-permute-start(f32[2,84,128]{2,1,0:T(8,128)S(1)} %get-tuple-element.39), channel_id=1, source_target_pairs={{0,1},{1,0},{2,3},{3,2},{4,5},{5,4},{6,7},{7,6},{8,9},{9,8},{10,11... | collective-permute-start | bytes 258056 | tf_op jit(solution)/shard_map/ppermute | solution.py:332
